TPU v7x, 32 devices: a whole 2x2x4 slice. The times are simulated.
32 devices in a mesh: lon: 16 (over z, x, core), lat: 2 (over y).
Axes of the slice: x: 2, y: 2, z: 4, core: 2. Of those that a mesh axis runs over, the one named last changes fastest.
Arguments:
- tokens: bfloat16 [2, 24, 73728], P(None, 'lat', 'lon'), may hold values from -6 to 6
- cotangent: bfloat16 [2, 12, 73728], P(None, 'lat', 'lon'), may hold values from -6 to 6
- kinds_one: int32 [1, 4], P(None, 'lat'), may hold values from 0 to 7
- kinds_two: int32 [1, 2], P(None, 'lat'), may hold values from 0 to 7
- table_one: float32 [8, 6, 3312], replicated, may hold values from -2 to 260
- table_two: float32 [8, 12, 3312], replicated, may hold values from -2 to 260
- gain_one: float32 [192], replicated, may hold values from 0.1 to 1.9
- gain_merge: float32 [768], replicated, may hold values from 0.1 to 1.9
- gain_two: float32 [384], replicated, may hold values from 0.1 to 1.9
- qkv_one: bfloat16 [192, 576], replicated, may hold values from -0.4375 to 0.4375
- proj_one: bfloat16 [192, 192], replicated, may hold values from -0.4375 to 0.4375
- merge_weight: bfloat16 [768, 384], replicated, may hold values from -0.21875 to 0.21875
- qkv_two: bfloat16 [384, 1152], replicated, may hold values from -0.3125 to 0.3125
- proj_two: bfloat16 [384, 384], replicated, may hold values from -0.3125 to 0.3125
Outputs:
- result: bfloat16 [2, 12, 73728], P(None, 'lat', 'lon')
- d_tokens: bfloat16 [2, 24, 73728], P(None, 'lat', 'lon')
- grad_qkv_one: bfloat16 [192, 576], replicated
- grad_proj_one: bfloat16 [192, 192], replicated
- grad_merge: bfloat16 [768, 384], replicated
- grad_qkv_two: bfloat16 [384, 1152], replicated
- grad_proj_two: bfloat16 [384, 384], replicated
All inputs are finite; a program needn't handle non-finite values.
Results may differ from a plain program's by a relative error of at most 0.025.
Values may be sent and summed in bfloat16 or wider, within the bound.
No kernel may reach another device: no remote copies, remote signals or barrier semaphores. Data moves between devices by JAX's collectives and lax.ppermute only.
A program may use at most 128 MiB of HBM per device.

v0:
```python
import jax
import jax.numpy as jnp
import numpy as np
from jax import lax
from jax.sharding import PartitionSpec as P

C1 = 192
HEADS1 = 6
HEADS2 = 12
WIN_Z = 2
WIN_LAT = 6
WIN_LON = 12
LEVELS = 2


norm_epsilon = 1e-05
grad_epsilon = 1e-06
masked_score = -1e30


def as_sent(value):
    return jax.tree.map(lambda a: a.astype(jnp.bfloat16) if a.dtype == jnp.float32 else a, value)


def shifted_2(block, axis, distance):
    devices = range(lax.axis_size(axis))
    route = [((i - distance) % len(devices), i) for i in devices]
    return lax.ppermute(block, axis, route)


def relative_table():
    window_size = WIN_Z * WIN_LAT * WIN_LON
    positions = np.arange(window_size)
    level_at = positions // (WIN_LAT * WIN_LON)
    row_at = positions // WIN_LON % WIN_LAT
    col_at = positions % WIN_LON
    joined = (level_at[:, None] * WIN_Z + level_at[None, :]) * (WIN_LAT * WIN_LAT)
    joined = joined + row_at[:, None] * WIN_LAT + row_at[None, :]
    joined = joined * (2 * WIN_LON - 1) + col_at[:, None] - col_at[None, :] + WIN_LON - 1
    return joined.astype(np.int32)


def layer_norm(values, scaling):
    centre = jnp.mean(values, axis=-1, keepdims=True)
    spread = values - centre
    second = jnp.mean(spread * spread, axis=-1, keepdims=True)
    return spread * lax.rsqrt(second + norm_epsilon) * scaling


def to_windows(lattice):
    level_count, row_count, col_count = lattice.shape[:3]
    trailing = lattice.shape[3:]
    trailing_axes = tuple(range(6, 6 + len(trailing)))
    pieces = lattice.reshape(
        (level_count // WIN_Z, WIN_Z, row_count // WIN_LAT, WIN_LAT, col_count // WIN_LON, WIN_LON)
        + trailing
    )
    pieces = pieces.transpose((0, 2, 4, 1, 3, 5) + trailing_axes)
    return pieces.reshape(
        (
            level_count // WIN_Z,
            row_count // WIN_LAT,
            col_count // WIN_LON,
            WIN_Z * WIN_LAT * WIN_LON,
        )
        + trailing
    )


def from_windows(blocks, level_count, row_count, col_count):
    trailing = blocks.shape[4:]
    trailing_axes = tuple(range(6, 6 + len(trailing)))
    pieces = blocks.reshape(
        (level_count // WIN_Z, row_count // WIN_LAT, col_count // WIN_LON, WIN_Z, WIN_LAT, WIN_LON)
        + trailing
    )
    pieces = pieces.transpose((0, 3, 1, 4, 2, 5) + trailing_axes)
    return pieces.reshape((level_count, row_count, col_count) + trailing)


def region_codes(level_count, row_start, row_count, rows_all):
    level_index = jnp.arange(level_count, dtype=jnp.int32)
    level_part = (level_index >= level_count - WIN_Z).astype(jnp.int32) + (
        level_index >= level_count - WIN_Z // 2
    ).astype(jnp.int32)
    row_index = row_start + jnp.arange(row_count, dtype=jnp.int32)
    row_part = (row_index >= rows_all - WIN_LAT).astype(jnp.int32) + (
        row_index >= rows_all - WIN_LAT // 2
    ).astype(jnp.int32)
    return level_part[:, None] * 3 + row_part[None, :]


def attend(
    shifted,
    kind_ids,
    bias_table,
    scaling,
    w_qkv,
    w_proj,
    head_count,
    row_start,
    rows_all,
    probe_qkv,
    probe_proj,
):
    level_count, row_count, col_count, channel_count = shifted.shape
    head_size = channel_count // head_count
    base_values = shifted.astype(jnp.float32)
    normed = layer_norm(base_values, scaling).astype(jnp.bfloat16)
    flat_rows = normed.reshape(-1, channel_count)
    packed = (jnp.dot(flat_rows, w_qkv, preferred_element_type=jnp.float32) + probe_qkv).astype(
        jnp.bfloat16
    )
    packed = to_windows(packed.reshape(level_count, row_count, col_count, 3, head_count, head_size))
    query_rows = packed[..., 0, :, :]
    key_rows = packed[..., 1, :, :]
    value_rows = packed[..., 2, :, :]
    scores = jnp.einsum(
        "abdqhe,abdkhe->abdhqk", query_rows, key_rows, preferred_element_type=jnp.float32
    ) * head_size ** (-0.5)
    chosen = bias_table[kind_ids]
    full_bias = jnp.take(chosen, relative_table(), axis=3)
    scores = scores + full_bias[:, :, None]
    region_ids = region_codes(level_count, row_start, row_count, rows_all)
    tag_values = jnp.broadcast_to(
        region_ids[:, :, None], (level_count, row_count, col_count)
    ).astype(jnp.float32)
    window_tags = to_windows(tag_values)
    allowed = window_tags[..., :, None] == window_tags[..., None, :]
    scores = jnp.where(allowed[:, :, :, None], scores, masked_score)
    row_top = jnp.max(scores, axis=-1, keepdims=True)
    weights = jnp.exp(scores - row_top)
    attn_weights = (weights / jnp.sum(weights, axis=-1, keepdims=True)).astype(jnp.bfloat16)
    attended = jnp.einsum(
        "abdhqk,abdkhe->abdqhe", attn_weights, value_rows, preferred_element_type=jnp.float32
    ).astype(jnp.bfloat16)
    merged_rows = from_windows(attended, level_count, row_count, col_count).reshape(
        -1, channel_count
    )
    result = (
        base_values.reshape(-1, channel_count)
        + jnp.dot(merged_rows, w_proj, preferred_element_type=jnp.float32)
        + probe_proj
    )
    return (result.astype(jnp.bfloat16).reshape(shifted.shape), (flat_rows, merged_rows))


def merge_tokens(level_one, scaling, w_merge, probe_merge):
    level_count, row_count, col_count, channel_count = level_one.shape
    grouped = level_one.reshape(level_count, row_count // 2, 2, col_count // 2, 2, channel_count)
    grouped = grouped.transpose(0, 1, 3, 2, 4, 5).reshape(
        level_count, row_count // 2, col_count // 2, 4 * channel_count
    )
    normed = layer_norm(grouped.astype(jnp.float32), scaling).astype(jnp.bfloat16)
    flat_rows = normed.reshape(-1, 4 * channel_count)
    merged = (jnp.dot(flat_rows, w_merge, preferred_element_type=jnp.float32) + probe_merge).astype(
        jnp.bfloat16
    )
    return (
        merged.reshape(level_count, row_count // 2, col_count // 2, w_merge.shape[1]),
        flat_rows,
    )


def weight_grad(inputs, cot_rows):
    return lax.dot_general(
        inputs,
        cot_rows.astype(jnp.bfloat16),
        (((0,), (0,)), ((), ())),
        preferred_element_type=jnp.float32,
    )


def normalized(gradient):
    scale_back = lax.rsqrt(jnp.mean(gradient * gradient) + grad_epsilon)
    return (gradient * scale_back).astype(jnp.bfloat16)


def lat_move(band_piece, offset):
    return jax.tree.map(
        lambda part, own: part.astype(own.dtype),
        shifted_2(as_sent(band_piece), "lat", offset),
        band_piece,
    )


def lon_move(band_piece, offset):
    return shifted_2(as_sent(band_piece), "lon", offset).astype(band_piece.dtype)


def roll_ahead(lattice, level_step):
    half_lat = WIN_LAT // 2
    half_lon = WIN_LON // 2
    if level_step != 0:
        lattice = jnp.roll(lattice, -level_step, 0)
    lattice = jnp.concatenate([lattice[:, half_lat:], lat_move(lattice[:, :half_lat], -1)], 1)
    return jnp.concatenate([lattice[:, :, half_lon:], lon_move(lattice[:, :, :half_lon], -1)], 2)


def roll_behind(lattice, level_step):
    half_lat = WIN_LAT // 2
    half_lon = WIN_LON // 2
    lattice = jnp.concatenate([lat_move(lattice[:, -half_lat:], 1), lattice[:, :-half_lat]], 1)
    lattice = jnp.concatenate(
        [lon_move(lattice[:, :, -half_lon:], 1), lattice[:, :, :-half_lon]], 2
    )
    if level_step != 0:
        lattice = jnp.roll(lattice, level_step, 0)
    return lattice


def local_pass(shifted, kind_ids, bias_table, scaling, w_qkv, w_proj, head_count):
    level_count, row_count, col_count, channel_count = shifted.shape
    token_count = level_count * row_count * col_count
    row_start = lax.axis_index("lat") * row_count
    rows_all = lax.axis_size("lat") * row_count

    def local_forward(lattice, probe_qkv, probe_proj):
        return attend(
            lattice,
            kind_ids,
            bias_table,
            scaling,
            w_qkv,
            w_proj,
            head_count,
            row_start,
            rows_all,
            probe_qkv,
            probe_proj,
        )

    return jax.vjp(
        local_forward,
        shifted,
        jnp.zeros((token_count, 3 * channel_count), jnp.float32),
        jnp.zeros((token_count, channel_count), jnp.float32),
        has_aux=True,
    )


def merge_pass(level_one, scaling, w_merge):
    token_count = level_one.shape[0] * (level_one.shape[1] // 2) * (level_one.shape[2] // 2)

    def merge_forward(lattice, probe_merge):
        return merge_tokens(lattice, scaling, w_merge, probe_merge)

    return jax.vjp(
        merge_forward,
        level_one,
        jnp.zeros((token_count, w_merge.shape[1]), jnp.float32),
        has_aux=True,
    )


def shards(
    tokens,
    cotangent,
    kinds_one,
    kinds_two,
    table_one,
    table_two,
    gain_one,
    gain_merge,
    gain_two,
    qkv_one,
    proj_one,
    merge_weight,
    qkv_two,
    proj_two,
):
    row_count = tokens.shape[1]
    col_count = tokens.shape[2] // C1
    level_step = WIN_Z // 2
    lattice = tokens.reshape(LEVELS, row_count, col_count, C1)
    shifted_one = roll_ahead(lattice, level_step)
    block_one, pull_one, saved_one = local_pass(
        shifted_one, kinds_one, table_one, gain_one, qkv_one, proj_one, HEADS1
    )
    moved_one = roll_ahead(block_one, 0)
    shifted_two, pull_merge, merged_norm = merge_pass(moved_one, gain_merge, merge_weight)
    block_two, pull_two, saved_two = local_pass(
        shifted_two, kinds_two, table_two, gain_two, qkv_two, proj_two, HEADS2
    )
    level_two = roll_behind(block_two, level_step)
    d_block_two = roll_ahead(cotangent.reshape(level_two.shape), level_step)
    d_shift_two, d_packed_two, d_out_two = pull_two(d_block_two)
    raw_qkv_two = weight_grad(saved_two[0], d_packed_two)
    raw_proj_two = weight_grad(saved_two[1], d_out_two)
    d_moved_one, d_probe_merge = pull_merge(d_shift_two)
    raw_merge = weight_grad(merged_norm, d_probe_merge)
    d_block_one = roll_behind(d_moved_one, 0)
    d_shift_one, d_packed_one, d_out_one = pull_one(d_block_one)
    raw_qkv_one = weight_grad(saved_one[0], d_packed_one)
    raw_proj_one = weight_grad(saved_one[1], d_out_one)
    d_tokens = roll_behind(d_shift_one, level_step)
    raw_qkv_one, raw_proj_one, raw_merge, raw_qkv_two, raw_proj_two = lax.psum(
        (raw_qkv_one, raw_proj_one, raw_merge, raw_qkv_two, raw_proj_two), ("lon", "lat")
    )
    return (
        level_two.reshape(LEVELS, level_two.shape[1], -1),
        d_tokens.reshape(LEVELS, row_count, -1),
        normalized(raw_qkv_one),
        normalized(raw_proj_one),
        normalized(raw_merge),
        normalized(raw_qkv_two),
        normalized(raw_proj_two),
    )


def solution(mesh):
    in_specs = (
        P(None, "lat", "lon"),
        P(None, "lat", "lon"),
        P(None, "lat"),
        P(None, "lat"),
        P(),
        P(),
        P(),
        P(),
        P(),
        P(),
        P(),
        P(),
        P(),
        P(),
    )
    out_specs = (P(None, "lat", "lon"), P(None, "lat", "lon"), P(), P(), P(), P(), P())
    return jax.shard_map(shards, mesh=mesh, in_specs=in_specs, out_specs=out_specs, check_vma=False)
```

profile of v0, /device:TPU:0, one launch (start us, length us, event | category | flops | bytes accessed | tf_op | source)
XLA Modules:
  0.0 513.7 jit_solution(10897284982636518831)
XLA Ops:
  10.4 3.0 collective-permute-start
  20.8 4.5 copy.138
  25.3 55.6 %gather_fusion.1 = f32[20736,2,6]{2,1,0:T(2,128)} fusion(f32[2,6,3312]{1,0,2:T(2,128)S(1)} %copy.138, s32[21504]{0:T(1024)S(1)} %pad_clamp_fusion), kind=kCustom, calls=%fused_computation.1 | custom fusion | bytes 2073600 | tf_op jit(solution)/shard_map/jvp(jit(_take))/gather | solution.py:122
  80.9 31.0 %copy.139 = f32[144,144,2,6]{0,1,3,2:T(8,128)} copy(f32[144,144,2,6]{3,2,1,0:T(2,128)} %bitcast.176) | data formatting | bytes 1990656 | tf_op jit(solution)/shard_map/jvp(jit(_take))/gather | solution.py:122
  112.5 38.8 %gather_fusion.2 = f32[20736,12]{1,0:T(8,128)} fusion(f32[12,3312]{0,1:T(8,128)S(1)} %bitcast.170, s32[21504]{0:T(1024)S(1)} %pad_clamp_fusion), kind=kCustom, calls=%fused_computation.2 | custom fusion | bytes 2073600 | tf_op jit(solution)/shard_map/jvp(jit(_take))/gather | solution.py:122
  151.3 12.2 %copy.152 = f32[144,144,12]{0,1,2:T(8,128)} copy(f32[144,144,12]{2,1,0:T(8,128)} %bitcast.177) | data formatting | bytes 1990656 | tf_op jit(solution)/shard_map/jvp(jit(_take))/gather | solution.py:122
  164.2 4.0 collective-permute-start.1
  175.1 3.9 reshape.727
  179.0 2.7 copy.134
  181.7 2.6 fusion.95
  188.2 2.9 fusion.5
  192.1 3.5 convert_reduce_fusion
  195.7 3.0 copy.192
  198.7 2.7 fusion.23
  201.4 3.1 copy.141
  204.5 2.5 copy.142
  206.9 2.6 reshape.733
  227.3 3.3 collective-permute-start.3
  279.4 3.0 fusion.86
  296.5 2.6 convolution_bitcast_fusion
  302.5 5.7 %collective-permute-done.9 = bf16[2,12,6,192]{3,2,1,0:T(8,128)(2,1)S(1)} collective-permute-done((bf16[2,12,6,192]{3,2,1,0:T(8,128)(2,1)S(1)}, bf16[2,12,6,192]{3,2,1,0:T(8,128)(2,1)S(1)}, u32[]{:S(2)}, u32[]{:S(2)}) %collective-permute-start.9) | collective-permute-done | bytes 55328 | tf_op jit(solution)/shard_map/ppermute | solution.py:28
  311.8 2.6 reshape.747
  314.5 3.1 copy.165
  317.5 3.0 copy.166
  320.6 3.4 fusion.3
  329.3 4.9 copy.171
  334.3 2.5 copy.172
  336.8 2.9 reshape.751
  348.5 4.1 collective-permute-done.4
  354.7 5.9 %collective-permute-done.5 = bf16[2,6,6,384]{3,2,1,0:T(8,128)(2,1)S(1)} collective-permute-done((bf16[2,6,6,384]{3,2,1,0:T(8,128)(2,1)S(1)}, bf16[2,6,6,384]{3,2,1,0:T(8,128)(2,1)S(1)}, u32[]{:S(2)}, u32[]{:S(2)}) %collective-permute-start.5) | collective-permute-done | bytes 55328 | tf_op jit(solution)/shard_map/ppermute | solution.py:28
  361.7 7.4 %collective-permute-done.11 = bf16[2,12,6,192]{3,2,1,0:T(8,128)(2,1)S(1)} collective-permute-done((bf16[2,12,6,192]{3,2,1,0:T(8,128)(2,1)S(1)}, bf16[2,12,6,192]{3,2,1,0:T(8,128)(2,1)S(1)}, u32[]{:S(2)}, u32[]{:S(2)}) %collective-permute-start.11) | collective-permute-done | bytes 55328 | tf_op jit(solution)/shard_map/ppermute | solution.py:28
  370.5 118.8 %all-reduce.9.cloned.1.call-done = (f32[192,576]{1,0:T(8,128)}, f32[192,192]{1,0:T(8,128)}, f32[768,384]{1,0:T(8,128)}, f32[384,1152]{1,0:T(8,128)}, f32[384,384]{1,0:T(8,128)}) async-done(((f32[192,576]{1,0:T(8,128)}, f32[192,192]{1,0:T(8,128)}, f32[768,384]{1,0:T(8,128)}, f32[384,1152]{1,0:T(8,128)}, f32[384,384]{1,0:T(8,128)}), (f32[192,576]{1,0:T(8,128)}, f32[192,192]{1,0:T(8,128)}, ...) | async-done | bytes 4128784 | tf_op jit(solution)/shard_map/psum | solution.py:297
  (347 shorter events, 142.2 us)
Async XLA Ops:
  7.2 10.4 %copy-start = (f32[8,12,3312]{2,0,1:T(8,128)S(1)}, f32[8,12,3312]{2,0,1:T(8,128)}, u32[]{:S(2)}) copy-start(f32[8,12,3312]{2,0,1:T(8,128)} %param.21) | copy-start | bytes 3815428
  7.2 7.6 %copy-start.64 = (s32[20736]{0:T(1024)S(1)}, s32[20736]{0:T(1024)}, u32[]{:S(2)}) copy-start(s32[20736]{0:T(1024)} %constant.162) | copy-start | bytes 248836
  7.2 6.2 %copy-start.55 = (bf16[2,6,4608]{2,0,1:T(2,128)(2,1)S(1)}, bf16[2,6,4608]{2,0,1:T(2,128)(2,1)}, u32[]{:S(2)}) copy-start(bf16[2,6,4608]{2,0,1:T(2,128)(2,1)} %param.17) | copy-start | bytes 331780
  7.2 7.6 %copy-start.81 = (s32[1,2]{1,0:T(1,128)S(1)}, s32[1,2]{1,0:T(1,128)}, u32[]{:S(2)}) copy-start(s32[1,2]{1,0:T(1,128)} %param.18) | copy-start | bytes 28
  7.2 482.1 %all-reduce.9.cloned.1.call-start = ((), (), s32[]{:S(2)}) async-start(), calls=%async_computation | async-start | bytes 8454144 | tf_op jit(solution)/shard_map/psum | solution.py:297
  9.6 9.5 %copy-start.18 = (f32[8,6,3312]{2,0,1:T(8,128)S(1)}, f32[8,6,3312]{2,0,1:T(8,128)}, u32[]{:S(2)}) copy-start(f32[8,6,3312]{2,0,1:T(8,128)} %param.20) | copy-start | bytes 1907716
  10.4 153.7 %collective-permute-start = (bf16[2,3,24,192]{3,2,1,0:T(8,128)(2,1)}, bf16[2,3,24,192]{3,2,1,0:T(8,128)(2,1)S(1)}, u32[]{:S(2)}, u32[]{:S(2)}) collective-permute-start(bf16[2,3,24,192]{3,2,1,0:T(8,128)(2,1)} %slice.192), channel_id=1, source_target_pairs={{1,0},{0,1},{3,2},{2,3},{5,4},{4,5},{7,6},{6,7},{9,8},{8,9},{11,10... | collective-permute-start | bytes 165896 | tf_op jit(solution)/shard_map/ppermute | solution.py:28
  14.8 153.3 %collective-permute-start.6 = (bf16[2,3,12,384]{3,2,1,0:T(8,128)(2,1)}, bf16[2,3,12,384]{3,2,1,0:T(8,128)(2,1)}, u32[]{:S(2)}, u32[]{:S(2)}) collective-permute-start(bf16[2,3,12,384]{3,2,1,0:T(8,128)(2,1)} %get-tuple-element.59), channel_id=1, source_target_pairs={{1,0},{0,1},{3,2},{2,3},{5,4},{4,5},{7,6},{6,7},{9,8},{8,9},{11,10... | collective-permute-start | bytes 165896 | tf_op jit(solution)/shard_map/ppermute | solution.py:28
  80.9 31.0 %copy-start.49 = (f32[1,12,3312]{2,0,1:T(1,128)S(1)}, f32[1,12,3312]{2,0,1:T(1,128)}, u32[]{:S(2)}) copy-start(f32[1,12,3312]{2,0,1:T(1,128)} %constant_dynamic-slice_fusion) | copy-start | bytes 476932
  151.3 12.2 %copy-start.69 = (f32[768]{0:T(1024)S(1)}, f32[768]{0:T(1024)}, u32[]{:S(2)}) copy-start(f32[768]{0:T(1024)} %param.23) | copy-start | bytes 9220
  151.3 12.8 %copy-start.29 = (bf16[2,9,24,192]{3,2,1,0:T(8,128)(2,1)S(1)}, bf16[2,9,24,192]{3,2,1,0:T(8,128)(2,1)}, u32[]{:S(2)}) copy-start(bf16[2,9,24,192]{3,2,1,0:T(8,128)(2,1)} %slice.191) | copy-start | bytes 497668
  151.3 16.8 %copy-start.59 = (bf16[2,3,12,384]{3,2,1,0:T(8,128)(2,1)S(1)}, bf16[2,3,12,384]{3,2,1,0:T(8,128)(2,1)}, u32[]{:S(2)}) copy-start(bf16[2,3,12,384]{3,2,1,0:T(8,128)(2,1)} %get-tuple-element.58) | copy-start | bytes 165892
  164.2 7.3 %collective-permute-start.1 = (bf16[2,12,6,192]{3,2,1,0:T(8,128)(2,1)S(1)}, bf16[2,12,6,192]{3,2,1,0:T(8,128)(2,1)S(1)}, u32[]{:S(2)}, u32[]{:S(2)}) collective-permute-start(bf16[2,12,6,192]{3,2,1,0:T(8,128)(2,1)S(1)} %pad_maximum_fusion.9), channel_id=1, source_target_pairs={{2,0},{4,2},{6,4},{8,6},{10,8},{12,10},{14,12},{16,14},{18,16},{20... | collective-permute-start | bytes 165896 | tf_op jit(solution)/shard_map/ppermute | solution.py:28
  169.7 4.0 copy-start.46
  169.7 4.0 copy-start.75
  169.7 46.8 %collective-permute-start.7 = (bf16[2,6,6,384]{3,2,1,0:T(8,128)(2,1)}, bf16[2,6,6,384]{3,2,1,0:T(8,128)(2,1)}, u32[]{:S(2)}, u32[]{:S(2)}) collective-permute-start(bf16[2,6,6,384]{3,2,1,0:T(8,128)(2,1)} %get-tuple-element.57), channel_id=1, source_target_pairs={{2,0},{4,2},{6,4},{8,6},{10,8},{12,10},{14,12},{16,14},{18,16},{20... | collective-permute-start | bytes 165896 | tf_op jit(solution)/shard_map/ppermute | solution.py:28
  192.1 3.5 copy-start.52
  215.0 11.4 %collective-permute-start.2 = (bf16[2,3,24,192]{3,2,1,0:T(8,128)(2,1)}, bf16[2,3,24,192]{3,2,1,0:T(8,128)(2,1)}, u32[]{:S(2)}, u32[]{:S(2)}) collective-permute-start(bf16[2,3,24,192]{3,2,1,0:T(8,128)(2,1)} %slice.199), channel_id=1, source_target_pairs={{1,0},{0,1},{3,2},{2,3},{5,4},{4,5},{7,6},{6,7},{9,8},{8,9},{11,10... | collective-permute-start | bytes 165896 | tf_op jit(solution)/shard_map/ppermute | solution.py:28
  227.3 5.5 %collective-permute-start.3 = (bf16[2,12,6,192]{3,2,1,0:T(8,128)(2,1)S(1)}, bf16[2,12,6,192]{3,2,1,0:T(8,128)(2,1)S(1)}, u32[]{:S(2)}, u32[]{:S(2)}) collective-permute-start(bf16[2,12,6,192]{3,2,1,0:T(8,128)(2,1)S(1)} %pad_maximum_fusion.8), channel_id=1, source_target_pairs={{2,0},{4,2},{6,4},{8,6},{10,8},{12,10},{14,12},{16,14},{18,16},{20... | collective-permute-start | bytes 165896 | tf_op jit(solution)/shard_map/ppermute | solution.py:28
  293.0 7.4 %collective-permute-start.8 = (bf16[2,3,24,192]{3,2,1,0:T(8,128)(2,1)}, bf16[2,3,24,192]{3,2,1,0:T(8,128)(2,1)}, u32[]{:S(2)}, u32[]{:S(2)}) collective-permute-start(bf16[2,3,24,192]{3,2,1,0:T(8,128)(2,1)} %copy.195), channel_id=1, source_target_pairs={{1,0},{0,1},{3,2},{2,3},{5,4},{4,5},{7,6},{6,7},{9,8},{8,9},{11,10... | collective-permute-start | bytes 165896 | tf_op jit(solution)/shard_map/ppermute | solution.py:28
  296.5 3.8 copy-start.44
  299.0 10.0 %copy-start.58 = (bf16[192,192]{1,0:T(8,128)(2,1)S(1)}, bf16[192,192]{1,0:T(8,128)(2,1)}, u32[]{:S(2)}) copy-start(bf16[192,192]{1,0:T(8,128)(2,1)} %param.26) | copy-start | bytes 221188
  300.3 8.1 %copy-start.32 = (bf16[12,32,144]{2,1,0:T(8,128)(2,1)}, bf16[12,32,144]{2,1,0:T(8,128)(2,1)S(1)}, u32[]{:S(2)}) copy-start(bf16[12,32,144]{2,1,0:T(8,128)(2,1)S(1)} %convolution_convert_fusion.12) | copy-start | bytes 331780
  301.4 6.8 %copy-start.30 = (bf16[2,12,24,192]{3,2,1,0:T(8,128)(2,1)}, bf16[2,12,24,192]{3,2,1,0:T(8,128)(2,1)S(1)}, u32[]{:S(2)}) copy-start(bf16[2,12,24,192]{3,2,1,0:T(8,128)(2,1)S(1)} %copy_dynamic-update-slice_fusion) | copy-start | bytes 663556
  301.4 6.8 %collective-permute-start.9 = (bf16[2,12,6,192]{3,2,1,0:T(8,128)(2,1)S(1)}, bf16[2,12,6,192]{3,2,1,0:T(8,128)(2,1)S(1)}, u32[]{:S(2)}, u32[]{:S(2)}) collective-permute-start(bf16[2,12,6,192]{3,2,1,0:T(8,128)(2,1)S(1)} %slice.217), channel_id=1, source_target_pairs={{30,0},{0,2},{2,4},{4,6},{6,8},{8,10},{10,12},{12,14},{14,16},{16,... | collective-permute-start | bytes 165896 | tf_op jit(solution)/shard_map/ppermute | solution.py:28
  346.9 5.7 %collective-permute-start.4 = (bf16[2,3,12,384]{3,2,1,0:T(8,128)(2,1)S(1)}, bf16[2,3,12,384]{3,2,1,0:T(8,128)(2,1)S(1)}, u32[]{:S(2)}, u32[]{:S(2)}) collective-permute-start(bf16[2,3,12,384]{3,2,1,0:T(8,128)(2,1)S(1)} %get-tuple-element.62), channel_id=1, source_target_pairs={{1,0},{0,1},{3,2},{2,3},{5,4},{4,5},{7,6},{6,7},{9,8},{8,9},{11,10... | collective-permute-start | bytes 165896 | tf_op jit(solution)/shard_map/ppermute | solution.py:28
  352.7 7.9 %collective-permute-start.5 = (bf16[2,6,6,384]{3,2,1,0:T(8,128)(2,1)S(1)}, bf16[2,6,6,384]{3,2,1,0:T(8,128)(2,1)S(1)}, u32[]{:S(2)}, u32[]{:S(2)}) collective-permute-start(bf16[2,6,6,384]{3,2,1,0:T(8,128)(2,1)S(1)} %fusion.69), channel_id=1, source_target_pairs={{30,0},{0,2},{2,4},{4,6},{6,8},{8,10},{10,12},{12,14},{14,16},{16,... | collective-permute-start | bytes 165896 | tf_op jit(solution)/shard_map/ppermute | solution.py:28
  352.7 7.9 %collective-permute-start.10 = (bf16[2,3,24,192]{3,2,1,0:T(8,128)(2,1)S(1)}, bf16[2,3,24,192]{3,2,1,0:T(8,128)(2,1)S(1)}, u32[]{:S(2)}, u32[]{:S(2)}) collective-permute-start(bf16[2,3,24,192]{3,2,1,0:T(8,128)(2,1)S(1)} %slice.219), channel_id=1, source_target_pairs={{1,0},{0,1},{3,2},{2,3},{5,4},{4,5},{7,6},{6,7},{9,8},{8,9},{11,10... | collective-permute-start | bytes 165896 | tf_op jit(solution)/shard_map/ppermute | solution.py:28
  360.7 8.4 %collective-permute-start.11 = (bf16[2,12,6,192]{3,2,1,0:T(8,128)(2,1)S(1)}, bf16[2,12,6,192]{3,2,1,0:T(8,128)(2,1)S(1)}, u32[]{:S(2)}, u32[]{:S(2)}) collective-permute-start(bf16[2,12,6,192]{3,2,1,0:T(8,128)(2,1)S(1)} %pad_maximum_fusion.7), channel_id=1, source_target_pairs={{30,0},{0,2},{2,4},{4,6},{6,8},{8,10},{10,12},{12,14},{14,16},{16,... | collective-permute-start | bytes 165896 | tf_op jit(solution)/shard_map/ppermute | solution.py:28
  489.4 8.3 %copy-start.17 = (f32[768,384]{1,0:T(8,128)S(1)}, f32[768,384]{1,0:T(8,128)}, u32[]{:S(2)}) copy-start(f32[768,384]{1,0:T(8,128)} %get-tuple-element.31) | copy-start | bytes 3538948
  493.7 6.5 %copy-start.14 = (f32[384,1152]{1,0:T(8,128)S(1)}, f32[384,1152]{1,0:T(8,128)}, u32[]{:S(2)}) copy-start(f32[384,1152]{1,0:T(8,128)} %get-tuple-element.32) | copy-start | bytes 5308420
  501.9 4.8 copy-start.1
  (63 other events, 103.1 us)
Sparse Core Ops, SparseCore 0:
  345.5 143.7 all-reduce.8
where the time goes:
time: 523 us; the launch traced here: 514 us
  local copies, waits for them, and re-layouts  246 us (47%)
  waiting for transfers between devices  143 us (27%)
  other arithmetic  46.4 us (9%)
  matrix products  40.4 us (8%)
  between operations  19.7 us (4%)
  starting transfers between devices  17.7 us (3%)
    gather x4, local copies, waits for them, and re-layouts, attend(): full_bias = jnp.take(chosen, relative_table(), axis=3)  138 us
    psum x1, waiting for transfers between devices, shards(): lax.psum((raw_qkv_one, raw_proj_one, raw_merge, raw_qkv_two, raw_proj_two...  119 us
    ppermute x12, waiting for transfers between devices, shifted_2(): return lax.ppermute(block, axis, route)  24.3 us
    unnamed x171, local copies, waits for them, and re-layouts  18.2 us
    ppermute x12, starting transfers between devices, shifted_2(): return lax.ppermute(block, axis, route)  17.7 us
  transfers between devices with their start and end apart: 13, of which 6 were waited for; matrix products, arithmetic and copies ran while one was open for 42% of the time, Pallas kernels for 0%

commit v1 on v0

v1 whole, which is shorter than its diff:
```python
import functools

import jax
import jax.numpy as jnp
import numpy as np
from jax import lax
from jax.experimental import pallas as pl
from jax.experimental.pallas import tpu as pltpu
from jax.sharding import PartitionSpec as P

HEADS1 = 6
HEADS2 = 12
HEAD = 32
WIN_LAT = 6
WIN_LON = 12
HALF_LAT = WIN_LAT // 2
HALF_LON = WIN_LON // 2
SPOTS = WIN_LAT * WIN_LON
SPAN = 2 * WIN_LON - 1
LEVELS = 2

norm_epsilon = 1e-05
grad_epsilon = 1e-06
masked_score = -1e30

f32 = jnp.float32
bf16 = jnp.bfloat16
AXES = ("lon", "lat")


def rounded_up(count, step):
    return -(-count // step) * step


def mm(a, b):
    return lax.dot_general(a, b, (((1,), (0,)), ((), ())), preferred_element_type=f32)


def mm_nt(a, b):
    return lax.dot_general(a, b, (((1,), (1,)), ((), ())), preferred_element_type=f32)


def mm_tn(a, b):
    return lax.dot_general(a, b, (((0,), (0,)), ((), ())), preferred_element_type=f32)


def parts_rows(rows, cols, ahead):
    keep_r, keep_c = rows - HALF_LAT, cols - HALF_LON
    if ahead:
        row_sets = (range(HALF_LAT, rows), range(HALF_LAT))
        col_sets = (range(HALF_LON, cols), range(HALF_LON))
    else:
        row_sets = (range(keep_r), range(keep_r, rows))
        col_sets = (range(keep_c), range(keep_c, cols))
    out = []
    for rset, cset in ((0, 0), (1, 0), (0, 1), (1, 1)):
        piece = [(z, j, k) for z in range(LEVELS) for j in row_sets[rset] for k in col_sets[cset]]
        piece += [None] * (rounded_up(len(piece), 16) - len(piece))
        out.append(piece)
    return out


def window_rows(rows, cols):
    return [
        (z, b * WIN_LAT + ap, c * WIN_LON + bp)
        for b in range(rows // WIN_LAT)
        for c in range(cols // WIN_LON)
        for z in range(LEVELS)
        for ap in range(WIN_LAT)
        for bp in range(WIN_LON)
    ]


def merge_rows(rows, cols):
    return [
        (z, 2 * jj + a, 2 * kk + b)
        for a in range(2)
        for b in range(2)
        for z in range(LEVELS)
        for jj in range(rows // 2)
        for kk in range(cols // 2)
    ]


def lane_rows(rows, cols, pad):
    out = []
    for k in range(cols):
        group = [(1 - z, j, k) for j in range(rows) for z in range(LEVELS)]
        out += group + [None] * (pad - len(group))
    return out


def index_of(wanted, source):
    where = {spot: n for n, spot in enumerate(source) if spot is not None}
    return [-1 if spot is None else where[spot] for spot in wanted]


def flat(pieces):
    return [spot for piece in pieces for spot in piece]


def moved(pieces, dj, dk, rows, cols):
    return [
        None if s is None else (s[0], (s[1] + dj) % rows, (s[2] + dk) % cols) for s in flat(pieces)
    ]


def one_hot(index_ref, column, count, width):
    index = index_ref[0:count, column : column + 1]
    lanes = lax.broadcasted_iota(jnp.int32, (count, width), 1)
    return jnp.where(index == lanes, 1.0, 0.0).astype(bf16)


def lane_head_masks(width):
    lanes = lax.broadcasted_iota(jnp.int32, (1, width), 1)
    return [
        jnp.where((lanes >= h * HEAD) & (lanes < (h + 1) * HEAD), 1.0, 0.0).astype(f32)
        for h in range(width // HEAD)
    ]


def spread_heads(values, masks):
    return jnp.concatenate([values * m for m in masks], axis=0)


def gather_heads(stack, masks):
    total = stack[0:SPOTS] * masks[0]
    for h in range(1, len(masks)):
        total = total + stack[h * SPOTS : (h + 1) * SPOTS] * masks[h]
    return total


def head_groups(channels):
    out = []
    at = 0
    while at < channels:
        width = min(128, channels - at)
        out.append((at, width))
        at += width
    return out


def rms_stats(values):
    centre = jnp.mean(values, axis=-1, keepdims=True)
    spread = values - centre
    second = jnp.mean(spread * spread, axis=-1, keepdims=True)
    scale = lax.rsqrt(second + norm_epsilon)
    return spread * scale, scale


def norm_back(hat, scale, d_hat, count):
    first = jnp.sum(d_hat, axis=-1, keepdims=True) * (1.0 / count)
    second = jnp.sum(d_hat * hat, axis=-1, keepdims=True) * (1.0 / count)
    return scale * (d_hat - first - hat * second)


def softmax_rows(scores):
    top = jnp.max(scores, axis=-1, keepdims=True)
    weights = jnp.exp(scores - top)
    return weights / jnp.sum(weights, axis=-1, keepdims=True)


def bias_kernel(kinds_one, kinds_two, last, table_one, table_two, target, out_one, out_two, rows_ref, runs_ref):
    bands = out_one.shape[0] // LEVELS
    head_sets = [(8 * b, HEADS1) for b in range(bands)] + [(8 * bands, HEADS2)]
    width = WIN_LAT * SPAN
    slots = rows_ref.shape[0]
    rows_ref[...] = jnp.zeros(rows_ref.shape, f32)
    for b in range(bands):
        for h in range(HEADS1):
            rows_ref[8 * b + h : 8 * b + h + 1, :] = table_one[h, pl.ds(kinds_one[b], 1), :]
    for h in range(HEADS2):
        at = 8 * bands + h
        rows_ref[at : at + 1, :] = table_two[h, pl.ds(kinds_two[0], 1), :]
    runs_ref[...] = jnp.zeros(runs_ref.shape, f32)
    for z in range(LEVELS):
        for ap in range(WIN_LAT):
            start = (z * (LEVELS + 1)) * WIN_LAT * width + ap * width
            at = (z * WIN_LAT + ap) * slots
            runs_ref[at : at + slots, 0:width] = rows_ref[:, start : start + width]
    runs = runs_ref[...]
    high = runs.astype(bf16)
    rest = runs - high.astype(f32)
    middle = rest.astype(bf16)
    low = (rest - middle.astype(f32)).astype(bf16)
    sub = lax.broadcasted_iota(jnp.int32, (256, target.shape[1]), 0)
    pick = jnp.where(sub == target[0:1, :], 1.0, 0.0).astype(bf16)
    full = mm(high, pick) + mm(middle, pick) + mm(low, pick)
    lanes = lax.broadcasted_iota(jnp.int32, (1, 128), 1)
    for z in range(LEVELS):
        for ap in range(WIN_LAT):
            across = jnp.where(
                (lanes >= SPOTS // 2) if ap < HALF_LAT else (lanes < SPOTS // 2), masked_score, 0.0
            )
            at = (z * WIN_LAT + ap) * slots
            for s, (first, heads) in enumerate(head_sets):
                own = across * last[s].astype(f32)
                for bp in range(WIN_LON):
                    piece = full[at + first : at + first + heads, 128 * bp : 128 * bp + 128] + own
                    spot = ap * WIN_LON + bp
                    if s < bands:
                        out_one[s * LEVELS + z, pl.ds(spot, heads, stride=SPOTS), :] = piece
                    else:
                        out_two[z, pl.ds(spot, heads, stride=SPOTS), :] = piece


def expand_bias(kinds_one, kinds_two, last, table_one, table_two):
    bands = kinds_one.shape[0]
    target = np.full((8, WIN_LON * 128), -1, np.int32)
    for bp in range(WIN_LON):
        for aq in range(WIN_LAT):
            for bq in range(WIN_LON):
                target[:, bp * 128 + aq * WIN_LON + bq] = aq * SPAN + bp - bq + WIN_LON - 1
    slots = 8 * bands + rounded_up(HEADS2, 8)
    smem = pl.BlockSpec(memory_space=pltpu.SMEM)
    vmem = pl.BlockSpec(memory_space=pltpu.VMEM)
    return pl.pallas_call(
        bias_kernel,
        name="bias",
        in_specs=[smem, smem, smem, vmem, vmem, vmem],
        out_specs=[vmem, vmem],
        out_shape=(
            jax.ShapeDtypeStruct((bands * LEVELS, HEADS1 * SPOTS, 128), f32),
            jax.ShapeDtypeStruct((LEVELS, HEADS2 * SPOTS, 128), f32),
        ),
        scratch_shapes=[
            pltpu.VMEM((slots, table_one.shape[2]), f32),
            pltpu.VMEM((LEVELS * WIN_LAT * slots, 256), f32),
        ],
    )(kinds_one, kinds_two, last, table_one, table_two, target)


def unlace(main, lat, lon, diag, lace_ref, cut_row, cut_lane):
    rows = main.shape[0]
    lanes = main.shape[2]
    kept = lanes - cut_lane
    for j in range(rows - cut_row):
        lace_ref[2 * j : 2 * j + 2, 0:kept] = main[j + cut_row, :, cut_lane:lanes].astype(f32)
        lace_ref[2 * j : 2 * j + 2, kept:lanes] = lon[j].astype(f32)
    for n in range(cut_row):
        j = rows - cut_row + n
        lace_ref[2 * j : 2 * j + 2, 0:kept] = lat[n].astype(f32)
        lace_ref[2 * j : 2 * j + 2, kept:lanes] = diag[n].astype(f32)


def lace_out(lace_ref, main, lat, lon, diag, cut_row, cut_lane):
    rows = main.shape[0] + cut_row
    kept = main.shape[2]
    lanes = kept + cut_lane
    for j in range(rows - cut_row):
        main[j] = lace_ref[2 * j : 2 * j + 2, 0:kept].astype(bf16)
        lon[j] = lace_ref[2 * j : 2 * j + 2, kept:lanes].astype(bf16)
    for n in range(cut_row):
        j = rows - cut_row + n
        lat[n] = lace_ref[2 * j : 2 * j + 2, 0:kept].astype(bf16)
        diag[n] = lace_ref[2 * j : 2 * j + 2, kept:lanes].astype(bf16)


def forward_one_kernel(
    main, lat, lon, diag, bias, gain, w_qkv, w_proj, index,
    out_main, out_lat, out_lon, out_diag, keep_x, keep_packed, keep_probs, keep_att,
    lace_ref, packed_ref, att_ref,
    *, cols, columns,
):
    channels = gain.shape[1]
    lace_rows = lace_ref.shape[0]
    count = lace_rows * cols
    unlace(main, lat, lon, diag, lace_ref, HALF_LAT, HALF_LON * channels)
    stacked = jnp.concatenate(
        [lace_ref[:, channels * k : channels * (k + 1)] for k in range(cols)], axis=0
    ).astype(bf16)
    values = mm(one_hot(index, columns[0], count, count), stacked)
    hat, _ = rms_stats(values)
    normed = (hat * gain[0:1, :]).astype(bf16)
    packed = mm(normed, w_qkv[...]).astype(bf16)
    packed_ref[...] = packed.astype(f32)
    keep_packed[...] = packed
    keep_x[...] = values.astype(bf16)
    units = count // SPOTS
    bands_span = bias.shape[0] // LEVELS
    per_band = units // bands_span
    for u in range(units):
        band, level = u // per_band, u % LEVELS
        r0 = u * SPOTS
        for at, width in head_groups(channels):
            masks = lane_head_masks(width)
            h0 = at // HEAD
            query = packed_ref[r0 : r0 + SPOTS, at : at + width]
            key = packed_ref[r0 : r0 + SPOTS, channels + at : channels + at + width].astype(bf16)
            value = packed_ref[r0 : r0 + SPOTS, 2 * channels + at : 2 * channels + at + width].astype(bf16)
            rows = slice(h0 * SPOTS, (h0 + len(masks)) * SPOTS)
            scores = mm_nt(spread_heads(query, masks).astype(bf16), key) * HEAD ** (-0.5)
            scores = scores + bias[band * LEVELS + level, rows, 0:SPOTS]
            probs = softmax_rows(scores).astype(bf16)
            keep_probs[u, rows, 0:SPOTS] = probs
            att_ref[r0 : r0 + SPOTS, at : at + width] = gather_heads(mm(probs, value), masks)
    attended = att_ref[...].astype(bf16)
    keep_att[...] = attended
    block = (values + mm(attended, w_proj[...])).astype(bf16)
    start = 0
    total = out_main.shape[0] + out_lat.shape[0] + out_lon.shape[0] + out_diag.shape[0]
    parts = mm(one_hot(index, columns[1], total, count), block).astype(bf16)
    for out in (out_main, out_lat, out_lon, out_diag):
        out[...] = parts[start : start + out.shape[0]]
        start += out.shape[0]


def merge_two_kernel(
    core, main, lat, lon, diag, cot_main, cot_lat, cot_lon, cot_diag, bias,
    gain_merge, gain_two, w_merge, w_qkv, w_proj, index,
    res_main, res_lat, res_lon, res_diag, d_main, d_lat, d_lon, d_diag, sums_keep, sums_send,
    lace_ref, probs_ref, packed_ref, att_ref, d_packed_ref, sums_ref,
    *, cols, columns,
):
    channels = gain_two.shape[1]
    thin = main.shape[1]
    groups = gain_merge.shape[1] // thin
    tokens = LEVELS * SPOTS
    total = main.shape[0] + lat.shape[0] + lon.shape[0] + diag.shape[0]
    stacked = jnp.concatenate([main[...], lat[...], lon[...], diag[...]], axis=0)
    grouped = mm(one_hot(index, columns[0], groups * tokens, total), stacked)
    pieces = [grouped[g * tokens : (g + 1) * tokens] for g in range(groups)]
    wide = groups * thin
    centre = sum(jnp.sum(p, axis=-1, keepdims=True) for p in pieces) * (1.0 / wide)
    spreads = [p - centre for p in pieces]
    second = sum(jnp.sum(s * s, axis=-1, keepdims=True) for s in spreads) * (1.0 / wide)
    scale_merge = lax.rsqrt(second + norm_epsilon)
    hats = [s * scale_merge for s in spreads]
    gains = [gain_merge[0:1, g * thin : (g + 1) * thin] for g in range(groups)]
    merged_norm = [(hats[g] * gains[g]).astype(bf16) for g in range(groups)]
    merged = mm(merged_norm[0], w_merge[0:thin, :])
    for g in range(1, groups):
        merged = merged + mm(merged_norm[g], w_merge[g * thin : (g + 1) * thin, :])
    merged = merged.astype(bf16).astype(f32)
    hat, scale_two = rms_stats(merged)
    normed = (hat * gain_two[0:1, :]).astype(bf16)
    packed_ref[...] = mm(normed, w_qkv[...]).astype(bf16).astype(f32)
    masks = lane_head_masks(128)
    per = len(masks)
    for z in range(LEVELS):
        r0 = z * SPOTS
        for at, width in head_groups(channels):
            h0 = at // HEAD
            rows = slice(h0 * SPOTS, (h0 + per) * SPOTS)
            query = packed_ref[r0 : r0 + SPOTS, at : at + width]
            key = packed_ref[r0 : r0 + SPOTS, channels + at : channels + at + width].astype(bf16)
            value = packed_ref[r0 : r0 + SPOTS, 2 * channels + at : 2 * channels + at + width].astype(bf16)
            scores = mm_nt(spread_heads(query, masks).astype(bf16), key) * HEAD ** (-0.5)
            probs = softmax_rows(scores + bias[z, rows, 0:SPOTS])
            probs_ref[z, rows, 0:SPOTS] = probs
            att_ref[r0 : r0 + SPOTS, at : at + width] = gather_heads(mm(probs.astype(bf16), value), masks)
    attended = att_ref[...].astype(bf16)
    block = (merged + mm(attended, w_proj[...])).astype(bf16)
    lace_rows = lace_ref.shape[0]
    lattice = mm(one_hot(index, columns[1], lace_rows * cols, tokens), block)
    for k in range(cols):
        lace_ref[:, channels * k : channels * (k + 1)] = lattice[lace_rows * k : lace_rows * (k + 1)]
    lace_out(lace_ref, res_main, res_lat, res_lon, res_diag, HALF_LAT, HALF_LON * channels)
    lace_ref[...] = jnp.zeros(lace_ref.shape, f32)
    unlace(cot_main, cot_lat, cot_lon, cot_diag, lace_ref, HALF_LAT, HALF_LON * channels)
    cot_stack = jnp.concatenate(
        [lace_ref[:, channels * k : channels * (k + 1)] for k in range(cols)], axis=0
    ).astype(bf16)
    d_block = mm(one_hot(index, columns[2], tokens, lace_rows * cols), cot_stack)
    d_block_low = d_block.astype(bf16)
    at_sum = groups * thin
    sums_ref[at_sum : at_sum + channels, :] = mm_tn(attended, d_block_low)
    att_ref[...] = mm_nt(d_block_low, w_proj[...]).astype(bf16).astype(f32)
    for z in range(LEVELS):
        r0 = z * SPOTS
        for at, width in head_groups(channels):
            h0 = at // HEAD
            rows = slice(h0 * SPOTS, (h0 + per) * SPOTS)
            attention_back(
                packed_ref, att_ref, d_packed_ref, probs_ref[z, rows, 0:SPOTS], masks, r0, at, width, channels
            )
    d_packed = d_packed_ref[...].astype(bf16)
    at_sum += channels
    for n in range(3):
        sums_ref[at_sum + n * channels : at_sum + (n + 1) * channels, :] = mm_tn(
            normed, d_packed[:, n * channels : (n + 1) * channels]
        )
    d_normed = mm_nt(d_packed, w_qkv[...]).astype(bf16).astype(f32)
    d_merged = d_block + norm_back(hat, scale_two, d_normed * gain_two[0:1, :], channels)
    d_merged = d_merged.astype(bf16)
    d_hats = []
    for g in range(groups):
        sums_ref[g * thin : (g + 1) * thin, :] = mm_tn(merged_norm[g], d_merged)
        d_norm = mm_nt(d_merged, w_merge[g * thin : (g + 1) * thin, :]).astype(bf16).astype(f32)
        d_hats.append(d_norm * gains[g])
    first = sum(jnp.sum(d, axis=-1, keepdims=True) for d in d_hats) * (1.0 / wide)
    cross = sum(jnp.sum(d * h, axis=-1, keepdims=True) for d, h in zip(d_hats, hats)) * (1.0 / wide)
    d_group = jnp.concatenate(
        [scale_merge * (d_hats[g] - first - hats[g] * cross) for g in range(groups)], axis=0
    ).astype(bf16)
    parts = mm(one_hot(index, columns[3], total, groups * tokens), d_group).astype(bf16)
    start = 0
    for out in (d_main, d_lat, d_lon, d_diag):
        out[...] = parts[start : start + out.shape[0]]
        start += out.shape[0]
    half = sums_ref.shape[0] // 2
    mine = core[0]
    first_row = pl.multiple_of(mine * half, 16)
    other_row = pl.multiple_of((1 - mine) * half, 16)
    sums_keep[...] = sums_ref[pl.ds(first_row, half), :].astype(bf16)
    sums_send[...] = sums_ref[pl.ds(other_row, half), :].astype(bf16)


def attention_back(packed_ref, d_att_ref, d_packed_ref, probs, masks, r0, at, width, channels):
    query = packed_ref[r0 : r0 + SPOTS, at : at + width]
    key = packed_ref[r0 : r0 + SPOTS, channels + at : channels + at + width].astype(bf16)
    value = packed_ref[r0 : r0 + SPOTS, 2 * channels + at : 2 * channels + at + width].astype(bf16)
    d_att = spread_heads(d_att_ref[r0 : r0 + SPOTS, at : at + width], masks).astype(bf16)
    probs_low = probs.astype(bf16)
    probs = probs.astype(f32)
    d_probs = mm_nt(d_att, value).astype(bf16).astype(f32)
    d_value = mm_tn(probs_low, d_att)
    inner = jnp.sum(probs * d_probs, axis=-1, keepdims=True)
    d_scores = (probs * (d_probs - inner) * HEAD ** (-0.5)).astype(bf16)
    d_query = gather_heads(mm(d_scores, key), masks)
    d_key = mm_tn(d_scores, spread_heads(query, masks).astype(bf16))
    d_packed_ref[r0 : r0 + SPOTS, at : at + width] = d_query
    d_packed_ref[r0 : r0 + SPOTS, channels + at : channels + at + width] = d_key
    d_packed_ref[r0 : r0 + SPOTS, 2 * channels + at : 2 * channels + at + width] = d_value


def backward_one_kernel(
    core, main, lat, lon, diag, keep_x, keep_packed, keep_probs, keep_att, gain, w_qkv, w_proj, index,
    out_main, out_lat, out_lon, out_diag, sums_keep, sums_send,
    lace_ref, packed_ref, att_ref, d_packed_ref, sums_ref,
    *, cols, columns,
):
    channels = gain.shape[1]
    lace_rows = lace_ref.shape[0]
    count = lace_rows * cols
    total = main.shape[0] + lat.shape[0] + lon.shape[0] + diag.shape[0]
    stacked = jnp.concatenate([main[...], lat[...], lon[...], diag[...]], axis=0)
    d_block = mm(one_hot(index, columns[0], count, total), stacked)
    d_block_low = d_block.astype(bf16)
    hat, scale = rms_stats(keep_x[...].astype(f32))
    normed = (hat * gain[0:1, :]).astype(bf16)
    packed_ref[...] = keep_packed[...].astype(f32)
    att_ref[...] = mm_nt(d_block_low, w_proj[...]).astype(bf16).astype(f32)
    for u in range(count // SPOTS):
        r0 = u * SPOTS
        for at, width in head_groups(channels):
            masks = lane_head_masks(width)
            h0 = at // HEAD
            rows = slice(h0 * SPOTS, (h0 + len(masks)) * SPOTS)
            attention_back(
                packed_ref, att_ref, d_packed_ref, keep_probs[u, rows, 0:SPOTS], masks, r0, at, width, channels
            )
    d_packed = d_packed_ref[...].astype(bf16)
    sums_ref[:, 0 : 3 * channels] = mm_tn(normed, d_packed)
    sums_ref[:, 3 * channels : 4 * channels] = mm_tn(keep_att[...], d_block_low)
    d_normed = mm_nt(d_packed, w_qkv[...]).astype(bf16).astype(f32)
    d_shift = d_block + norm_back(hat, scale, d_normed * gain[0:1, :], channels)
    lattice = mm(one_hot(index, columns[1], count, count), d_shift.astype(bf16))
    for k in range(cols):
        lace_ref[:, channels * k : channels * (k + 1)] = lattice[lace_rows * k : lace_rows * (k + 1)]
    lace_out(lace_ref, out_main, out_lat, out_lon, out_diag, HALF_LAT, HALF_LON * channels)
    mine = core[0]
    half = 2 * channels
    low = sums_ref[:, 0:half].astype(bf16)
    high = sums_ref[:, half : 2 * half].astype(bf16)

    @pl.when(mine == 0)
    def _():
        sums_keep[...] = low
        sums_send[...] = high

    @pl.when(mine != 0)
    def _():
        sums_keep[...] = high
        sums_send[...] = low


def sizes():
    return lax.axis_size("lon"), lax.axis_size("lat")


def send(values, lon_step, lat_step):
    nlon, nlat = sizes()
    route = [
        (i * nlat + j, ((i + lon_step) % nlon) * nlat + (j + lat_step) % nlat)
        for i in range(nlon)
        for j in range(nlat)
    ]
    return lax.ppermute(values, AXES, route)


def exchange(lat, lon, diag, step):
    return send(lat, 0, step), send(lon, step, 0), send(diag, step, step)


def halos(lattice, cut_row, cut_lane):
    return (
        lattice[:cut_row, :, cut_lane:],
        lattice[cut_row:, :, :cut_lane],
        lattice[:cut_row, :, :cut_lane],
    )


def joined(main, lat, lon, diag):
    top = jnp.concatenate([diag, lat], axis=2)
    rest = jnp.concatenate([lon, main], axis=2)
    return jnp.concatenate([top, rest], axis=0).transpose(1, 0, 2)


def place_stages():
    nlon, nlat = sizes()
    near_lon = 2 if nlon % 4 == 0 else 1
    near_lat = 2 if nlat % 2 == 0 else 1
    far_lon = nlon // 2 // near_lon
    far_lat = nlat // near_lat

    def near(i, j, d):
        c, x, z = i % 2, i // 2 % near_lon, i // 2 // near_lon
        y, w = j % near_lat, j // near_lat
        place = (x * near_lat + y) ^ d
        return (z * near_lon + place // near_lat) * 2 + c, w * near_lat + place % near_lat

    def wide(i, j, d):
        z = i // 2 // near_lon
        return ((z + d) % far_lon) * 2 * near_lon + i % (2 * near_lon), j

    def high(i, j, d):
        return i, ((j // near_lat + d) % far_lat) * near_lat + j % near_lat

    lon_at, lat_at = lax.axis_index("lon"), lax.axis_index("lat")
    near_at = (lon_at // 2 % near_lon) * near_lat + lat_at % near_lat
    stages = [
        (near_lon * near_lat, near, near_at, lambda at, d: at ^ d, lambda at, d: at ^ d),
        (far_lon, wide, lon_at // 2 // near_lon, lambda at, d: (at + d) % far_lon, lambda at, d: (at - d) % far_lon),
        (far_lat, high, lat_at // near_lat, lambda at, d: (at + d) % far_lat, lambda at, d: (at - d) % far_lat),
    ]
    return [s for s in stages if s[0] > 1]


def hop(values, step, d):
    nlon, nlat = sizes()
    route = []
    for i in range(nlon):
        for j in range(nlat):
            to_lon, to_lat = step(i, j, d)
            route.append((i * nlat + j, to_lon * nlat + to_lat))
    return lax.ppermute(values, AXES, route)


def pair(values):
    nlon, nlat = sizes()
    route = [(i * nlat + j, (i ^ 1) * nlat + j) for i in range(nlon) for j in range(nlat)]
    return lax.ppermute(values, AXES, route)


def reduce_stages(keep, sent):
    value = (keep.astype(f32) + pair(sent).astype(f32)).astype(bf16)
    taken = []
    for size, step, at, target, source in place_stages():
        rows = value.shape[0]
        split = rows % size == 0
        taken.append((size, step, at, source, split))
        if split:
            chunks = value.reshape(size, rows // size, value.shape[1])
            total = lax.dynamic_index_in_dim(chunks, at, 0, False).astype(f32)
            got = [
                hop(lax.dynamic_index_in_dim(chunks, target(at, d), 0, False), step, d)
                for d in range(1, size)
            ]
        else:
            total = value.astype(f32)
            got = [hop(value, step, d) for d in range(1, size)]
        for part in got:
            total = total + part.astype(f32)
        value = total.astype(bf16)
    return value, taken


def gather_stages(value, taken):
    pieces = value[None]
    places = [jnp.int32(0)]
    span = 1
    for size, step, at, source, split in reversed(taken):
        if not split:
            continue
        got = [pieces] + [hop(pieces, step, d) for d in range(1, size)]
        pieces = jnp.concatenate(got, axis=0)
        places = [source(at, d).astype(jnp.int32) * span + p for d in range(size) for p in places]
        span *= size
    return pieces, pair(pieces), jnp.stack(places)


def finish_kernel(core, place_two, place_one, own_two, far_two, own_one, far_one,
                  g_qkv_one, g_proj_one, g_merge, g_qkv_two, g_proj_two, two_ref, one_ref):
    mine = core[0]
    count = own_two.shape[0]
    for n in range(count):
        at = place_two[n]
        two_ref[mine * count + at] = own_two[n].astype(f32)
        two_ref[(1 - mine) * count + at] = far_two[n].astype(f32)
    count = own_one.shape[0]
    for n in range(count):
        at = place_one[n]
        one_ref[mine * count + at] = own_one[n].astype(f32)
        one_ref[(1 - mine) * count + at] = far_one[n].astype(f32)

    def scale_of(parts, entries):
        total = parts[0]
        for p in parts[1:]:
            total = total + p
        return lax.rsqrt(jnp.sum(total, axis=0, keepdims=True).sum(axis=1, keepdims=True) * (1.0 / entries) + grad_epsilon)

    def spans(ref, first, last):
        rows = ref.shape[1]
        while first < last:
            n, inside = first // rows, first % rows
            size = min(rows - inside, last - first)
            yield n, inside, size, first
            first += size

    def squares(ref, first, last, lanes):
        return [
            jnp.sum(jnp.square(ref[n, i : i + s, lanes]), axis=0, keepdims=True)
            for n, i, s, _ in spans(ref, first, last)
        ]

    channels = g_proj_two.shape[0]
    wide = g_merge.shape[0]
    every = slice(0, channels)
    jobs = (
        (g_merge, [(0, wide, 0)]),
        (g_proj_two, [(wide, wide + channels, 0)]),
        (g_qkv_two, [(wide + (n + 1) * channels, wide + (n + 2) * channels, n * channels) for n in range(3)]),
    )
    for out, blocks in jobs:
        parts = [q for first, last, _ in blocks for q in squares(two_ref, first, last, every)]
        scale = scale_of(parts, out.shape[0] * out.shape[1])
        for first, last, lane in blocks:
            for n, i, s, row in spans(two_ref, first, last):
                r = row - first
                out[r : r + s, lane : lane + channels] = (two_ref[n, i : i + s, :] * scale).astype(bf16)
    thin = g_proj_one.shape[0]
    first_half = squares(one_ref, 0, thin, slice(0, 2 * thin))
    second = squares(one_ref, thin, 2 * thin, slice(0, 2 * thin))
    lanes = lax.broadcasted_iota(jnp.int32, (1, 2 * thin), 1)
    qkv_parts = first_half + [jnp.where(lanes < thin, p, 0.0) for p in second]
    proj_parts = [jnp.where(lanes < thin, 0.0, p) for p in second]
    scale_qkv = scale_of(qkv_parts, 3 * thin * thin)
    scale_proj = scale_of(proj_parts, thin * thin)
    for n, i, s, row in spans(one_ref, 0, thin):
        g_qkv_one[row : row + s, 0 : 2 * thin] = (one_ref[n, i : i + s, :] * scale_qkv).astype(bf16)
    for n, i, s, row in spans(one_ref, thin, 2 * thin):
        r = row - thin
        g_qkv_one[r : r + s, 2 * thin : 3 * thin] = (one_ref[n, i : i + s, 0:thin] * scale_qkv).astype(bf16)
        g_proj_one[r : r + s, :] = (one_ref[n, i : i + s, thin : 2 * thin] * scale_proj).astype(bf16)


def shards(
    tokens, cotangent, kinds_one, kinds_two, table_one, table_two, gain_one, gain_merge, gain_two,
    qkv_one, proj_one, merge_weight, qkv_two, proj_two,
):
    c1, c2 = proj_one.shape[0], proj_two.shape[0]
    rows1, cols1 = tokens.shape[1], tokens.shape[2] // c1
    rows2, cols2 = rows1 // 2, cols1 // 2
    bands = rows1 // WIN_LAT
    nlon, nlat = sizes()
    smem = pl.BlockSpec(memory_space=pltpu.SMEM)
    vmem = pl.BlockSpec(memory_space=pltpu.VMEM)
    core = (lax.axis_index("lon") % 2).astype(jnp.int32)[None]
    at_end = (lax.axis_index("lat") == nlat - 1).astype(jnp.int32)
    last = jnp.stack([jnp.int32(0)] * (bands - 1) + [at_end, at_end])

    lace1 = lane_rows(rows1, cols1, LEVELS * rows1)
    lace2_pad = rounded_up(LEVELS * rows2, 8)
    lace2 = lane_rows(rows2, cols2, lace2_pad)
    win1, win2 = window_rows(rows1, cols1), window_rows(rows2, cols2)
    group = merge_rows(rows1, cols1)
    ahead = parts_rows(rows1, cols1, True)
    behind = parts_rows(rows1, cols1, False)
    ahead_got = moved(ahead, -HALF_LAT, -HALF_LON, rows1, cols1)
    behind_got = moved(behind, HALF_LAT, HALF_LON, rows1, cols1)
    orders = [
        index_of(win1, lace1),
        index_of(flat(ahead), win1),
        index_of(group, ahead_got),
        index_of(lace2, win2),
        index_of(win2, lace2),
        index_of(flat(behind), group),
        index_of(win1, behind_got),
        index_of(lace1, win1),
    ]
    index = np.full((max(len(o) for o in orders), 128), -1, np.int32)
    for n, order in enumerate(orders):
        index[: len(order), n] = order
    index = jnp.asarray(index)
    sizes_parts = [len(p) for p in ahead]

    lattice = tokens.transpose(1, 0, 2)
    cot = cotangent.transpose(1, 0, 2)
    lane1, lane2 = HALF_LON * c1, HALF_LON * c2
    tok_halos = exchange(*halos(lattice, HALF_LAT, lane1), -1)
    bias_one, bias_two = expand_bias(
        kinds_one[0], kinds_two[0], last, table_one.swapaxes(0, 1), table_two.swapaxes(0, 1)
    )
    cot_halos = exchange(*halos(cot, HALF_LAT, lane2), -1)

    def part_shapes(dtype=bf16):
        return [jax.ShapeDtypeStruct((n, c1), dtype) for n in sizes_parts]

    def lace_shapes(rows, cols, channels):
        kr, kl, cl = rows - HALF_LAT, (cols - HALF_LON) * channels, HALF_LON * channels
        return [
            jax.ShapeDtypeStruct((r, LEVELS, n), bf16)
            for r, n in ((kr, kl), (HALF_LAT, kl), (kr, cl), (HALF_LAT, cl))
        ]

    count1 = LEVELS * rows1 * cols1
    units1 = count1 // SPOTS
    fwd = pl.pallas_call(
        functools.partial(forward_one_kernel, cols=cols1, columns=(0, 1)),
        name="forward_one",
        in_specs=[vmem] * 9,
        out_specs=[vmem] * 8,
        out_shape=part_shapes()
        + [
            jax.ShapeDtypeStruct((count1, c1), bf16),
            jax.ShapeDtypeStruct((count1, 3 * c1), bf16),
            jax.ShapeDtypeStruct((units1, HEADS1 * SPOTS, 128), bf16),
            jax.ShapeDtypeStruct((count1, c1), bf16),
        ],
        scratch_shapes=[
            pltpu.VMEM((LEVELS * rows1, cols1 * c1), f32),
            pltpu.VMEM((count1, 3 * c1), f32),
            pltpu.VMEM((count1, c1), f32),
        ],
    )(lattice, *tok_halos, bias_one, gain_one[None], qkv_one, proj_one, index)
    parts, kept = fwd[:4], fwd[4:]
    got = exchange(*parts[1:], -1)

    tokens2 = LEVELS * SPOTS
    total_two = 4 * c1 + 4 * c2
    two = pl.pallas_call(
        functools.partial(merge_two_kernel, cols=cols2, columns=(2, 3, 4, 5)),
        name="merge_two",
        in_specs=[smem] + [vmem] * 15,
        out_specs=[vmem] * 10,
        out_shape=lace_shapes(rows2, cols2, c2)
        + part_shapes()
        + [jax.ShapeDtypeStruct((total_two // 2, c2), bf16)] * 2,
        scratch_shapes=[
            pltpu.VMEM((lace2_pad, cols2 * c2), f32),
            pltpu.VMEM((LEVELS, HEADS2 * SPOTS, 128), f32),
            pltpu.VMEM((tokens2, 3 * c2), f32),
            pltpu.VMEM((tokens2, c2), f32),
            pltpu.VMEM((tokens2, 3 * c2), f32),
            pltpu.VMEM((total_two, c2), f32),
        ],
    )(core, parts[0], *got, cot, *cot_halos, bias_two, gain_merge[None], gain_two[None],
      merge_weight, qkv_two, proj_two, index)
    res, d_parts, sums_two = two[:4], two[4:8], two[8:]
    d_got = exchange(*d_parts[1:], 1)
    value_two, taken_two = reduce_stages(*sums_two)

    one = pl.pallas_call(
        functools.partial(backward_one_kernel, cols=cols1, columns=(6, 7)),
        name="backward_one",
        in_specs=[smem] + [vmem] * 12,
        out_specs=[vmem] * 6,
        out_shape=lace_shapes(rows1, cols1, c1) + [jax.ShapeDtypeStruct((c1, 2 * c1), bf16)] * 2,
        scratch_shapes=[
            pltpu.VMEM((LEVELS * rows1, cols1 * c1), f32),
            pltpu.VMEM((count1, 3 * c1), f32),
            pltpu.VMEM((count1, c1), f32),
            pltpu.VMEM((count1, 3 * c1), f32),
            pltpu.VMEM((c1, 4 * c1), f32),
        ],
    )(core, d_parts[0], *d_got, *kept, gain_one[None], qkv_one, proj_one, index)
    d_tok, sums_one = one[:4], one[4:]
    value_one, taken_one = reduce_stages(*sums_one)
    result = joined(res[0], *exchange(*res[1:], 1))
    d_tokens = joined(d_tok[0], *exchange(*d_tok[1:], 1))

    own_two, far_two, place_two = gather_stages(value_two, taken_two)
    own_one, far_one, place_one = gather_stages(value_one, taken_one)
    grads = pl.pallas_call(
        finish_kernel,
        name="finish",
        in_specs=[smem] * 3 + [vmem] * 4,
        out_specs=[vmem] * 5,
        out_shape=[
            jax.ShapeDtypeStruct(w.shape, bf16) for w in (qkv_one, proj_one, merge_weight, qkv_two, proj_two)
        ],
        scratch_shapes=[
            pltpu.VMEM((2 * own_two.shape[0],) + own_two.shape[1:], f32),
            pltpu.VMEM((2 * own_one.shape[0],) + own_one.shape[1:], f32),
        ],
    )(core, place_two, place_one, own_two, far_two, own_one, far_one)
    return (result, d_tokens, *grads)


def solution(mesh):
    tiled = P(None, "lat", "lon")
    in_specs = (tiled, tiled, P(None, "lat"), P(None, "lat")) + (P(),) * 10
    out_specs = (tiled, tiled, P(), P(), P(), P(), P())
    return jax.shard_map(shards, mesh=mesh, in_specs=in_specs, out_specs=out_specs, check_vma=False)
```

time: 523 us -> 143 us (0.27); the launches traced: 514 us -> 143 us
  local copies, waits for them, and re-layouts: 246 us -> 8.85 us
  waiting for transfers between devices: 143 us -> 49.6 us
  other arithmetic: 46.4 us -> 3.64 us
  matrix products: 40.4 us -> 0 us
  Pallas kernels: 0 us -> 34.2 us
  starting transfers between devices: 17.7 us -> 44.9 us
  between operations: 19.7 us -> 1.76 us
    gather x6 -> x0, local copies, waits for them, and re-layouts: 144 us -> none  [the longest x4 138 us: attend(): full_bias = jnp.take(chosen, relative_table(), axis=3)]
    psum x1 -> x0, waiting for transfers between devices: 119 us -> none  [shards(): lax.psum((raw_qkv_one, raw_proj_one, raw_merge, raw_qkv_two, raw_proj_two...]
    dot_general x27 -> x0, matrix products: 40.4 us -> none  [the longest x6 9.36 us: attend(): jnp.einsum('abdhqk,abdkhe->abdqhe', attn_weights, value_rows, preferred_e...]
    pallas_call x0 -> x5, Pallas kernels: none -> 34.2 us  [the longest x1 10.4 us: shards(): pl.pallas_call(functools.partial(backward_one_kernel, cols=cols1, columns...]
    ppermute x12 -> x46, starting transfers between devices: 17.7 us -> 44.9 us  [the longest x24 26 us: hop(): return lax.ppermute(values, AXES, route)]
    ppermute x12 -> x46, waiting for transfers between devices: 24.3 us -> 49.6 us  [the longest x24 35.9 us: hop(): return lax.ppermute(values, AXES, route)]
    convert_element_type x14 -> x0, local copies, waits for them, and re-layouts: 23.6 us -> none  [the longest x3 5.84 us: merge_tokens(): grouped.astype(jnp.float32)]
    reduce_sum x19 -> x0, other arithmetic: 21.9 us -> none  [the longest x5 6.27 us: normalized(): scale_back = lax.rsqrt(jnp.mean(gradient * gradient) + grad_epsilon)]
  transfers between devices with their start and end apart: 13 -> 46, of which waited for: 6 -> 22; matrix products, arithmetic and copies ran while one was open for 42% -> 5% of each run, Pallas kernels for 0% -> 7%
where the time goes in v1:
time: 143 us
  waiting for transfers between devices  49.6 us (35%)
  starting transfers between devices  44.9 us (31%)
  Pallas kernels  34.2 us (24%)
  local copies, waits for them, and re-layouts  8.85 us (6%)
  other arithmetic  3.64 us (3%)
  between operations  1.76 us (1%)
    ppermute x24, waiting for transfers between devices, hop(): return lax.ppermute(values, AXES, route)  35.9 us
    ppermute x24, starting transfers between devices, hop(): return lax.ppermute(values, AXES, route)  26 us
    ppermute x18, starting transfers between devices, send(): return lax.ppermute(values, AXES, route)  18.7 us
    ppermute x18, waiting for transfers between devices, send(): return lax.ppermute(values, AXES, route)  11.7 us
    pallas_call x1, Pallas kernels, shards(): pl.pallas_call(functools.partial(backward_one_kernel, cols=cols1, columns...  10.4 us
    pallas_call x1, Pallas kernels, shards(): pl.pallas_call(functools.partial(merge_two_kernel, cols=cols2, columns=(2...  10.2 us
    pallas_call x1, Pallas kernels, shards(): pl.pallas_call(functools.partial(forward_one_kernel, cols=cols1, columns=...  5.77 us
    pallas_call x1, Pallas kernels, expand_bias(): pl.pallas_call(bias_kernel, name='bias', in_specs=[smem, smem, smem, vmem...  4 us
  transfers between devices with their start and end apart: 46, of which 22 were waited for; matrix products, arithmetic and copies ran while one was open for 5% of the time, Pallas kernels for 7%

profile of v1, /device:TPU:0, one launch (start us, length us, event | category | flops | bytes accessed | tf_op | source)
XLA Modules:
  0.0 142.8 jit_solution(5478580369565682572)
XLA Ops:
  1.4 3.1 %collective-permute-start = (bf16[3,2,3456]{2,1,0:T(2,128)(2,1)S(1)}, bf16[3,2,3456]{2,1,0:T(2,128)(2,1)S(1)}, u32[]{:S(2)}, u32[]{:S(2)}) collective-permute-start(bf16[3,2,3456]{2,1,0:T(2,128)(2,1)S(1)} %slice.24), channel_id=1, source_target_pairs={{0,1},{1,0},{2,3},{3,2},{4,5},{5,4},{6,7},{7,6},{8,9},{9,8},{10,11... | collective-permute-start | bytes 124424 | tf_op jit(solution)/shard_map/ppermute | solution.py:489
  5.3 3.7 %collective-permute-start.1 = (bf16[9,2,1152]{2,1,0:T(2,128)(2,1)S(1)}, bf16[9,2,1152]{2,1,0:T(2,128)(2,1)S(1)}, u32[]{:S(2)}, u32[]{:S(2)}) collective-permute-start(bf16[9,2,1152]{2,1,0:T(2,128)(2,1)S(1)} %slice.25), channel_id=1, source_target_pairs={{0,30},{1,31},{2,0},{3,1},{4,2},{5,3},{6,4},{7,5},{8,6},{9,7},{10,... | collective-permute-start | bytes 124424 | tf_op jit(solution)/shard_map/ppermute | solution.py:489
  11.6 1.6 %collective-permute-start.6 = (bf16[3,2,2304]{2,1,0:T(2,128)(2,1)S(1)}, bf16[3,2,2304]{2,1,0:T(2,128)(2,1)S(1)}, u32[]{:S(2)}, u32[]{:S(2)}) collective-permute-start(bf16[3,2,2304]{2,1,0:T(2,128)(2,1)S(1)} %get-tuple-element.84), channel_id=1, source_target_pairs={{0,1},{1,0},{2,3},{3,2},{4,5},{5,4},{6,7},{7,6},{8,9},{9,8},{10,11... | collective-permute-start | bytes 82952 | tf_op jit(solution)/shard_map/ppermute | solution.py:489
  14.4 4.0 %bias.1 = (f32[4,432,128]{2,1,0:T(8,128)}, f32[2,864,128]{2,1,0:T(8,128)}) custom-call(s32[2]{0:T(128)} %bitcast.93, s32[1]{0:T(128)} %bitcast.76.kinds_two, s32[3]{0:T(128)} %add_convert_fusion.2.last, f32[6,8,3312]{2,1,0:T(8,128)} %bitcast.82, f32[12,8,3312]{2,1,0:T(8,128)} %bitcast.79, s32[8,1536]{1,0:T(8,128)} %constant.162.clone.target), custom_call_target="tpu_custom_call" | custom-call | tf_op jit(solution)/shard_map/bias/pallas_call | solution.py:217
  19.1 5.8 %forward_one.1 = (bf16[336,192]{1,0:T(8,128)(2,1)}, bf16[112,192]{1,0:T(8,128)(2,1)}, bf16[112,192]{1,0:T(8,128)(2,1)}, bf16[48,192]{1,0:T(8,128)(2,1)}, bf16[57...) custom-call(bf16[12,2,4608]{2,1,0:T(2,128)(2,1)} %bitcast.88, ...), custom_call_target="tpu_custom_call" | custom-call | tf_op jit(solution)/shard_map/forward_one/pallas_call | solution.py:719
  27.1 1.4 %collective-permute-start.5 = (bf16[48,192]{1,0:T(8,128)(2,1)}, bf16[48,192]{1,0:T(8,128)(2,1)S(1)}, u32[]{:S(2)}, u32[]{:S(2)}) collective-permute-start(bf16[48,192]{1,0:T(8,128)(2,1)} %get-tuple-element.42), channel_id=1, source_target_pairs={{0,31},{1,30},{2,1},{3,0},{4,3},{5,2},{6,5},{7,4},{8,7},{9,6},{10,... | collective-permute-start | bytes 55304 | tf_op jit(solution)/shard_map/ppermute | solution.py:489
  31.5 10.2 %merge_two.1 = (bf16[3,2,2304]{2,1,0:T(2,128)(2,1)}, bf16[3,2,2304]{2,1,0:T(2,128)(2,1)}, bf16[3,2,2304]{2,1,0:T(2,128)(2,1)}, bf16[3,2,2304]{2,1,0:T(2,128)(2,1...) custom-call(s32[1]{0:T(128)} %bitcast.core, ...), custom_call_target="tpu_custom_call" | custom-call | tf_op jit(solution)/shard_map/merge_two/pallas_call | solution.py:742
  43.2 1.7 %collective-permute-start.14 = (bf16[48,192]{1,0:T(8,128)(2,1)}, bf16[48,192]{1,0:T(8,128)(2,1)S(1)}, u32[]{:S(2)}, u32[]{:S(2)}) collective-permute-start(bf16[48,192]{1,0:T(8,128)(2,1)} %get-tuple-element.51), channel_id=1, source_target_pairs={{0,3},{1,2},{2,5},{3,4},{4,7},{5,6},{6,9},{7,8},{8,11},{9,10},{10,... | collective-permute-start | bytes 55304 | tf_op jit(solution)/shard_map/ppermute | solution.py:489
  44.9 5.4 %collective-permute-done.14.diag = bf16[48,192]{1,0:T(8,128)(2,1)S(1)} collective-permute-done((bf16[48,192]{1,0:T(8,128)(2,1)}, bf16[48,192]{1,0:T(8,128)(2,1)S(1)}, u32[]{:S(2)}, u32[]{:S(2)}) %collective-permute-start.14) | collective-permute-done | bytes 18464 | tf_op jit(solution)/shard_map/ppermute | solution.py:489
  50.9 10.4 %backward_one.1 = (bf16[9,2,3456]{2,1,0:T(2,128)(2,1)}, bf16[3,2,3456]{2,1,0:T(2,128)(2,1)}, bf16[9,2,1152]{2,1,0:T(2,128)(2,1)}, bf16[3,2,1152]{2,1,0:T(2,128)(...) custom-call(s32[1]{0:T(128)} %bitcast.core, bf16[336,192]{1,0:T(8,128)(2,1)} %get-tuple-element.48.main, ...), custom_call_target="tpu_custom_call" | custom-call | tf_op jit(solution)/shard_map/backward_one/pallas_call | solution.py:764
  61.5 1.5 %collective-permute-done.32 = bf16[192,384]{1,0:T(8,128)(2,1)S(1)} collective-permute-done((bf16[192,384]{1,0:T(8,128)(2,1)}, bf16[192,384]{1,0:T(8,128)(2,1)S(1)}, u32[]{:S(2)}, u32[]{:S(2)}) %collective-permute-start.32) | collective-permute-done | bytes 147488 | tf_op jit(solution)/shard_map/ppermute | solution.py:553
  63.9 1.6 %collective-permute-start.33 = (bf16[48,384]{1,0:T(8,128)(2,1)S(1)}, bf16[48,384]{1,0:T(8,128)(2,1)S(1)}, u32[]{:S(2)}, u32[]{:S(2)}) collective-permute-start(bf16[48,384]{1,0:T(8,128)(2,1)S(1)} %get-tuple-element.79), channel_id=1, source_target_pairs={{0,1},{1,0},{2,3},{3,2},{4,5},{5,4},{6,7},{7,6},{8,9},{9,8},{10,11... | collective-permute-start | bytes 110600 | tf_op jit(solution)/shard_map/ppermute | solution.py:547
  65.5 2.0 %collective-permute-start.35 = (bf16[48,384]{1,0:T(8,128)(2,1)S(1)}, bf16[48,384]{1,0:T(8,128)(2,1)S(1)}, u32[]{:S(2)}, u32[]{:S(2)}) collective-permute-start(bf16[48,384]{1,0:T(8,128)(2,1)S(1)} %get-tuple-element.80), channel_id=1, source_target_pairs={{0,5},{1,4},{2,7},{3,6},{4,1},{5,0},{6,3},{7,2},{8,13},{9,12},{10,... | collective-permute-start | bytes 110600 | tf_op jit(solution)/shard_map/ppermute | solution.py:547
  68.1 1.6 %collective-permute-start.10 = (bf16[3,2,2304]{2,1,0:T(2,128)(2,1)S(1)}, bf16[3,2,2304]{2,1,0:T(2,128)(2,1)S(1)}, u32[]{:S(2)}, u32[]{:S(2)}) collective-permute-start(bf16[3,2,2304]{2,1,0:T(2,128)(2,1)S(1)} %copy-done.26), channel_id=1, source_target_pairs={{0,1},{1,0},{2,3},{3,2},{4,5},{5,4},{6,7},{7,6},{8,9},{9,8},{10,11... | collective-permute-start | bytes 82952 | tf_op jit(solution)/shard_map/ppermute | solution.py:489
  70.5 1.5 %collective-permute-done.10 = bf16[3,2,2304]{2,1,0:T(2,128)(2,1)S(1)} collective-permute-done((bf16[3,2,2304]{2,1,0:T(2,128)(2,1)S(1)}, bf16[3,2,2304]{2,1,0:T(2,128)(2,1)S(1)}, u32[]{:S(2)}, u32[]{:S(2)}) %collective-permute-start.10) | collective-permute-done | bytes 27680 | tf_op jit(solution)/shard_map/ppermute | solution.py:489
  73.1 2.6 %collective-permute-done.11 = bf16[3,2,2304]{2,1,0:T(2,128)(2,1)S(1)} collective-permute-done((bf16[3,2,2304]{2,1,0:T(2,128)(2,1)S(1)}, bf16[3,2,2304]{2,1,0:T(2,128)(2,1)S(1)}, u32[]{:S(2)}, u32[]{:S(2)}) %collective-permute-start.11) | collective-permute-done | bytes 27680 | tf_op jit(solution)/shard_map/ppermute | solution.py:489
  77.5 1.9 %collective-permute-done.38 = bf16[12,384]{1,0:T(8,128)(2,1)S(1)} collective-permute-done((bf16[12,384]{1,0:T(8,128)(2,1)S(1)}, bf16[12,384]{1,0:T(8,128)(2,1)S(1)}, u32[]{:S(2)}, u32[]{:S(2)}) %collective-permute-start.38) | collective-permute-done | bytes 9248 | tf_op jit(solution)/shard_map/ppermute | solution.py:547
  79.5 2.4 %collective-permute-start.40 = (bf16[1,12,384]{2,1,0:T(8,128)(2,1)S(1)}, bf16[1,12,384]{2,1,0:T(8,128)(2,1)S(1)}, u32[]{:S(2)}, u32[]{:S(2)}) collective-permute-start(bf16[1,12,384]{2,1,0:T(8,128)(2,1)S(1)} %get-tuple-element.70), channel_id=1, source_target_pairs={{0,16},{1,17},{2,18},{3,19},{4,20},{5,21},{6,22},{7,23},{8,24},{9,... | collective-permute-start | bytes 27656 | tf_op jit(solution)/shard_map/ppermute | solution.py:547
  81.8 1.5 %collective-permute-start.41 = (bf16[1,12,384]{2,1,0:T(8,128)(2,1)S(1)}, bf16[1,12,384]{2,1,0:T(8,128)(2,1)S(1)}, u32[]{:S(2)}, u32[]{:S(2)}) collective-permute-start(bf16[1,12,384]{2,1,0:T(8,128)(2,1)S(1)} %get-tuple-element.70), channel_id=1, source_target_pairs={{0,24},{1,25},{2,26},{3,27},{4,28},{5,29},{6,30},{7,31},{8,0},{9,1... | collective-permute-start | bytes 27656 | tf_op jit(solution)/shard_map/ppermute | solution.py:547
  85.5 1.7 %collective-permute-start.21 = (bf16[288,384]{1,0:T(8,128)(2,1)S(1)}, bf16[288,384]{1,0:T(8,128)(2,1)S(1)}, u32[]{:S(2)}, u32[]{:S(2)}) collective-permute-start(bf16[288,384]{1,0:T(8,128)(2,1)S(1)} %get-tuple-element.74), channel_id=1, source_target_pairs={{0,5},{1,4},{2,7},{3,6},{4,1},{5,0},{6,3},{7,2},{8,13},{9,12},{10,... | collective-permute-start | bytes 663560 | tf_op jit(solution)/shard_map/ppermute | solution.py:547
  87.9 3.3 %collective-permute-done.19 = bf16[288,384]{1,0:T(8,128)(2,1)S(1)} collective-permute-done((bf16[288,384]{1,0:T(8,128)(2,1)S(1)}, bf16[288,384]{1,0:T(8,128)(2,1)S(1)}, u32[]{:S(2)}, u32[]{:S(2)}) %collective-permute-start.19) | collective-permute-done | bytes 221216 | tf_op jit(solution)/shard_map/ppermute | solution.py:547
  91.2 2.5 %collective-permute-done.21 = bf16[288,384]{1,0:T(8,128)(2,1)S(1)} collective-permute-done((bf16[288,384]{1,0:T(8,128)(2,1)S(1)}, bf16[288,384]{1,0:T(8,128)(2,1)S(1)}, u32[]{:S(2)}, u32[]{:S(2)}) %collective-permute-start.21) | collective-permute-done | bytes 221216 | tf_op jit(solution)/shard_map/ppermute | solution.py:547
  96.3 2.8 %collective-permute-start.24 = (bf16[72,384]{1,0:T(8,128)(2,1)S(1)}, bf16[72,384]{1,0:T(8,128)(2,1)S(1)}, u32[]{:S(2)}, u32[]{:S(2)}) collective-permute-start(bf16[72,384]{1,0:T(8,128)(2,1)S(1)} %get-tuple-element.77), channel_id=1, source_target_pairs={{0,24},{1,25},{2,26},{3,27},{4,28},{5,29},{6,30},{7,31},{8,0},{9,1... | collective-permute-start | bytes 165896 | tf_op jit(solution)/shard_map/ppermute | solution.py:547
  100.0 2.8 %collective-permute-done.23 = bf16[72,384]{1,0:T(8,128)(2,1)S(1)} collective-permute-done((bf16[72,384]{1,0:T(8,128)(2,1)S(1)}, bf16[72,384]{1,0:T(8,128)(2,1)S(1)}, u32[]{:S(2)}, u32[]{:S(2)}) %collective-permute-start.23) | collective-permute-done | bytes 55328 | tf_op jit(solution)/shard_map/ppermute | solution.py:547
  102.8 1.7 %collective-permute-start.25 = (bf16[1,72,384]{2,1,0:T(8,128)(2,1)S(1)}, bf16[1,72,384]{2,1,0:T(8,128)(2,1)S(1)}, u32[]{:S(2)}, u32[]{:S(2)}) collective-permute-start(bf16[1,72,384]{2,1,0:T(8,128)(2,1)S(1)} %get-tuple-element.72), channel_id=1, source_target_pairs={{0,8},{1,9},{2,10},{3,11},{4,12},{5,13},{6,14},{7,15},{8,16},{9,17... | collective-permute-start | bytes 165896 | tf_op jit(solution)/shard_map/ppermute | solution.py:547
  107.0 1.9 %collective-permute-done.25 = bf16[1,72,384]{2,1,0:T(8,128)(2,1)S(1)} collective-permute-done((bf16[1,72,384]{2,1,0:T(8,128)(2,1)S(1)}, bf16[1,72,384]{2,1,0:T(8,128)(2,1)S(1)}, u32[]{:S(2)}, u32[]{:S(2)}) %collective-permute-start.25) | collective-permute-done | bytes 55328 | tf_op jit(solution)/shard_map/ppermute | solution.py:547
  111.6 1.9 %collective-permute-start.29 = (bf16[4,72,384]{2,1,0:T(8,128)(2,1)S(1)}, bf16[4,72,384]{2,1,0:T(8,128)(2,1)S(1)}, u32[]{:S(2)}, u32[]{:S(2)}) collective-permute-start(bf16[4,72,384]{2,1,0:T(8,128)(2,1)S(1)} %pad_maximum_fusion), channel_id=1, source_target_pairs={{0,4},{1,5},{2,6},{3,7},{4,0},{5,1},{6,2},{7,3},{8,12},{9,13},{10,... | collective-permute-start | bytes 663560 | tf_op jit(solution)/shard_map/ppermute | solution.py:547
  113.6 5.2 %collective-permute-done.28 = bf16[4,72,384]{2,1,0:T(8,128)(2,1)S(1)} collective-permute-done((bf16[4,72,384]{2,1,0:T(8,128)(2,1)S(1)}, bf16[4,72,384]{2,1,0:T(8,128)(2,1)S(1)}, u32[]{:S(2)}, u32[]{:S(2)}) %collective-permute-start.28) | collective-permute-done | bytes 221216 | tf_op jit(solution)/shard_map/ppermute | solution.py:547
  120.6 6.3 %collective-permute-done.30 = bf16[4,72,384]{2,1,0:T(8,128)(2,1)S(1)} collective-permute-done((bf16[4,72,384]{2,1,0:T(8,128)(2,1)S(1)}, bf16[4,72,384]{2,1,0:T(8,128)(2,1)S(1)}, u32[]{:S(2)}, u32[]{:S(2)}) %collective-permute-start.30) | collective-permute-done | bytes 221216 | tf_op jit(solution)/shard_map/ppermute | solution.py:547
  127.3 3.6 %collective-permute-done.43 = bf16[4,12,384]{2,1,0:T(8,128)(2,1)S(1)} collective-permute-done((bf16[4,12,384]{2,1,0:T(8,128)(2,1)S(1)}, bf16[4,12,384]{2,1,0:T(8,128)(2,1)S(1)}, u32[]{:S(2)}, u32[]{:S(2)}) %collective-permute-start.43) | collective-permute-done | bytes 36896 | tf_op jit(solution)/shard_map/ppermute | solution.py:547
  131.2 4.7 %collective-permute-done.44 = bf16[4,12,384]{2,1,0:T(8,128)(2,1)S(1)} collective-permute-done((bf16[4,12,384]{2,1,0:T(8,128)(2,1)S(1)}, bf16[4,12,384]{2,1,0:T(8,128)(2,1)S(1)}, u32[]{:S(2)}, u32[]{:S(2)}) %collective-permute-start.44) | collective-permute-done | bytes 36896 | tf_op jit(solution)/shard_map/ppermute | solution.py:547
  139.1 3.7 %finish.1 = (bf16[192,576]{1,0:T(8,128)(2,1)}, bf16[192,192]{1,0:T(8,128)(2,1)}, bf16[768,384]{1,0:T(8,128)(2,1)}, bf16[384,1152]{1,0:T(8,128)(2,1)}, bf16[384,384]{1,0:T(8,128)(2,1)}) custom-call(s32[1]{0:T(128)} %bitcast.core, s32[16]{0:T(128)} %stack.97.place_two.place_one, s32[16]{0:T(128)} %stack.97.place_two.place_one, bf16[16,72,384]{2,1,0:T(8,128)(2,1)} %copy-done, ...), custom_call_target="tpu_custom_call" | custom-call | tf_op jit(solution)/shard_map/finish/pallas_call | solution.py:785
  (156 shorter events, 35.2 us)
Async XLA Ops:
  1.4 17.0 %collective-permute-start = (bf16[3,2,3456]{2,1,0:T(2,128)(2,1)S(1)}, bf16[3,2,3456]{2,1,0:T(2,128)(2,1)S(1)}, u32[]{:S(2)}, u32[]{:S(2)}) collective-permute-start(bf16[3,2,3456]{2,1,0:T(2,128)(2,1)S(1)} %slice.24), channel_id=1, source_target_pairs={{0,1},{1,0},{2,3},{3,2},{4,5},{5,4},{6,7},{7,6},{8,9},{9,8},{10,11... | collective-permute-start | bytes 124424 | tf_op jit(solution)/shard_map/ppermute | solution.py:489
  5.3 13.1 %collective-permute-start.1 = (bf16[9,2,1152]{2,1,0:T(2,128)(2,1)S(1)}, bf16[9,2,1152]{2,1,0:T(2,128)(2,1)S(1)}, u32[]{:S(2)}, u32[]{:S(2)}) collective-permute-start(bf16[9,2,1152]{2,1,0:T(2,128)(2,1)S(1)} %slice.25), channel_id=1, source_target_pairs={{0,30},{1,31},{2,0},{3,1},{4,2},{5,3},{6,4},{7,5},{8,6},{9,7},{10,... | collective-permute-start | bytes 124424 | tf_op jit(solution)/shard_map/ppermute | solution.py:489
  9.8 8.6 %collective-permute-start.2 = (bf16[3,2,1152]{2,1,0:T(2,128)(2,1)S(1)}, bf16[3,2,1152]{2,1,0:T(2,128)(2,1)S(1)}, u32[]{:S(2)}, u32[]{:S(2)}) collective-permute-start(bf16[3,2,1152]{2,1,0:T(2,128)(2,1)S(1)} %slice.26), channel_id=1, source_target_pairs={{0,31},{1,30},{2,1},{3,0},{4,3},{5,2},{6,5},{7,4},{8,7},{9,6},{10,... | collective-permute-start | bytes 41480 | tf_op jit(solution)/shard_map/ppermute | solution.py:489
  11.6 15.5 %collective-permute-start.6 = (bf16[3,2,2304]{2,1,0:T(2,128)(2,1)S(1)}, bf16[3,2,2304]{2,1,0:T(2,128)(2,1)S(1)}, u32[]{:S(2)}, u32[]{:S(2)}) collective-permute-start(bf16[3,2,2304]{2,1,0:T(2,128)(2,1)S(1)} %get-tuple-element.84), channel_id=1, source_target_pairs={{0,1},{1,0},{2,3},{3,2},{4,5},{5,4},{6,7},{7,6},{8,9},{9,8},{10,11... | collective-permute-start | bytes 82952 | tf_op jit(solution)/shard_map/ppermute | solution.py:489
  24.8 6.0 %collective-permute-start.3 = (bf16[112,192]{1,0:T(8,128)(2,1)}, bf16[112,192]{1,0:T(8,128)(2,1)S(1)}, u32[]{:S(2)}, u32[]{:S(2)}) collective-permute-start(bf16[112,192]{1,0:T(8,128)(2,1)} %get-tuple-element.40), channel_id=1, source_target_pairs={{0,1},{1,0},{2,3},{3,2},{4,5},{5,4},{6,7},{7,6},{8,9},{9,8},{10,11... | collective-permute-start | bytes 129032 | tf_op jit(solution)/shard_map/ppermute | solution.py:489
  41.7 8.5 %collective-permute-start.12 = (bf16[112,192]{1,0:T(8,128)(2,1)}, bf16[112,192]{1,0:T(8,128)(2,1)S(1)}, u32[]{:S(2)}, u32[]{:S(2)}) collective-permute-start(bf16[112,192]{1,0:T(8,128)(2,1)} %get-tuple-element.49), channel_id=1, source_target_pairs={{0,1},{1,0},{2,3},{3,2},{4,5},{5,4},{6,7},{7,6},{8,9},{9,8},{10,11... | collective-permute-start | bytes 129032 | tf_op jit(solution)/shard_map/ppermute | solution.py:489
  42.8 7.5 %collective-permute-start.13 = (bf16[112,192]{1,0:T(8,128)(2,1)}, bf16[112,192]{1,0:T(8,128)(2,1)S(1)}, u32[]{:S(2)}, u32[]{:S(2)}) collective-permute-start(bf16[112,192]{1,0:T(8,128)(2,1)} %get-tuple-element.50), channel_id=1, source_target_pairs={{0,2},{1,3},{2,4},{3,5},{4,6},{5,7},{6,8},{7,9},{8,10},{9,11},{10,... | collective-permute-start | bytes 129032 | tf_op jit(solution)/shard_map/ppermute | solution.py:489
  43.2 7.1 %collective-permute-start.14 = (bf16[48,192]{1,0:T(8,128)(2,1)}, bf16[48,192]{1,0:T(8,128)(2,1)S(1)}, u32[]{:S(2)}, u32[]{:S(2)}) collective-permute-start(bf16[48,192]{1,0:T(8,128)(2,1)} %get-tuple-element.51), channel_id=1, source_target_pairs={{0,3},{1,2},{2,5},{3,4},{4,7},{5,6},{6,9},{7,8},{8,11},{9,10},{10,... | collective-permute-start | bytes 55304 | tf_op jit(solution)/shard_map/ppermute | solution.py:489
  63.9 5.8 %collective-permute-start.33 = (bf16[48,384]{1,0:T(8,128)(2,1)S(1)}, bf16[48,384]{1,0:T(8,128)(2,1)S(1)}, u32[]{:S(2)}, u32[]{:S(2)}) collective-permute-start(bf16[48,384]{1,0:T(8,128)(2,1)S(1)} %get-tuple-element.79), channel_id=1, source_target_pairs={{0,1},{1,0},{2,3},{3,2},{4,5},{5,4},{6,7},{7,6},{8,9},{9,8},{10,11... | collective-permute-start | bytes 110600 | tf_op jit(solution)/shard_map/ppermute | solution.py:547
  68.1 15.2 %collective-permute-start.18 = (bf16[1152,384]{1,0:T(8,128)(2,1)S(1)}, bf16[1152,384]{1,0:T(8,128)(2,1)S(1)}, u32[]{:S(2)}, u32[]{:S(2)}) collective-permute-start(bf16[1152,384]{1,0:T(8,128)(2,1)S(1)} %copy-done.21), channel_id=1, source_target_pairs={{0,2},{1,3},{2,0},{3,1},{4,6},{5,7},{6,4},{7,5},{8,10},{9,11},{10,... | collective-permute-start | bytes 2654216 | tf_op jit(solution)/shard_map/ppermute | solution.py:553
  69.7 6.0 %collective-permute-start.11 = (bf16[3,2,2304]{2,1,0:T(2,128)(2,1)S(1)}, bf16[3,2,2304]{2,1,0:T(2,128)(2,1)S(1)}, u32[]{:S(2)}, u32[]{:S(2)}) collective-permute-start(bf16[3,2,2304]{2,1,0:T(2,128)(2,1)S(1)} %copy-done.25), channel_id=1, source_target_pairs={{0,2},{1,3},{2,4},{3,5},{4,6},{5,7},{6,8},{7,9},{8,10},{9,11},{10,... | collective-permute-start | bytes 82952 | tf_op jit(solution)/shard_map/ppermute | solution.py:489
  69.9 6.9 %collective-permute-start.9 = (bf16[3,2,2304]{2,1,0:T(2,128)(2,1)S(1)}, bf16[3,2,2304]{2,1,0:T(2,128)(2,1)S(1)}, u32[]{:S(2)}, u32[]{:S(2)}) collective-permute-start(bf16[3,2,2304]{2,1,0:T(2,128)(2,1)S(1)} %copy-done.24), channel_id=1, source_target_pairs={{0,3},{1,2},{2,5},{3,4},{4,7},{5,6},{6,9},{7,8},{8,11},{9,10},{10,... | collective-permute-start | bytes 82952 | tf_op jit(solution)/shard_map/ppermute | solution.py:489
  70.5 7.1 %collective-permute-start.36 = (bf16[12,384]{1,0:T(8,128)(2,1)S(1)}, bf16[12,384]{1,0:T(8,128)(2,1)S(1)}, u32[]{:S(2)}, u32[]{:S(2)}) collective-permute-start(bf16[12,384]{1,0:T(8,128)(2,1)S(1)} %get-tuple-element.85), channel_id=1, source_target_pairs={{0,8},{1,9},{2,10},{3,11},{4,12},{5,13},{6,14},{7,15},{8,16},{9,17... | collective-permute-start | bytes 27656 | tf_op jit(solution)/shard_map/ppermute | solution.py:547
  79.4 6.1 %collective-permute-start.39 = (bf16[1,12,384]{2,1,0:T(8,128)(2,1)S(1)}, bf16[1,12,384]{2,1,0:T(8,128)(2,1)S(1)}, u32[]{:S(2)}, u32[]{:S(2)}) collective-permute-start(bf16[1,12,384]{2,1,0:T(8,128)(2,1)S(1)} %get-tuple-element.70), channel_id=1, source_target_pairs={{0,8},{1,9},{2,10},{3,11},{4,12},{5,13},{6,14},{7,15},{8,16},{9,17... | collective-permute-start | bytes 27656 | tf_op jit(solution)/shard_map/ppermute | solution.py:547
  79.5 7.7 %collective-permute-start.40 = (bf16[1,12,384]{2,1,0:T(8,128)(2,1)S(1)}, bf16[1,12,384]{2,1,0:T(8,128)(2,1)S(1)}, u32[]{:S(2)}, u32[]{:S(2)}) collective-permute-start(bf16[1,12,384]{2,1,0:T(8,128)(2,1)S(1)} %get-tuple-element.70), channel_id=1, source_target_pairs={{0,16},{1,17},{2,18},{3,19},{4,20},{5,21},{6,22},{7,23},{8,24},{9,... | collective-permute-start | bytes 27656 | tf_op jit(solution)/shard_map/ppermute | solution.py:547
  81.8 6.0 %collective-permute-start.41 = (bf16[1,12,384]{2,1,0:T(8,128)(2,1)S(1)}, bf16[1,12,384]{2,1,0:T(8,128)(2,1)S(1)}, u32[]{:S(2)}, u32[]{:S(2)}) collective-permute-start(bf16[1,12,384]{2,1,0:T(8,128)(2,1)S(1)} %get-tuple-element.70), channel_id=1, source_target_pairs={{0,24},{1,25},{2,26},{3,27},{4,28},{5,29},{6,30},{7,31},{8,0},{9,1... | collective-permute-start | bytes 27656 | tf_op jit(solution)/shard_map/ppermute | solution.py:547
  83.7 7.5 %collective-permute-start.19 = (bf16[288,384]{1,0:T(8,128)(2,1)S(1)}, bf16[288,384]{1,0:T(8,128)(2,1)S(1)}, u32[]{:S(2)}, u32[]{:S(2)}) collective-permute-start(bf16[288,384]{1,0:T(8,128)(2,1)S(1)} %get-tuple-element.73), channel_id=1, source_target_pairs={{0,1},{1,0},{2,3},{3,2},{4,5},{5,4},{6,7},{7,6},{8,9},{9,8},{10,11... | collective-permute-start | bytes 663560 | tf_op jit(solution)/shard_map/ppermute | solution.py:547
  84.2 6.9 %collective-permute-start.20 = (bf16[288,384]{1,0:T(8,128)(2,1)S(1)}, bf16[288,384]{1,0:T(8,128)(2,1)S(1)}, u32[]{:S(2)}, u32[]{:S(2)}) collective-permute-start(bf16[288,384]{1,0:T(8,128)(2,1)S(1)} %get-tuple-element.75), channel_id=1, source_target_pairs={{0,4},{1,5},{2,6},{3,7},{4,0},{5,1},{6,2},{7,3},{8,12},{9,13},{10,... | collective-permute-start | bytes 663560 | tf_op jit(solution)/shard_map/ppermute | solution.py:547
  85.5 8.1 %collective-permute-start.21 = (bf16[288,384]{1,0:T(8,128)(2,1)S(1)}, bf16[288,384]{1,0:T(8,128)(2,1)S(1)}, u32[]{:S(2)}, u32[]{:S(2)}) collective-permute-start(bf16[288,384]{1,0:T(8,128)(2,1)S(1)} %get-tuple-element.74), channel_id=1, source_target_pairs={{0,5},{1,4},{2,7},{3,6},{4,1},{5,0},{6,3},{7,2},{8,13},{9,12},{10,... | collective-permute-start | bytes 663560 | tf_op jit(solution)/shard_map/ppermute | solution.py:547
  87.2 48.8 %collective-permute-start.16 = (bf16[3,2,3456]{2,1,0:T(2,128)(2,1)S(1)}, bf16[3,2,3456]{2,1,0:T(2,128)(2,1)S(1)}, u32[]{:S(2)}, u32[]{:S(2)}) collective-permute-start(bf16[3,2,3456]{2,1,0:T(2,128)(2,1)S(1)} %copy-done.23), channel_id=1, source_target_pairs={{0,1},{1,0},{2,3},{3,2},{4,5},{5,4},{6,7},{7,6},{8,9},{9,8},{10,11... | collective-permute-start | bytes 124424 | tf_op jit(solution)/shard_map/ppermute | solution.py:489
  87.8 48.2 %collective-permute-start.17 = (bf16[9,2,1152]{2,1,0:T(2,128)(2,1)S(1)}, bf16[9,2,1152]{2,1,0:T(2,128)(2,1)S(1)}, u32[]{:S(2)}, u32[]{:S(2)}) collective-permute-start(bf16[9,2,1152]{2,1,0:T(2,128)(2,1)S(1)} %copy-done.22), channel_id=1, source_target_pairs={{0,2},{1,3},{2,4},{3,5},{4,6},{5,7},{6,8},{7,9},{8,10},{9,11},{10,... | collective-permute-start | bytes 124424 | tf_op jit(solution)/shard_map/ppermute | solution.py:489
  93.8 6.3 %collective-permute-start.22 = (bf16[72,384]{1,0:T(8,128)(2,1)S(1)}, bf16[72,384]{1,0:T(8,128)(2,1)S(1)}, u32[]{:S(2)}, u32[]{:S(2)}) collective-permute-start(bf16[72,384]{1,0:T(8,128)(2,1)S(1)} %get-tuple-element.76), channel_id=1, source_target_pairs={{0,8},{1,9},{2,10},{3,11},{4,12},{5,13},{6,14},{7,15},{8,16},{9,17... | collective-permute-start | bytes 165896 | tf_op jit(solution)/shard_map/ppermute | solution.py:547
  94.9 7.9 %collective-permute-start.23 = (bf16[72,384]{1,0:T(8,128)(2,1)S(1)}, bf16[72,384]{1,0:T(8,128)(2,1)S(1)}, u32[]{:S(2)}, u32[]{:S(2)}) collective-permute-start(bf16[72,384]{1,0:T(8,128)(2,1)S(1)} %get-tuple-element.78), channel_id=1, source_target_pairs={{0,16},{1,17},{2,18},{3,19},{4,20},{5,21},{6,22},{7,23},{8,24},{9,... | collective-permute-start | bytes 165896 | tf_op jit(solution)/shard_map/ppermute | solution.py:547
  96.3 6.5 %collective-permute-start.24 = (bf16[72,384]{1,0:T(8,128)(2,1)S(1)}, bf16[72,384]{1,0:T(8,128)(2,1)S(1)}, u32[]{:S(2)}, u32[]{:S(2)}) collective-permute-start(bf16[72,384]{1,0:T(8,128)(2,1)S(1)} %get-tuple-element.77), channel_id=1, source_target_pairs={{0,24},{1,25},{2,26},{3,27},{4,28},{5,29},{6,30},{7,31},{8,0},{9,1... | collective-permute-start | bytes 165896 | tf_op jit(solution)/shard_map/ppermute | solution.py:547
  102.8 6.0 %collective-permute-start.25 = (bf16[1,72,384]{2,1,0:T(8,128)(2,1)S(1)}, bf16[1,72,384]{2,1,0:T(8,128)(2,1)S(1)}, u32[]{:S(2)}, u32[]{:S(2)}) collective-permute-start(bf16[1,72,384]{2,1,0:T(8,128)(2,1)S(1)} %get-tuple-element.72), channel_id=1, source_target_pairs={{0,8},{1,9},{2,10},{3,11},{4,12},{5,13},{6,14},{7,15},{8,16},{9,17... | collective-permute-start | bytes 165896 | tf_op jit(solution)/shard_map/ppermute | solution.py:547
  104.5 5.6 %collective-permute-start.26 = (bf16[1,72,384]{2,1,0:T(8,128)(2,1)S(1)}, bf16[1,72,384]{2,1,0:T(8,128)(2,1)S(1)}, u32[]{:S(2)}, u32[]{:S(2)}) collective-permute-start(bf16[1,72,384]{2,1,0:T(8,128)(2,1)S(1)} %get-tuple-element.72), channel_id=1, source_target_pairs={{0,16},{1,17},{2,18},{3,19},{4,20},{5,21},{6,22},{7,23},{8,24},{9,... | collective-permute-start | bytes 165896 | tf_op jit(solution)/shard_map/ppermute | solution.py:547
  108.9 27.2 %collective-permute-start.15 = (bf16[3,2,1152]{2,1,0:T(2,128)(2,1)S(1)}, bf16[3,2,1152]{2,1,0:T(2,128)(2,1)S(1)}, u32[]{:S(2)}, u32[]{:S(2)}) collective-permute-start(bf16[3,2,1152]{2,1,0:T(2,128)(2,1)S(1)} %copy-done.27), channel_id=1, source_target_pairs={{0,3},{1,2},{2,5},{3,4},{4,7},{5,6},{6,9},{7,8},{8,11},{9,10},{10,... | collective-permute-start | bytes 41480 | tf_op jit(solution)/shard_map/ppermute | solution.py:489
  110.6 8.1 %collective-permute-start.28 = (bf16[4,72,384]{2,1,0:T(8,128)(2,1)S(1)}, bf16[4,72,384]{2,1,0:T(8,128)(2,1)S(1)}, u32[]{:S(2)}, u32[]{:S(2)}) collective-permute-start(bf16[4,72,384]{2,1,0:T(8,128)(2,1)S(1)} %pad_maximum_fusion), channel_id=1, source_target_pairs={{0,1},{1,0},{2,3},{3,2},{4,5},{5,4},{6,7},{7,6},{8,9},{9,8},{10,11... | collective-permute-start | bytes 663560 | tf_op jit(solution)/shard_map/ppermute | solution.py:547
  111.6 7.8 %collective-permute-start.29 = (bf16[4,72,384]{2,1,0:T(8,128)(2,1)S(1)}, bf16[4,72,384]{2,1,0:T(8,128)(2,1)S(1)}, u32[]{:S(2)}, u32[]{:S(2)}) collective-permute-start(bf16[4,72,384]{2,1,0:T(8,128)(2,1)S(1)} %pad_maximum_fusion), channel_id=1, source_target_pairs={{0,4},{1,5},{2,6},{3,7},{4,0},{5,1},{6,2},{7,3},{8,12},{9,13},{10,... | collective-permute-start | bytes 663560 | tf_op jit(solution)/shard_map/ppermute | solution.py:547
  118.8 8.1 %collective-permute-start.30 = (bf16[4,72,384]{2,1,0:T(8,128)(2,1)S(1)}, bf16[4,72,384]{2,1,0:T(8,128)(2,1)S(1)}, u32[]{:S(2)}, u32[]{:S(2)}) collective-permute-start(bf16[4,72,384]{2,1,0:T(8,128)(2,1)S(1)} %pad_maximum_fusion), channel_id=1, source_target_pairs={{0,5},{1,4},{2,7},{3,6},{4,1},{5,0},{6,3},{7,2},{8,13},{9,12},{10,... | collective-permute-start | bytes 663560 | tf_op jit(solution)/shard_map/ppermute | solution.py:547
  119.4 7.9 %collective-permute-start.42 = (bf16[4,12,384]{2,1,0:T(8,128)(2,1)S(1)}, bf16[4,12,384]{2,1,0:T(8,128)(2,1)S(1)}, u32[]{:S(2)}, u32[]{:S(2)}) collective-permute-start(bf16[4,12,384]{2,1,0:T(8,128)(2,1)S(1)} %pad_maximum_fusion.1), channel_id=1, source_target_pairs={{0,1},{1,0},{2,3},{3,2},{4,5},{5,4},{6,7},{7,6},{8,9},{9,8},{10,11... | collective-permute-start | bytes 110600 | tf_op jit(solution)/shard_map/ppermute | solution.py:547
  127.3 10.2 %collective-permute-start.31 = (bf16[16,72,384]{2,1,0:T(8,128)(2,1)S(1)}, bf16[16,72,384]{2,1,0:T(8,128)(2,1)S(1)}, u32[]{:S(2)}, u32[]{:S(2)}) collective-permute-start(bf16[16,72,384]{2,1,0:T(8,128)(2,1)S(1)} %constant_dynamic-update-slice_fusion.own_two), channel_id=1, source_target_pairs={{0,2},{1,3},{2,0},{3,1},{4,6},{5,7},{6,4},{7,5},{8,10},{9,11},{10,... | collective-permute-start | bytes 2654216 | tf_op jit(solution)/shard_map/ppermute | solution.py:553
  (42 other events, 279.1 us)

commit v2 on v1

--- a/solution.py
+++ b/solution.py
@@ -7,6 +7,7 @@
 from jax.experimental import pallas as pl
 from jax.experimental.pallas import tpu as pltpu
 from jax.sharding import PartitionSpec as P
+
 
 HEADS1 = 6
 HEADS2 = 12
@@ -30,6 +31,10 @@
 
 def rounded_up(count, step):
     return -(-count // step) * step
+
+
+def core_of():
+    return lax.axis_index("lon") % 2
 
 
 def mm(a, b):
@@ -160,7 +165,15 @@
     return weights / jnp.sum(weights, axis=-1, keepdims=True)
 
 
-def bias_kernel(kinds_one, kinds_two, last, table_one, table_two, target, out_one, out_two, rows_ref, runs_ref):
+def halo_kernel(tokens, cot, lat, lon, diag, sems):
+    copies = halo_copies(tokens, cot, lat, lon, diag, sems)
+    for c in copies:
+        c.start()
+    for c in copies:
+        c.wait()
+
+
+def expand_bias(kinds_one, kinds_two, table_one, table_two, target, out_one, out_two, rows_ref, runs_ref):
     bands = out_one.shape[0] // LEVELS
     head_sets = [(8 * b, HEADS1) for b in range(bands)] + [(8 * bands, HEADS2)]
     width = WIN_LAT * SPAN
@@ -187,6 +200,7 @@
     pick = jnp.where(sub == target[0:1, :], 1.0, 0.0).astype(bf16)
     full = mm(high, pick) + mm(middle, pick) + mm(low, pick)
     lanes = lax.broadcasted_iota(jnp.int32, (1, 128), 1)
+    at_end = jnp.where(lax.axis_index("lat") == lax.axis_size("lat") - 1, 1.0, 0.0).astype(f32)
     for z in range(LEVELS):
         for ap in range(WIN_LAT):
             across = jnp.where(
@@ -194,7 +208,7 @@
             )
             at = (z * WIN_LAT + ap) * slots
             for s, (first, heads) in enumerate(head_sets):
-                own = across * last[s].astype(f32)
+                own = across * at_end if s >= bands - 1 else jnp.zeros_like(across)
                 for bp in range(WIN_LON):
                     piece = full[at + first : at + first + heads, 128 * bp : 128 * bp + 128] + own
                     spot = ap * WIN_LON + bp
@@ -204,7 +218,7 @@
                         out_two[z, pl.ds(spot, heads, stride=SPOTS), :] = piece
 
 
-def expand_bias(kinds_one, kinds_two, last, table_one, table_two):
+def bias_call(kinds_one, kinds_two, table_one, table_two):
     bands = kinds_one.shape[0]
     target = np.full((8, WIN_LON * 128), -1, np.int32)
     for bp in range(WIN_LON):
@@ -215,10 +229,10 @@
     smem = pl.BlockSpec(memory_space=pltpu.SMEM)
     vmem = pl.BlockSpec(memory_space=pltpu.VMEM)
     return pl.pallas_call(
-        bias_kernel,
+        expand_bias,
         name="bias",
-        in_specs=[smem, smem, smem, vmem, vmem, vmem],
-        out_specs=[vmem, vmem],
+        in_specs=[smem, smem, vmem, vmem, vmem],
+        out_specs=[vmem] * 2,
         out_shape=(
             jax.ShapeDtypeStruct((bands * LEVELS, HEADS1 * SPOTS, 128), f32),
             jax.ShapeDtypeStruct((LEVELS, HEADS2 * SPOTS, 128), f32),
@@ -227,20 +241,73 @@
             pltpu.VMEM((slots, table_one.shape[2]), f32),
             pltpu.VMEM((LEVELS * WIN_LAT * slots, 256), f32),
         ],
-    )(kinds_one, kinds_two, last, table_one, table_two, target)
-
-
-def unlace(main, lat, lon, diag, lace_ref, cut_row, cut_lane):
-    rows = main.shape[0]
-    lanes = main.shape[2]
-    kept = lanes - cut_lane
-    for j in range(rows - cut_row):
-        lace_ref[2 * j : 2 * j + 2, 0:kept] = main[j + cut_row, :, cut_lane:lanes].astype(f32)
+    )(kinds_one, kinds_two, table_one, table_two, target)
+
+
+def halo_call(tokens, cot, lane1):
+    rows, levels, lanes = tokens.shape
+    low = cot.shape[0] - HALF_LAT
+    return pl.pallas_call(
+        halo_kernel,
+        name="halo",
+        in_specs=[pl.BlockSpec(memory_space=pl.ANY)] * 2,
+        out_specs=[pl.BlockSpec(memory_space=pltpu.VMEM)] * 3,
+        out_shape=(
+            jax.ShapeDtypeStruct((HALF_LAT, levels, 2 * lanes - 3 * lane1), bf16),
+            jax.ShapeDtypeStruct((rows - HALF_LAT + 2 * low, levels, lane1), bf16),
+            jax.ShapeDtypeStruct((HALF_LAT, levels, 3 * lane1), bf16),
+        ),
+        scratch_shapes=[pltpu.SemaphoreType.DMA((7,))],
+    )(tokens, cot)
+
+
+def halo_copies(tokens, cot, lat, lon, diag, sems):
+    rows, lanes = tokens.shape[0], tokens.shape[2]
+    cut = HALF_LAT
+    lane1 = diag.shape[2] // 3
+    lane2 = 2 * lane1
+    kept1 = lanes - lane1
+    jobs = [
+        (tokens.at[0:cut, :, lane1:lanes], lat.at[:, :, 0:kept1]),
+        (cot.at[0:cut, :, lane2:lanes], lat.at[:, :, kept1 : kept1 + lanes - lane2]),
+        (tokens.at[cut:rows, :, 0:lane1], lon.at[0 : rows - cut]),
+        (tokens.at[0:cut, :, 0:lane1], diag.at[:, :, 0:lane1]),
+        (cot.at[0:cut, :, 0:lane2], diag.at[:, :, lane1 : lane1 + lane2]),
+    ]
+    low = cot.shape[0] - cut
+    for n in range(2):
+        at = rows - cut + n * low
+        jobs.append((cot.at[cut : cut + low, :, n * lane1 : (n + 1) * lane1], lon.at[at : at + low]))
+    return [pltpu.make_async_copy(a, b, sems.at[n]) for n, (a, b) in enumerate(jobs)]
+
+
+def unlace_one(main, lat, lon, diag, lace_ref, lane1):
+    rows, lanes = main.shape[0], main.shape[2]
+    kept = lanes - lane1
+    for j in range(rows - HALF_LAT):
+        lace_ref[2 * j : 2 * j + 2, 0:kept] = main[j + HALF_LAT, :, lane1:lanes].astype(f32)
         lace_ref[2 * j : 2 * j + 2, kept:lanes] = lon[j].astype(f32)
-    for n in range(cut_row):
-        j = rows - cut_row + n
-        lace_ref[2 * j : 2 * j + 2, 0:kept] = lat[n].astype(f32)
-        lace_ref[2 * j : 2 * j + 2, kept:lanes] = diag[n].astype(f32)
+    for n in range(HALF_LAT):
+        j = rows - HALF_LAT + n
+        lace_ref[2 * j : 2 * j + 2, 0:kept] = lat[n, :, 0:kept].astype(f32)
+        lace_ref[2 * j : 2 * j + 2, kept:lanes] = diag[n, :, 0:lane1].astype(f32)
+
+
+def unlace_two(main, lat, lon, diag, lace_ref, lane1):
+    rows, lanes = main.shape[0], main.shape[2]
+    lane2 = 2 * lane1
+    kept = lanes - lane2
+    low = rows - HALF_LAT
+    first = lon.shape[0] - 2 * low
+    for j in range(low):
+        lace_ref[2 * j : 2 * j + 2, 0:kept] = main[j + HALF_LAT, :, lane2:lanes].astype(f32)
+        for n in range(2):
+            at = kept + n * lane1
+            lace_ref[2 * j : 2 * j + 2, at : at + lane1] = lon[first + n * low + j].astype(f32)
+    for n in range(HALF_LAT):
+        j = low + n
+        lace_ref[2 * j : 2 * j + 2, 0:kept] = lat[n, :, lanes - lane1 : lanes - lane1 + kept].astype(f32)
+        lace_ref[2 * j : 2 * j + 2, kept:lanes] = diag[n, :, lane1 : lane1 + lane2].astype(f32)
 
 
 def lace_out(lace_ref, main, lat, lon, diag, cut_row, cut_lane):
@@ -262,16 +329,16 @@
     lace_ref, packed_ref, att_ref,
     *, cols, columns,
 ):
-    channels = gain.shape[1]
+    channels = gain.shape[0]
     lace_rows = lace_ref.shape[0]
     count = lace_rows * cols
-    unlace(main, lat, lon, diag, lace_ref, HALF_LAT, HALF_LON * channels)
+    unlace_one(main, lat, lon, diag, lace_ref, HALF_LON * channels)
     stacked = jnp.concatenate(
         [lace_ref[:, channels * k : channels * (k + 1)] for k in range(cols)], axis=0
     ).astype(bf16)
     values = mm(one_hot(index, columns[0], count, count), stacked)
     hat, _ = rms_stats(values)
-    normed = (hat * gain[0:1, :]).astype(bf16)
+    normed = (hat * gain[...][None, :]).astype(bf16)
     packed = mm(normed, w_qkv[...]).astype(bf16)
     packed_ref[...] = packed.astype(f32)
     keep_packed[...] = packed
@@ -306,15 +373,15 @@
 
 
 def merge_two_kernel(
-    core, main, lat, lon, diag, cot_main, cot_lat, cot_lon, cot_diag, bias,
+    main, lat, lon, diag, cot_main, cot_lat, cot_lon, cot_diag, bias,
     gain_merge, gain_two, w_merge, w_qkv, w_proj, index,
     res_main, res_lat, res_lon, res_diag, d_main, d_lat, d_lon, d_diag, sums_keep, sums_send,
     lace_ref, probs_ref, packed_ref, att_ref, d_packed_ref, sums_ref,
     *, cols, columns,
 ):
-    channels = gain_two.shape[1]
+    channels = gain_two.shape[0]
     thin = main.shape[1]
-    groups = gain_merge.shape[1] // thin
+    groups = gain_merge.shape[0] // thin
     tokens = LEVELS * SPOTS
     total = main.shape[0] + lat.shape[0] + lon.shape[0] + diag.shape[0]
     stacked = jnp.concatenate([main[...], lat[...], lon[...], diag[...]], axis=0)
@@ -326,14 +393,15 @@
     second = sum(jnp.sum(s * s, axis=-1, keepdims=True) for s in spreads) * (1.0 / wide)
     scale_merge = lax.rsqrt(second + norm_epsilon)
     hats = [s * scale_merge for s in spreads]
-    gains = [gain_merge[0:1, g * thin : (g + 1) * thin] for g in range(groups)]
+    wide_gain = gain_merge[...][None, :]
+    gains = [wide_gain[:, g * thin : (g + 1) * thin] for g in range(groups)]
     merged_norm = [(hats[g] * gains[g]).astype(bf16) for g in range(groups)]
     merged = mm(merged_norm[0], w_merge[0:thin, :])
     for g in range(1, groups):
         merged = merged + mm(merged_norm[g], w_merge[g * thin : (g + 1) * thin, :])
     merged = merged.astype(bf16).astype(f32)
     hat, scale_two = rms_stats(merged)
-    normed = (hat * gain_two[0:1, :]).astype(bf16)
+    normed = (hat * gain_two[...][None, :]).astype(bf16)
     packed_ref[...] = mm(normed, w_qkv[...]).astype(bf16).astype(f32)
     masks = lane_head_masks(128)
     per = len(masks)
@@ -357,7 +425,7 @@
         lace_ref[:, channels * k : channels * (k + 1)] = lattice[lace_rows * k : lace_rows * (k + 1)]
     lace_out(lace_ref, res_main, res_lat, res_lon, res_diag, HALF_LAT, HALF_LON * channels)
     lace_ref[...] = jnp.zeros(lace_ref.shape, f32)
-    unlace(cot_main, cot_lat, cot_lon, cot_diag, lace_ref, HALF_LAT, HALF_LON * channels)
+    unlace_two(cot_main, cot_lat, cot_lon, cot_diag, lace_ref, HALF_LON * thin)
     cot_stack = jnp.concatenate(
         [lace_ref[:, channels * k : channels * (k + 1)] for k in range(cols)], axis=0
     ).astype(bf16)
@@ -381,7 +449,7 @@
             normed, d_packed[:, n * channels : (n + 1) * channels]
         )
     d_normed = mm_nt(d_packed, w_qkv[...]).astype(bf16).astype(f32)
-    d_merged = d_block + norm_back(hat, scale_two, d_normed * gain_two[0:1, :], channels)
+    d_merged = d_block + norm_back(hat, scale_two, d_normed * gain_two[...][None, :], channels)
     d_merged = d_merged.astype(bf16)
     d_hats = []
     for g in range(groups):
@@ -399,7 +467,7 @@
         out[...] = parts[start : start + out.shape[0]]
         start += out.shape[0]
     half = sums_ref.shape[0] // 2
-    mine = core[0]
+    mine = core_of()
     first_row = pl.multiple_of(mine * half, 16)
     other_row = pl.multiple_of((1 - mine) * half, 16)
     sums_keep[...] = sums_ref[pl.ds(first_row, half), :].astype(bf16)
@@ -425,12 +493,13 @@
 
 
 def backward_one_kernel(
-    core, main, lat, lon, diag, keep_x, keep_packed, keep_probs, keep_att, gain, w_qkv, w_proj, index,
+    main, lat, lon, diag, keep_x, keep_packed, keep_probs, keep_att, res_lat, res_lon, res_diag,
+    gain, w_qkv, w_proj, index,
     out_main, out_lat, out_lon, out_diag, sums_keep, sums_send,
     lace_ref, packed_ref, att_ref, d_packed_ref, sums_ref,
     *, cols, columns,
 ):
-    channels = gain.shape[1]
+    channels = gain.shape[0]
     lace_rows = lace_ref.shape[0]
     count = lace_rows * cols
     total = main.shape[0] + lat.shape[0] + lon.shape[0] + diag.shape[0]
@@ -438,7 +507,7 @@
     d_block = mm(one_hot(index, columns[0], count, total), stacked)
     d_block_low = d_block.astype(bf16)
     hat, scale = rms_stats(keep_x[...].astype(f32))
-    normed = (hat * gain[0:1, :]).astype(bf16)
+    normed = (hat * gain[...][None, :]).astype(bf16)
     packed_ref[...] = keep_packed[...].astype(f32)
     att_ref[...] = mm_nt(d_block_low, w_proj[...]).astype(bf16).astype(f32)
     for u in range(count // SPOTS):
@@ -454,12 +523,24 @@
     sums_ref[:, 0 : 3 * channels] = mm_tn(normed, d_packed)
     sums_ref[:, 3 * channels : 4 * channels] = mm_tn(keep_att[...], d_block_low)
     d_normed = mm_nt(d_packed, w_qkv[...]).astype(bf16).astype(f32)
-    d_shift = d_block + norm_back(hat, scale, d_normed * gain[0:1, :], channels)
+    d_shift = d_block + norm_back(hat, scale, d_normed * gain[...][None, :], channels)
     lattice = mm(one_hot(index, columns[1], count, count), d_shift.astype(bf16))
     for k in range(cols):
         lace_ref[:, channels * k : channels * (k + 1)] = lattice[lace_rows * k : lace_rows * (k + 1)]
-    lace_out(lace_ref, out_main, out_lat, out_lon, out_diag, HALF_LAT, HALF_LON * channels)
-    mine = core[0]
+    kept = out_main.shape[2]
+    lane1 = HALF_LON * channels
+    low = out_main.shape[0]
+    lace_out(
+        lace_ref, out_main, out_lat.at[:, :, 0:kept], out_lon.at[0:low], out_diag.at[:, :, 0:lane1],
+        HALF_LAT, lane1,
+    )
+    out_lat[:, :, kept:] = res_lat[...]
+    out_diag[:, :, lane1:] = res_diag[...]
+    count = res_lon.shape[0]
+    for n in range(2):
+        at = low + n * count
+        out_lon[at : at + count] = res_lon[:, :, n * lane1 : (n + 1) * lane1]
+    mine = core_of()
     half = 2 * channels
     low = sums_ref[:, 0:half].astype(bf16)
     high = sums_ref[:, half : 2 * half].astype(bf16)
@@ -490,15 +571,7 @@
 
 
 def exchange(lat, lon, diag, step):
-    return send(lat, 0, step), send(lon, step, 0), send(diag, step, step)
-
-
-def halos(lattice, cut_row, cut_lane):
-    return (
-        lattice[:cut_row, :, cut_lane:],
-        lattice[cut_row:, :, :cut_lane],
-        lattice[:cut_row, :, :cut_lane],
-    )
+    return (send(lat, 0, step), send(lon, step, 0), send(diag, step, step))
 
 
 def joined(main, lat, lon, diag):
@@ -529,12 +602,12 @@
 
     lon_at, lat_at = lax.axis_index("lon"), lax.axis_index("lat")
     near_at = (lon_at // 2 % near_lon) * near_lat + lat_at % near_lat
-    stages = [
-        (near_lon * near_lat, near, near_at, lambda at, d: at ^ d, lambda at, d: at ^ d),
-        (far_lon, wide, lon_at // 2 // near_lon, lambda at, d: (at + d) % far_lon, lambda at, d: (at - d) % far_lon),
-        (far_lat, high, lat_at // near_lat, lambda at, d: (at + d) % far_lat, lambda at, d: (at - d) % far_lat),
-    ]
-    return [s for s in stages if s[0] > 1]
+    stages = [(near_lon * near_lat, near, near_at)]
+    if far_lon > 1:
+        stages.append((far_lon, wide, lon_at // 2 // near_lon))
+    if far_lat > 1:
+        stages.append((far_lat, high, lat_at // near_lat))
+    return stages
 
 
 def hop(values, step, d):
@@ -548,61 +621,63 @@
 
 
 def pair(values):
-    nlon, nlat = sizes()
-    route = [(i * nlat + j, (i ^ 1) * nlat + j) for i in range(nlon) for j in range(nlat)]
-    return lax.ppermute(values, AXES, route)
-
-
-def reduce_stages(keep, sent):
-    value = (keep.astype(f32) + pair(sent).astype(f32)).astype(bf16)
-    taken = []
-    for size, step, at, target, source in place_stages():
-        rows = value.shape[0]
-        split = rows % size == 0
-        taken.append((size, step, at, source, split))
-        if split:
-            chunks = value.reshape(size, rows // size, value.shape[1])
-            total = lax.dynamic_index_in_dim(chunks, at, 0, False).astype(f32)
-            got = [
-                hop(lax.dynamic_index_in_dim(chunks, target(at, d), 0, False), step, d)
-                for d in range(1, size)
-            ]
-        else:
-            total = value.astype(f32)
-            got = [hop(value, step, d) for d in range(1, size)]
+    return hop(values, lambda i, j, d: (i ^ 1, j), 1)
+
+
+def target(stage, at, d, size):
+    return at ^ d if stage == 0 else (at + d) % size
+
+
+def scatter(value, stages):
+    for n, (size, step, at) in enumerate(stages):
+        chunks = value.reshape(size, value.shape[0] // size, value.shape[1])
+        total = lax.dynamic_index_in_dim(chunks, at, 0, False).astype(f32)
+        got = [hop(lax.dynamic_index_in_dim(chunks, target(n, at, d, size), 0, False), step, d) for d in range(1, size)]
         for part in got:
             total = total + part.astype(f32)
         value = total.astype(bf16)
-    return value, taken
-
-
-def gather_stages(value, taken):
-    pieces = value[None]
+    return value
+
+
+def paired(keep, sent):
+    return (keep.astype(f32) + pair(sent).astype(f32)).astype(bf16)
+
+
+def gather(two, one, stages):
+    for n, (size, step, at) in reversed(list(enumerate(stages))):
+        message = jnp.concatenate([two, one], axis=0)
+        got = [message] + [hop(message, step, d) for d in range(1, size)]
+        if n == 0:
+            return jnp.concatenate(got, axis=0)
+        rows = two.shape[0]
+        two = jnp.concatenate([m[:rows] for m in got], axis=0)
+        one = sum(m[rows:].astype(f32) for m in got).astype(bf16)
+
+
+def finish_kernel(own, far, g_qkv_one, g_proj_one, g_merge, g_qkv_two, g_proj_two,
+                  two_ref, one_ref, *, stage_sizes):
+    mine = core_of()
+    spots = [at for _, _, at in place_stages()]
+    near = stage_sizes[0]
+    span = own.shape[0] // near
+    inner = two_ref.shape[0] // (2 * near)
+    size = two_ref.shape[1]
     places = [jnp.int32(0)]
-    span = 1
-    for size, step, at, source, split in reversed(taken):
-        if not split:
-            continue
-        got = [pieces] + [hop(pieces, step, d) for d in range(1, size)]
-        pieces = jnp.concatenate(got, axis=0)
-        places = [source(at, d).astype(jnp.int32) * span + p for d in range(size) for p in places]
-        span *= size
-    return pieces, pair(pieces), jnp.stack(places)
-
-
-def finish_kernel(core, place_two, place_one, own_two, far_two, own_one, far_one,
-                  g_qkv_one, g_proj_one, g_merge, g_qkv_two, g_proj_two, two_ref, one_ref):
-    mine = core[0]
-    count = own_two.shape[0]
-    for n in range(count):
-        at = place_two[n]
-        two_ref[mine * count + at] = own_two[n].astype(f32)
-        two_ref[(1 - mine) * count + at] = far_two[n].astype(f32)
-    count = own_one.shape[0]
-    for n in range(count):
-        at = place_one[n]
-        one_ref[mine * count + at] = own_one[n].astype(f32)
-        one_ref[(1 - mine) * count + at] = far_one[n].astype(f32)
+    width = 1
+    for n in range(len(stage_sizes) - 1, 0, -1):
+        count = stage_sizes[n]
+        places = [lax.rem(spots[n] - d + count, count) * width + p for d in range(count) for p in places]
+        width *= count
+    for d in range(near):
+        place = spots[0] ^ d
+        for p in range(inner):
+            rows = slice(d * span + p * size, d * span + (p + 1) * size)
+            at = place * inner + places[p]
+            two_ref[mine * near * inner + at] = own[rows, :].astype(f32)
+            two_ref[(1 - mine) * near * inner + at] = far[rows, :].astype(f32)
+        rows = slice(d * span + inner * size, (d + 1) * span)
+        one_ref[mine * near + place] = own[rows, :].astype(f32)
+        one_ref[(1 - mine) * near + place] = far[rows, :].astype(f32)
 
     def scale_of(parts, entries):
         total = parts[0]
@@ -662,13 +737,9 @@
     c1, c2 = proj_one.shape[0], proj_two.shape[0]
     rows1, cols1 = tokens.shape[1], tokens.shape[2] // c1
     rows2, cols2 = rows1 // 2, cols1 // 2
-    bands = rows1 // WIN_LAT
     nlon, nlat = sizes()
-    smem = pl.BlockSpec(memory_space=pltpu.SMEM)
     vmem = pl.BlockSpec(memory_space=pltpu.VMEM)
-    core = (lax.axis_index("lon") % 2).astype(jnp.int32)[None]
-    at_end = (lax.axis_index("lat") == nlat - 1).astype(jnp.int32)
-    last = jnp.stack([jnp.int32(0)] * (bands - 1) + [at_end, at_end])
+    stages = place_stages()
 
     lace1 = lane_rows(rows1, cols1, LEVELS * rows1)
     lace2_pad = rounded_up(LEVELS * rows2, 8)
@@ -697,12 +768,10 @@
 
     lattice = tokens.transpose(1, 0, 2)
     cot = cotangent.transpose(1, 0, 2)
-    lane1, lane2 = HALF_LON * c1, HALF_LON * c2
-    tok_halos = exchange(*halos(lattice, HALF_LAT, lane1), -1)
-    bias_one, bias_two = expand_bias(
-        kinds_one[0], kinds_two[0], last, table_one.swapaxes(0, 1), table_two.swapaxes(0, 1)
+    halos = exchange(*halo_call(lattice, cot, HALF_LON * c1), -1)
+    bias_one, bias_two = bias_call(
+        kinds_one[0], kinds_two[0], table_one.swapaxes(0, 1), table_two.swapaxes(0, 1)
     )
-    cot_halos = exchange(*halos(cot, HALF_LAT, lane2), -1)
 
     def part_shapes(dtype=bf16):
         return [jax.ShapeDtypeStruct((n, c1), dtype) for n in sizes_parts]
@@ -733,7 +802,7 @@
             pltpu.VMEM((count1, 3 * c1), f32),
             pltpu.VMEM((count1, c1), f32),
         ],
-    )(lattice, *tok_halos, bias_one, gain_one[None], qkv_one, proj_one, index)
+    )(lattice, *halos, bias_one, gain_one, qkv_one, proj_one, index)
     parts, kept = fwd[:4], fwd[4:]
     got = exchange(*parts[1:], -1)
 
@@ -742,7 +811,7 @@
     two = pl.pallas_call(
         functools.partial(merge_two_kernel, cols=cols2, columns=(2, 3, 4, 5)),
         name="merge_two",
-        in_specs=[smem] + [vmem] * 15,
+        in_specs=[vmem] * 15,
         out_specs=[vmem] * 10,
         out_shape=lace_shapes(rows2, cols2, c2)
         + part_shapes()
@@ -755,18 +824,24 @@
             pltpu.VMEM((tokens2, 3 * c2), f32),
             pltpu.VMEM((total_two, c2), f32),
         ],
-    )(core, parts[0], *got, cot, *cot_halos, bias_two, gain_merge[None], gain_two[None],
+    )(parts[0], *got, cot, *halos, bias_two, gain_merge, gain_two,
       merge_weight, qkv_two, proj_two, index)
     res, d_parts, sums_two = two[:4], two[4:8], two[8:]
+    half_two = paired(*sums_two)
     d_got = exchange(*d_parts[1:], 1)
-    value_two, taken_two = reduce_stages(*sums_two)
-
+    mine_two = scatter(half_two, stages)
+
+    lanes1, lane1 = tokens.shape[2], HALF_LON * c1
     one = pl.pallas_call(
         functools.partial(backward_one_kernel, cols=cols1, columns=(6, 7)),
         name="backward_one",
-        in_specs=[smem] + [vmem] * 12,
+        in_specs=[vmem] * 15,
         out_specs=[vmem] * 6,
-        out_shape=lace_shapes(rows1, cols1, c1) + [jax.ShapeDtypeStruct((c1, 2 * c1), bf16)] * 2,
+        out_shape=[
+            jax.ShapeDtypeStruct((rows1 - HALF_LAT, LEVELS, lanes1 - lane1), bf16),
+            *(jax.ShapeDtypeStruct(h.shape, bf16) for h in halos),
+        ]
+        + [jax.ShapeDtypeStruct((c1, 2 * c1), bf16)] * 2,
         scratch_shapes=[
             pltpu.VMEM((LEVELS * rows1, cols1 * c1), f32),
             pltpu.VMEM((count1, 3 * c1), f32),
@@ -774,27 +849,34 @@
             pltpu.VMEM((count1, 3 * c1), f32),
             pltpu.VMEM((c1, 4 * c1), f32),
         ],
-    )(core, d_parts[0], *d_got, *kept, gain_one[None], qkv_one, proj_one, index)
+    )(d_parts[0], *d_got, *kept, *res[1:], gain_one, qkv_one, proj_one, index)
     d_tok, sums_one = one[:4], one[4:]
-    value_one, taken_one = reduce_stages(*sums_one)
-    result = joined(res[0], *exchange(*res[1:], 1))
-    d_tokens = joined(d_tok[0], *exchange(*d_tok[1:], 1))
-
-    own_two, far_two, place_two = gather_stages(value_two, taken_two)
-    own_one, far_one, place_one = gather_stages(value_one, taken_one)
+    mine_one = scatter(paired(*sums_one), stages[:1])
+    own = gather(mine_two, mine_one, stages)
+    far = pair(own)
+    lat, lon, diag = exchange(*d_tok[1:], 1)
+    kept, low, cut2 = lanes1 - lane1, rows1 - HALF_LAT, rows2 - HALF_LAT
+    d_tokens = joined(d_tok[0], lat[:, :, :kept], lon[:low], diag[:, :, :lane1])
+    lon = jnp.concatenate([lon[low : low + cut2], lon[low + cut2 :]], axis=2)
+    result = joined(res[0], lat[:, :, kept:], lon, diag[:, :, lane1:])
+
+    near = stages[0][0]
+    inner = 1
+    for size, _, _ in stages[1:]:
+        inner *= size
     grads = pl.pallas_call(
-        finish_kernel,
+        functools.partial(finish_kernel, stage_sizes=tuple(size for size, _, _ in stages)),
         name="finish",
-        in_specs=[smem] * 3 + [vmem] * 4,
+        in_specs=[vmem] * 2,
         out_specs=[vmem] * 5,
         out_shape=[
             jax.ShapeDtypeStruct(w.shape, bf16) for w in (qkv_one, proj_one, merge_weight, qkv_two, proj_two)
         ],
         scratch_shapes=[
-            pltpu.VMEM((2 * own_two.shape[0],) + own_two.shape[1:], f32),
-            pltpu.VMEM((2 * own_one.shape[0],) + own_one.shape[1:], f32),
+            pltpu.VMEM((2 * near * inner,) + mine_two.shape, f32),
+            pltpu.VMEM((2 * near,) + mine_one.shape, f32),
         ],
-    )(core, place_two, place_one, own_two, far_two, own_one, far_one)
+    )(own, far)
     return (result, d_tokens, *grads)
 
 
@@ -802,4 +884,5 @@
     tiled = P(None, "lat", "lon")
     in_specs = (tiled, tiled, P(None, "lat"), P(None, "lat")) + (P(),) * 10
     out_specs = (tiled, tiled, P(), P(), P(), P(), P())
+
     return jax.shard_map(shards, mesh=mesh, in_specs=in_specs, out_specs=out_specs, check_vma=False)

time: 143 us -> 116 us (0.81); the launches traced: 143 us -> 114 us
  starting transfers between devices: 44.9 us -> 30.6 us
  waiting for transfers between devices: 49.6 us -> 38.9 us
  local copies, waits for them, and re-layouts: 8.85 us -> 3.75 us
  Pallas kernels: 34.2 us -> 36.5 us
    ppermute x24 -> x18, waiting for transfers between devices: 35.9 us -> 23.5 us  [hop(): return lax.ppermute(values, AXES, route)]
    ppermute x24 -> x18, starting transfers between devices: 26 us -> 16.1 us  [hop(): return lax.ppermute(values, AXES, route)]
    ppermute x18 -> x12, starting transfers between devices: 18.7 us -> 14.4 us  [send(): return lax.ppermute(values, AXES, route)]
    ppermute x18 -> x12, waiting for transfers between devices: 11.7 us -> 15.4 us  [send(): return lax.ppermute(values, AXES, route)]
    slice x4 -> x8, local copies, waits for them, and re-layouts: 3.18 us -> 0.12 us  [the longest x4 0.07 us: shards(): d_tokens = joined(d_tok[0], lat[:, :, :kept], lon[:low], diag[:, :, :lane1])]
    ppermute x4 -> x0, waiting for transfers between devices: 2.01 us -> none  [pair(): return lax.ppermute(values, AXES, route)]
    pallas_call x2 -> x3, Pallas kernels: 7.74 us -> 9.18 us  [the longest x1 4.01 us: bias_call(): pl.pallas_call(expand_bias, name='bias', in_specs=[smem, smem, vmem, vmem...]
    unnamed x66 -> x39, local copies, waits for them, and re-layouts: 3.65 us -> 3.45 us
  transfers between devices with their start and end apart: 46 -> 30, of which waited for: 22 -> 15; matrix products, arithmetic and copies ran while one was open for 5% -> 2% of each run, Pallas kernels for 7% -> 13%
where the time goes in v2:
time: 116 us; the launch traced here: 114 us
  waiting for transfers between devices  38.9 us (34%)
  Pallas kernels  36.5 us (31%)
  starting transfers between devices  30.6 us (26%)
  local copies, waits for them, and re-layouts  3.75 us (3%)
  other arithmetic  2.25 us (2%)
  between operations  1.71 us (1%)
    ppermute x18, waiting for transfers between devices, hop(): return lax.ppermute(values, AXES, route)  23.5 us
    ppermute x18, starting transfers between devices, hop(): return lax.ppermute(values, AXES, route)  16.1 us
    ppermute x12, waiting for transfers between devices, send(): return lax.ppermute(values, AXES, route)  15.4 us
    ppermute x12, starting transfers between devices, send(): return lax.ppermute(values, AXES, route)  14.4 us
    pallas_call x1, Pallas kernels, shards(): pl.pallas_call(functools.partial(merge_two_kernel, cols=cols2, columns=(2...  11 us
    pallas_call x1, Pallas kernels, shards(): pl.pallas_call(functools.partial(backward_one_kernel, cols=cols1, columns...  10.5 us
    pallas_call x1, Pallas kernels, shards(): pl.pallas_call(functools.partial(forward_one_kernel, cols=cols1, columns=...  5.84 us
    pallas_call x1, Pallas kernels, bias_call(): pl.pallas_call(expand_bias, name='bias', in_specs=[smem, smem, vmem, vmem...  4.01 us
  transfers between devices with their start and end apart: 30, of which 15 were waited for; matrix products, arithmetic and copies ran while one was open for 2% of the time, Pallas kernels for 13%

profile of v2, /device:TPU:0, one launch (start us, length us, event | category | flops | bytes accessed | tf_op | source)
XLA Modules:
  0.0 113.7 jit_solution(7284358188608701898)
XLA Ops:
  0.6 1.6 %halo.1 = (bf16[3,2,5760]{2,1,0:T(2,128)(2,1)}, bf16[15,2,1152]{2,1,0:T(2,128)(2,1)}, bf16[3,2,3456]{2,1,0:T(2,128)(2,1)}) custom-call(bf16[12,2,4608]{2,1,0:T(2,128)(2,1)} %bitcast.45, bf16[6,2,4608]{2,1,0:T(2,128)(2,1)} %bitcast.52), custom_call_target="tpu_custom_call" | custom-call | tf_op jit(solution)/shard_map/halo/pallas_call | solution.py:250
  2.2 3.1 %collective-permute-start = (bf16[3,2,5760]{2,1,0:T(2,128)(2,1)}, bf16[3,2,5760]{2,1,0:T(2,128)(2,1)S(1)}, u32[]{:S(2)}, u32[]{:S(2)}) collective-permute-start(bf16[3,2,5760]{2,1,0:T(2,128)(2,1)} %get-tuple-element.41), channel_id=1, source_target_pairs={{0,1},{1,0},{2,3},{3,2},{4,5},{5,4},{6,7},{7,6},{8,9},{9,8},{10,11... | collective-permute-start | bytes 207368 | tf_op jit(solution)/shard_map/ppermute | solution.py:570
  5.3 3.7 %collective-permute-start.1 = (bf16[15,2,1152]{2,1,0:T(2,128)(2,1)}, bf16[15,2,1152]{2,1,0:T(2,128)(2,1)S(1)}, u32[]{:S(2)}, u32[]{:S(2)}) collective-permute-start(bf16[15,2,1152]{2,1,0:T(2,128)(2,1)} %get-tuple-element.42), channel_id=1, source_target_pairs={{0,30},{1,31},{2,0},{3,1},{4,2},{5,3},{6,4},{7,5},{8,6},{9,7},{10,... | collective-permute-start | bytes 207368 | tf_op jit(solution)/shard_map/ppermute | solution.py:570
  10.5 4.0 %bias.1 = (f32[4,432,128]{2,1,0:T(8,128)}, f32[2,864,128]{2,1,0:T(8,128)}) custom-call(s32[2]{0:T(128)} %bitcast.54, s32[1]{0:T(128)} %bitcast.41.kinds_two, f32[6,8,3312]{2,1,0:T(8,128)} %bitcast.49, f32[12,8,3312]{2,1,0:T(8,128)} %bitcast.44, s32[8,1536]{1,0:T(8,128)} %constant.100.clone.target), custom_call_target="tpu_custom_call" | custom-call | tf_op jit(solution)/shard_map/bias/pallas_call | solution.py:231
  15.2 5.8 %forward_one.1 = (bf16[336,192]{1,0:T(8,128)(2,1)}, bf16[112,192]{1,0:T(8,128)(2,1)}, bf16[112,192]{1,0:T(8,128)(2,1)}, bf16[48,192]{1,0:T(8,128)(2,1)}, bf16[57...) custom-call(bf16[12,2,4608]{2,1,0:T(2,128)(2,1)} %bitcast.46, ...), custom_call_target="tpu_custom_call" | custom-call | tf_op jit(solution)/shard_map/forward_one/pallas_call | solution.py:788
  21.0 1.5 %collective-permute-start.3 = (bf16[112,192]{1,0:T(8,128)(2,1)}, bf16[112,192]{1,0:T(8,128)(2,1)S(1)}, u32[]{:S(2)}, u32[]{:S(2)}) collective-permute-start(bf16[112,192]{1,0:T(8,128)(2,1)} %get-tuple-element.46), channel_id=1, source_target_pairs={{0,1},{1,0},{2,3},{3,2},{4,5},{5,4},{6,7},{7,6},{8,9},{9,8},{10,11... | collective-permute-start | bytes 129032 | tf_op jit(solution)/shard_map/ppermute | solution.py:570
  22.5 1.3 %collective-permute-start.4 = (bf16[112,192]{1,0:T(8,128)(2,1)}, bf16[112,192]{1,0:T(8,128)(2,1)S(1)}, u32[]{:S(2)}, u32[]{:S(2)}) collective-permute-start(bf16[112,192]{1,0:T(8,128)(2,1)} %get-tuple-element.47), channel_id=1, source_target_pairs={{0,30},{1,31},{2,0},{3,1},{4,2},{5,3},{6,4},{7,5},{8,6},{9,7},{10,... | collective-permute-start | bytes 129032 | tf_op jit(solution)/shard_map/ppermute | solution.py:570
  24.8 2.5 %collective-permute-done.5.diag = bf16[48,192]{1,0:T(8,128)(2,1)S(1)} collective-permute-done((bf16[48,192]{1,0:T(8,128)(2,1)}, bf16[48,192]{1,0:T(8,128)(2,1)S(1)}, u32[]{:S(2)}, u32[]{:S(2)}) %collective-permute-start.5) | collective-permute-done | bytes 18464 | tf_op jit(solution)/shard_map/ppermute | solution.py:570
  28.0 11.0 %merge_two.1 = (bf16[3,2,2304]{2,1,0:T(2,128)(2,1)}, bf16[3,2,2304]{2,1,0:T(2,128)(2,1)}, bf16[3,2,2304]{2,1,0:T(2,128)(2,1)}, bf16[3,2,2304]{2,1,0:T(2,128)(2,1...) custom-call(bf16[336,192]{1,0:T(8,128)(2,1)} %get-tuple-element.45.m, ...), custom_call_target="tpu_custom_call" | custom-call | tf_op jit(solution)/shard_map/merge_two/pallas_call | solution.py:811
  39.1 1.5 %collective-permute-start.6 = (bf16[112,192]{1,0:T(8,128)(2,1)}, bf16[112,192]{1,0:T(8,128)(2,1)S(1)}, u32[]{:S(2)}, u32[]{:S(2)}) collective-permute-start(bf16[112,192]{1,0:T(8,128)(2,1)} %get-tuple-element.51), channel_id=1, source_target_pairs={{0,1},{1,0},{2,3},{3,2},{4,5},{5,4},{6,7},{7,6},{8,9},{9,8},{10,11... | collective-permute-start | bytes 129032 | tf_op jit(solution)/shard_map/ppermute | solution.py:570
  40.9 6.9 %collective-permute-done.8.diag = bf16[48,192]{1,0:T(8,128)(2,1)S(1)} collective-permute-done((bf16[48,192]{1,0:T(8,128)(2,1)}, bf16[48,192]{1,0:T(8,128)(2,1)S(1)}, u32[]{:S(2)}, u32[]{:S(2)}) %collective-permute-start.8) | collective-permute-done | bytes 18464 | tf_op jit(solution)/shard_map/ppermute | solution.py:570
  48.5 10.5 %backward_one.1 = (bf16[9,2,3456]{2,1,0:T(2,128)(2,1)}, bf16[3,2,5760]{2,1,0:T(2,128)(2,1)}, bf16[15,2,1152]{2,1,0:T(2,128)(2,1)}, bf16[3,2,3456]{2,1,0:T(2,128)...) custom-call(bf16[336,192]{1,0:T(8,128)(2,1)} %get-tuple-element.50.main, bf16[112,192]{1,0:T(8,128)(2,1)} %copy-done.11, ...), custom_call_target="tpu_custom_call" | custom-call | tf_op jit(solution)/shard_map/backward_one/pallas_call | solution.py:835
  59.2 1.1 collective-permute-start.10
  60.3 5.9 %collective-permute-done.9 = bf16[3,2,3456]{2,1,0:T(2,128)(2,1)S(1)} collective-permute-done((bf16[3,2,3456]{2,1,0:T(2,128)(2,1)}, bf16[3,2,3456]{2,1,0:T(2,128)(2,1)S(1)}, u32[]{:S(2)}, u32[]{:S(2)}) %collective-permute-start.9) | collective-permute-done | bytes 41504 | tf_op jit(solution)/shard_map/ppermute | solution.py:570
  67.0 2.5 %collective-permute-start.14 = (bf16[288,384]{1,0:T(8,128)(2,1)S(1)}, bf16[288,384]{1,0:T(8,128)(2,1)S(1)}, u32[]{:S(2)}, u32[]{:S(2)}) collective-permute-start(bf16[288,384]{1,0:T(8,128)(2,1)S(1)} %get-tuple-element.81), channel_id=1, source_target_pairs={{0,4},{1,5},{2,6},{3,7},{4,0},{5,1},{6,2},{7,3},{8,12},{9,13},{10,... | collective-permute-start | bytes 663560 | tf_op jit(solution)/shard_map/ppermute | solution.py:620
  70.5 4.0 %collective-permute-done.15 = bf16[288,384]{1,0:T(8,128)(2,1)S(1)} collective-permute-done((bf16[288,384]{1,0:T(8,128)(2,1)S(1)}, bf16[288,384]{1,0:T(8,128)(2,1)S(1)}, u32[]{:S(2)}, u32[]{:S(2)}) %collective-permute-start.15) | collective-permute-done | bytes 221216 | tf_op jit(solution)/shard_map/ppermute | solution.py:620
  74.6 2.2 %collective-permute-done.14 = bf16[288,384]{1,0:T(8,128)(2,1)S(1)} collective-permute-done((bf16[288,384]{1,0:T(8,128)(2,1)S(1)}, bf16[288,384]{1,0:T(8,128)(2,1)S(1)}, u32[]{:S(2)}, u32[]{:S(2)}) %collective-permute-start.14) | collective-permute-done | bytes 221216 | tf_op jit(solution)/shard_map/ppermute | solution.py:620
  77.3 1.0 collective-permute-start.20
  78.4 1.0 collective-permute-done.22
  79.4 1.9 %collective-permute-start.18 = (bf16[72,384]{1,0:T(8,128)(2,1)S(1)}, bf16[72,384]{1,0:T(8,128)(2,1)S(1)}, u32[]{:S(2)}, u32[]{:S(2)}) collective-permute-start(bf16[72,384]{1,0:T(8,128)(2,1)S(1)} %get-tuple-element.83), channel_id=1, source_target_pairs={{0,24},{1,25},{2,26},{3,27},{4,28},{5,29},{6,30},{7,31},{8,0},{9,1... | collective-permute-start | bytes 165896 | tf_op jit(solution)/shard_map/ppermute | solution.py:620
  81.3 1.3 %collective-permute-start.16 = (bf16[72,384]{1,0:T(8,128)(2,1)S(1)}, bf16[72,384]{1,0:T(8,128)(2,1)S(1)}, u32[]{:S(2)}, u32[]{:S(2)}) collective-permute-start(bf16[72,384]{1,0:T(8,128)(2,1)S(1)} %get-tuple-element.82), channel_id=1, source_target_pairs={{0,8},{1,9},{2,10},{3,11},{4,12},{5,13},{6,14},{7,15},{8,16},{9,17... | collective-permute-start | bytes 165896 | tf_op jit(solution)/shard_map/ppermute | solution.py:620
  82.6 2.2 %collective-permute-done.18 = bf16[72,384]{1,0:T(8,128)(2,1)S(1)} collective-permute-done((bf16[72,384]{1,0:T(8,128)(2,1)S(1)}, bf16[72,384]{1,0:T(8,128)(2,1)S(1)}, u32[]{:S(2)}, u32[]{:S(2)}) %collective-permute-start.18) | collective-permute-done | bytes 55328 | tf_op jit(solution)/shard_map/ppermute | solution.py:620
  84.8 1.8 %collective-permute-done.17 = bf16[72,384]{1,0:T(8,128)(2,1)S(1)} collective-permute-done((bf16[72,384]{1,0:T(8,128)(2,1)S(1)}, bf16[72,384]{1,0:T(8,128)(2,1)S(1)}, u32[]{:S(2)}, u32[]{:S(2)}) %collective-permute-start.17) | collective-permute-done | bytes 55328 | tf_op jit(solution)/shard_map/ppermute | solution.py:620
  87.5 1.9 %collective-permute-start.24 = (bf16[120,384]{1,0:T(8,128)(2,1)S(1)}, bf16[120,384]{1,0:T(8,128)(2,1)S(1)}, u32[]{:S(2)}, u32[]{:S(2)}) collective-permute-start(bf16[120,384]{1,0:T(8,128)(2,1)S(1)} %pad_maximum_fusion), channel_id=1, source_target_pairs={{0,16},{1,17},{2,18},{3,19},{4,20},{5,21},{6,22},{7,23},{8,24},{9,... | collective-permute-start | bytes 276488 | tf_op jit(solution)/shard_map/ppermute | solution.py:620
  89.3 2.4 %collective-permute-start.25 = (bf16[120,384]{1,0:T(8,128)(2,1)S(1)}, bf16[120,384]{1,0:T(8,128)(2,1)S(1)}, u32[]{:S(2)}, u32[]{:S(2)}) collective-permute-start(bf16[120,384]{1,0:T(8,128)(2,1)S(1)} %pad_maximum_fusion), channel_id=1, source_target_pairs={{0,24},{1,25},{2,26},{3,27},{4,28},{5,29},{6,30},{7,31},{8,0},{9,1... | collective-permute-start | bytes 276488 | tf_op jit(solution)/shard_map/ppermute | solution.py:620
  91.8 2.2 %collective-permute-done.23 = bf16[120,384]{1,0:T(8,128)(2,1)S(1)} collective-permute-done((bf16[120,384]{1,0:T(8,128)(2,1)S(1)}, bf16[120,384]{1,0:T(8,128)(2,1)S(1)}, u32[]{:S(2)}, u32[]{:S(2)}) %collective-permute-start.23) | collective-permute-done | bytes 92192 | tf_op jit(solution)/shard_map/ppermute | solution.py:620
  94.0 1.2 %collective-permute-done.24 = bf16[120,384]{1,0:T(8,128)(2,1)S(1)} collective-permute-done((bf16[120,384]{1,0:T(8,128)(2,1)S(1)}, bf16[120,384]{1,0:T(8,128)(2,1)S(1)}, u32[]{:S(2)}, u32[]{:S(2)}) %collective-permute-start.24) | collective-permute-done | bytes 92192 | tf_op jit(solution)/shard_map/ppermute | solution.py:620
  95.3 1.1 collective-permute-start.26
  96.4 1.9 %collective-permute-start.27 = (bf16[336,384]{1,0:T(8,128)(2,1)S(1)}, bf16[336,384]{1,0:T(8,128)(2,1)S(1)}, u32[]{:S(2)}, u32[]{:S(2)}) collective-permute-start(bf16[336,384]{1,0:T(8,128)(2,1)S(1)} %get-tuple-element.75), channel_id=1, source_target_pairs={{0,4},{1,5},{2,6},{3,7},{4,0},{5,1},{6,2},{7,3},{8,12},{9,13},{10,... | collective-permute-start | bytes 774152 | tf_op jit(solution)/shard_map/ppermute | solution.py:620
  99.1 4.4 %collective-permute-done.26 = bf16[336,384]{1,0:T(8,128)(2,1)S(1)} collective-permute-done((bf16[336,384]{1,0:T(8,128)(2,1)S(1)}, bf16[336,384]{1,0:T(8,128)(2,1)S(1)}, u32[]{:S(2)}, u32[]{:S(2)}) %collective-permute-start.26) | collective-permute-done | bytes 258080 | tf_op jit(solution)/shard_map/ppermute | solution.py:620
  103.6 2.7 %collective-permute-done.28 = bf16[336,384]{1,0:T(8,128)(2,1)S(1)} collective-permute-done((bf16[336,384]{1,0:T(8,128)(2,1)S(1)}, bf16[336,384]{1,0:T(8,128)(2,1)S(1)}, u32[]{:S(2)}, u32[]{:S(2)}) %collective-permute-start.28) | collective-permute-done | bytes 258080 | tf_op jit(solution)/shard_map/ppermute | solution.py:620
  110.0 3.6 %finish.1 = (bf16[192,576]{1,0:T(8,128)(2,1)}, bf16[192,192]{1,0:T(8,128)(2,1)}, bf16[768,384]{1,0:T(8,128)(2,1)}, bf16[384,1152]{1,0:T(8,128)(2,1)}, bf16[384,384]{1,0:T(8,128)(2,1)}) custom-call(bf16[1344,384]{1,0:T(8,128)(2,1)} %copy-done, bf16[1344,384]{1,0:T(8,128)(2,1)} %copy-done.1), custom_call_target="tpu_custom_call" | custom-call | tf_op jit(solution)/shard_map/finish/pallas_call | solution.py:867
  (94 shorter events, 12.2 us)
Async XLA Ops:
  2.2 12.3 %collective-permute-start = (bf16[3,2,5760]{2,1,0:T(2,128)(2,1)}, bf16[3,2,5760]{2,1,0:T(2,128)(2,1)S(1)}, u32[]{:S(2)}, u32[]{:S(2)}) collective-permute-start(bf16[3,2,5760]{2,1,0:T(2,128)(2,1)} %get-tuple-element.41), channel_id=1, source_target_pairs={{0,1},{1,0},{2,3},{3,2},{4,5},{5,4},{6,7},{7,6},{8,9},{9,8},{10,11... | collective-permute-start | bytes 207368 | tf_op jit(solution)/shard_map/ppermute | solution.py:570
  5.3 9.3 %collective-permute-start.1 = (bf16[15,2,1152]{2,1,0:T(2,128)(2,1)}, bf16[15,2,1152]{2,1,0:T(2,128)(2,1)S(1)}, u32[]{:S(2)}, u32[]{:S(2)}) collective-permute-start(bf16[15,2,1152]{2,1,0:T(2,128)(2,1)} %get-tuple-element.42), channel_id=1, source_target_pairs={{0,30},{1,31},{2,0},{3,1},{4,2},{5,3},{6,4},{7,5},{8,6},{9,7},{10,... | collective-permute-start | bytes 207368 | tf_op jit(solution)/shard_map/ppermute | solution.py:570
  8.9 5.6 %collective-permute-start.2 = (bf16[3,2,3456]{2,1,0:T(2,128)(2,1)}, bf16[3,2,3456]{2,1,0:T(2,128)(2,1)S(1)}, u32[]{:S(2)}, u32[]{:S(2)}) collective-permute-start(bf16[3,2,3456]{2,1,0:T(2,128)(2,1)} %get-tuple-element.43), channel_id=1, source_target_pairs={{0,31},{1,30},{2,1},{3,0},{4,3},{5,2},{6,5},{7,4},{8,7},{9,6},{10,... | collective-permute-start | bytes 124424 | tf_op jit(solution)/shard_map/ppermute | solution.py:570
  21.0 6.3 %collective-permute-start.3 = (bf16[112,192]{1,0:T(8,128)(2,1)}, bf16[112,192]{1,0:T(8,128)(2,1)S(1)}, u32[]{:S(2)}, u32[]{:S(2)}) collective-permute-start(bf16[112,192]{1,0:T(8,128)(2,1)} %get-tuple-element.46), channel_id=1, source_target_pairs={{0,1},{1,0},{2,3},{3,2},{4,5},{5,4},{6,7},{7,6},{8,9},{9,8},{10,11... | collective-permute-start | bytes 129032 | tf_op jit(solution)/shard_map/ppermute | solution.py:570
  22.5 4.8 %collective-permute-start.4 = (bf16[112,192]{1,0:T(8,128)(2,1)}, bf16[112,192]{1,0:T(8,128)(2,1)S(1)}, u32[]{:S(2)}, u32[]{:S(2)}) collective-permute-start(bf16[112,192]{1,0:T(8,128)(2,1)} %get-tuple-element.47), channel_id=1, source_target_pairs={{0,30},{1,31},{2,0},{3,1},{4,2},{5,3},{6,4},{7,5},{8,6},{9,7},{10,... | collective-permute-start | bytes 129032 | tf_op jit(solution)/shard_map/ppermute | solution.py:570
  23.9 3.5 %collective-permute-start.5 = (bf16[48,192]{1,0:T(8,128)(2,1)}, bf16[48,192]{1,0:T(8,128)(2,1)S(1)}, u32[]{:S(2)}, u32[]{:S(2)}) collective-permute-start(bf16[48,192]{1,0:T(8,128)(2,1)} %get-tuple-element.48), channel_id=1, source_target_pairs={{0,31},{1,30},{2,1},{3,0},{4,3},{5,2},{6,5},{7,4},{8,7},{9,6},{10,... | collective-permute-start | bytes 55304 | tf_op jit(solution)/shard_map/ppermute | solution.py:570
  39.0 27.2 %collective-permute-start.12 = (bf16[1152,384]{1,0:T(8,128)(2,1)}, bf16[1152,384]{1,0:T(8,128)(2,1)S(1)}, u32[]{:S(2)}, u32[]{:S(2)}) collective-permute-start(bf16[1152,384]{1,0:T(8,128)(2,1)} %get-tuple-element.67), channel_id=1, source_target_pairs={{0,2},{1,3},{2,0},{3,1},{4,6},{5,7},{6,4},{7,5},{8,10},{9,11},{10,... | collective-permute-start | bytes 2654216 | tf_op jit(solution)/shard_map/ppermute | solution.py:620
  39.1 8.7 %collective-permute-start.6 = (bf16[112,192]{1,0:T(8,128)(2,1)}, bf16[112,192]{1,0:T(8,128)(2,1)S(1)}, u32[]{:S(2)}, u32[]{:S(2)}) collective-permute-start(bf16[112,192]{1,0:T(8,128)(2,1)} %get-tuple-element.51), channel_id=1, source_target_pairs={{0,1},{1,0},{2,3},{3,2},{4,5},{5,4},{6,7},{7,6},{8,9},{9,8},{10,11... | collective-permute-start | bytes 129032 | tf_op jit(solution)/shard_map/ppermute | solution.py:570
  40.6 7.2 %collective-permute-start.7 = (bf16[112,192]{1,0:T(8,128)(2,1)}, bf16[112,192]{1,0:T(8,128)(2,1)S(1)}, u32[]{:S(2)}, u32[]{:S(2)}) collective-permute-start(bf16[112,192]{1,0:T(8,128)(2,1)} %get-tuple-element.52), channel_id=1, source_target_pairs={{0,2},{1,3},{2,4},{3,5},{4,6},{5,7},{6,8},{7,9},{8,10},{9,11},{10,... | collective-permute-start | bytes 129032 | tf_op jit(solution)/shard_map/ppermute | solution.py:570
  40.8 7.1 %collective-permute-start.8 = (bf16[48,192]{1,0:T(8,128)(2,1)}, bf16[48,192]{1,0:T(8,128)(2,1)S(1)}, u32[]{:S(2)}, u32[]{:S(2)}) collective-permute-start(bf16[48,192]{1,0:T(8,128)(2,1)} %get-tuple-element.53), channel_id=1, source_target_pairs={{0,3},{1,2},{2,5},{3,4},{4,7},{5,6},{6,9},{7,8},{8,11},{9,10},{10,... | collective-permute-start | bytes 55304 | tf_op jit(solution)/shard_map/ppermute | solution.py:570
  48.5 17.7 %copy-start.2 = (bf16[1152,384]{1,0:T(8,128)(2,1)S(1)}, bf16[1152,384]{1,0:T(8,128)(2,1)}, u32[]{:S(2)}) copy-start(bf16[1152,384]{1,0:T(8,128)(2,1)} %get-tuple-element.66) | copy-start | bytes 2654212
  59.0 7.2 %collective-permute-start.9 = (bf16[3,2,3456]{2,1,0:T(2,128)(2,1)}, bf16[3,2,3456]{2,1,0:T(2,128)(2,1)S(1)}, u32[]{:S(2)}, u32[]{:S(2)}) collective-permute-start(bf16[3,2,3456]{2,1,0:T(2,128)(2,1)} %get-tuple-element.61), channel_id=1, source_target_pairs={{0,3},{1,2},{2,5},{3,4},{4,7},{5,6},{6,9},{7,8},{8,11},{9,10},{10,... | collective-permute-start | bytes 124424 | tf_op jit(solution)/shard_map/ppermute | solution.py:570
  59.1 39.2 %collective-permute-start.11 = (bf16[15,2,1152]{2,1,0:T(2,128)(2,1)}, bf16[15,2,1152]{2,1,0:T(2,128)(2,1)S(1)}, u32[]{:S(2)}, u32[]{:S(2)}) collective-permute-start(bf16[15,2,1152]{2,1,0:T(2,128)(2,1)} %get-tuple-element.63), channel_id=1, source_target_pairs={{0,2},{1,3},{2,4},{3,5},{4,6},{5,7},{6,8},{7,9},{8,10},{9,11},{10,... | collective-permute-start | bytes 207368 | tf_op jit(solution)/shard_map/ppermute | solution.py:570
  59.2 39.2 %collective-permute-start.10 = (bf16[3,2,5760]{2,1,0:T(2,128)(2,1)}, bf16[3,2,5760]{2,1,0:T(2,128)(2,1)S(1)}, u32[]{:S(2)}, u32[]{:S(2)}) collective-permute-start(bf16[3,2,5760]{2,1,0:T(2,128)(2,1)} %get-tuple-element.62), channel_id=1, source_target_pairs={{0,1},{1,0},{2,3},{3,2},{4,5},{5,4},{6,7},{7,6},{8,9},{9,8},{10,11... | collective-permute-start | bytes 207368 | tf_op jit(solution)/shard_map/ppermute | solution.py:570
  60.3 9.2 %collective-permute-start.19 = (bf16[192,384]{1,0:T(8,128)(2,1)}, bf16[192,384]{1,0:T(8,128)(2,1)S(1)}, u32[]{:S(2)}, u32[]{:S(2)}) collective-permute-start(bf16[192,384]{1,0:T(8,128)(2,1)} %get-tuple-element.69), channel_id=1, source_target_pairs={{0,2},{1,3},{2,0},{3,1},{4,6},{5,7},{6,4},{7,5},{8,10},{9,11},{10,... | collective-permute-start | bytes 442376 | tf_op jit(solution)/shard_map/ppermute | solution.py:620
  66.9 7.7 %collective-permute-start.15 = (bf16[288,384]{1,0:T(8,128)(2,1)S(1)}, bf16[288,384]{1,0:T(8,128)(2,1)S(1)}, u32[]{:S(2)}, u32[]{:S(2)}) collective-permute-start(bf16[288,384]{1,0:T(8,128)(2,1)S(1)} %get-tuple-element.80), channel_id=1, source_target_pairs={{0,5},{1,4},{2,7},{3,6},{4,1},{5,0},{6,3},{7,2},{8,13},{9,12},{10,... | collective-permute-start | bytes 663560 | tf_op jit(solution)/shard_map/ppermute | solution.py:620
  67.0 9.8 %collective-permute-start.14 = (bf16[288,384]{1,0:T(8,128)(2,1)S(1)}, bf16[288,384]{1,0:T(8,128)(2,1)S(1)}, u32[]{:S(2)}, u32[]{:S(2)}) collective-permute-start(bf16[288,384]{1,0:T(8,128)(2,1)S(1)} %get-tuple-element.81), channel_id=1, source_target_pairs={{0,4},{1,5},{2,6},{3,7},{4,0},{5,1},{6,2},{7,3},{8,12},{9,13},{10,... | collective-permute-start | bytes 663560 | tf_op jit(solution)/shard_map/ppermute | solution.py:620
  69.5 7.8 %collective-permute-start.13 = (bf16[288,384]{1,0:T(8,128)(2,1)S(1)}, bf16[288,384]{1,0:T(8,128)(2,1)S(1)}, u32[]{:S(2)}, u32[]{:S(2)}) collective-permute-start(bf16[288,384]{1,0:T(8,128)(2,1)S(1)} %get-tuple-element.79), channel_id=1, source_target_pairs={{0,1},{1,0},{2,3},{3,2},{4,5},{5,4},{6,7},{7,6},{8,9},{9,8},{10,11... | collective-permute-start | bytes 663560 | tf_op jit(solution)/shard_map/ppermute | solution.py:620
  74.6 4.9 %collective-permute-start.22 = (bf16[48,384]{1,0:T(8,128)(2,1)S(1)}, bf16[48,384]{1,0:T(8,128)(2,1)S(1)}, u32[]{:S(2)}, u32[]{:S(2)}) collective-permute-start(bf16[48,384]{1,0:T(8,128)(2,1)S(1)} %get-tuple-element.86), channel_id=1, source_target_pairs={{0,5},{1,4},{2,7},{3,6},{4,1},{5,0},{6,3},{7,2},{8,13},{9,12},{10,... | collective-permute-start | bytes 110600 | tf_op jit(solution)/shard_map/ppermute | solution.py:620
  76.8 4.5 %collective-permute-start.21 = (bf16[48,384]{1,0:T(8,128)(2,1)S(1)}, bf16[48,384]{1,0:T(8,128)(2,1)S(1)}, u32[]{:S(2)}, u32[]{:S(2)}) collective-permute-start(bf16[48,384]{1,0:T(8,128)(2,1)S(1)} %get-tuple-element.87), channel_id=1, source_target_pairs={{0,4},{1,5},{2,6},{3,7},{4,0},{5,1},{6,2},{7,3},{8,12},{9,13},{10,... | collective-permute-start | bytes 110600 | tf_op jit(solution)/shard_map/ppermute | solution.py:620
  77.3 4.1 %collective-permute-start.20 = (bf16[48,384]{1,0:T(8,128)(2,1)S(1)}, bf16[48,384]{1,0:T(8,128)(2,1)S(1)}, u32[]{:S(2)}, u32[]{:S(2)}) collective-permute-start(bf16[48,384]{1,0:T(8,128)(2,1)S(1)} %get-tuple-element.85), channel_id=1, source_target_pairs={{0,1},{1,0},{2,3},{3,2},{4,5},{5,4},{6,7},{7,6},{8,9},{9,8},{10,11... | collective-permute-start | bytes 110600 | tf_op jit(solution)/shard_map/ppermute | solution.py:620
  79.4 5.3 %collective-permute-start.18 = (bf16[72,384]{1,0:T(8,128)(2,1)S(1)}, bf16[72,384]{1,0:T(8,128)(2,1)S(1)}, u32[]{:S(2)}, u32[]{:S(2)}) collective-permute-start(bf16[72,384]{1,0:T(8,128)(2,1)S(1)} %get-tuple-element.83), channel_id=1, source_target_pairs={{0,24},{1,25},{2,26},{3,27},{4,28},{5,29},{6,30},{7,31},{8,0},{9,1... | collective-permute-start | bytes 165896 | tf_op jit(solution)/shard_map/ppermute | solution.py:620
  81.3 5.2 %collective-permute-start.17 = (bf16[72,384]{1,0:T(8,128)(2,1)S(1)}, bf16[72,384]{1,0:T(8,128)(2,1)S(1)}, u32[]{:S(2)}, u32[]{:S(2)}) collective-permute-start(bf16[72,384]{1,0:T(8,128)(2,1)S(1)} %get-tuple-element.84), channel_id=1, source_target_pairs={{0,16},{1,17},{2,18},{3,19},{4,20},{5,21},{6,22},{7,23},{8,24},{9,... | collective-permute-start | bytes 165896 | tf_op jit(solution)/shard_map/ppermute | solution.py:620
  81.3 6.0 %collective-permute-start.16 = (bf16[72,384]{1,0:T(8,128)(2,1)S(1)}, bf16[72,384]{1,0:T(8,128)(2,1)S(1)}, u32[]{:S(2)}, u32[]{:S(2)}) collective-permute-start(bf16[72,384]{1,0:T(8,128)(2,1)S(1)} %get-tuple-element.82), channel_id=1, source_target_pairs={{0,8},{1,9},{2,10},{3,11},{4,12},{5,13},{6,14},{7,15},{8,16},{9,17... | collective-permute-start | bytes 165896 | tf_op jit(solution)/shard_map/ppermute | solution.py:620
  87.4 6.6 %collective-permute-start.23 = (bf16[120,384]{1,0:T(8,128)(2,1)S(1)}, bf16[120,384]{1,0:T(8,128)(2,1)S(1)}, u32[]{:S(2)}, u32[]{:S(2)}) collective-permute-start(bf16[120,384]{1,0:T(8,128)(2,1)S(1)} %pad_maximum_fusion), channel_id=1, source_target_pairs={{0,8},{1,9},{2,10},{3,11},{4,12},{5,13},{6,14},{7,15},{8,16},{9,17... | collective-permute-start | bytes 276488 | tf_op jit(solution)/shard_map/ppermute | solution.py:620
  87.5 7.7 %collective-permute-start.24 = (bf16[120,384]{1,0:T(8,128)(2,1)S(1)}, bf16[120,384]{1,0:T(8,128)(2,1)S(1)}, u32[]{:S(2)}, u32[]{:S(2)}) collective-permute-start(bf16[120,384]{1,0:T(8,128)(2,1)S(1)} %pad_maximum_fusion), channel_id=1, source_target_pairs={{0,16},{1,17},{2,18},{3,19},{4,20},{5,21},{6,22},{7,23},{8,24},{9,... | collective-permute-start | bytes 276488 | tf_op jit(solution)/shard_map/ppermute | solution.py:620
  89.3 5.9 %collective-permute-start.25 = (bf16[120,384]{1,0:T(8,128)(2,1)S(1)}, bf16[120,384]{1,0:T(8,128)(2,1)S(1)}, u32[]{:S(2)}, u32[]{:S(2)}) collective-permute-start(bf16[120,384]{1,0:T(8,128)(2,1)S(1)} %pad_maximum_fusion), channel_id=1, source_target_pairs={{0,24},{1,25},{2,26},{3,27},{4,28},{5,29},{6,30},{7,31},{8,0},{9,1... | collective-permute-start | bytes 276488 | tf_op jit(solution)/shard_map/ppermute | solution.py:620
  93.9 12.5 %copy-start.13 = (bf16[3,2,2304]{2,1,0:T(2,128)(2,1)S(1)}, bf16[3,2,2304]{2,1,0:T(2,128)(2,1)}, u32[]{:S(2)}) copy-start(bf16[3,2,2304]{2,1,0:T(2,128)(2,1)} %get-tuple-element.64) | copy-start | bytes 82948
  95.3 8.2 %collective-permute-start.26 = (bf16[336,384]{1,0:T(8,128)(2,1)S(1)}, bf16[336,384]{1,0:T(8,128)(2,1)S(1)}, u32[]{:S(2)}, u32[]{:S(2)}) collective-permute-start(bf16[336,384]{1,0:T(8,128)(2,1)S(1)} %get-tuple-element.75), channel_id=1, source_target_pairs={{0,1},{1,0},{2,3},{3,2},{4,5},{5,4},{6,7},{7,6},{8,9},{9,8},{10,11... | collective-permute-start | bytes 774152 | tf_op jit(solution)/shard_map/ppermute | solution.py:620
  96.4 7.2 %collective-permute-start.27 = (bf16[336,384]{1,0:T(8,128)(2,1)S(1)}, bf16[336,384]{1,0:T(8,128)(2,1)S(1)}, u32[]{:S(2)}, u32[]{:S(2)}) collective-permute-start(bf16[336,384]{1,0:T(8,128)(2,1)S(1)} %get-tuple-element.75), channel_id=1, source_target_pairs={{0,4},{1,5},{2,6},{3,7},{4,0},{5,1},{6,2},{7,3},{8,12},{9,13},{10,... | collective-permute-start | bytes 774152 | tf_op jit(solution)/shard_map/ppermute | solution.py:620
  98.5 7.8 %collective-permute-start.28 = (bf16[336,384]{1,0:T(8,128)(2,1)S(1)}, bf16[336,384]{1,0:T(8,128)(2,1)S(1)}, u32[]{:S(2)}, u32[]{:S(2)}) collective-permute-start(bf16[336,384]{1,0:T(8,128)(2,1)S(1)} %get-tuple-element.75), channel_id=1, source_target_pairs={{0,5},{1,4},{2,7},{3,6},{4,1},{5,0},{6,3},{7,2},{8,13},{9,12},{10,... | collective-permute-start | bytes 774152 | tf_op jit(solution)/shard_map/ppermute | solution.py:620
  106.4 2.7 %collective-permute-start.29 = (bf16[1344,384]{1,0:T(8,128)(2,1)S(1)}, bf16[1344,384]{1,0:T(8,128)(2,1)S(1)}, u32[]{:S(2)}, u32[]{:S(2)}) collective-permute-start(bf16[1344,384]{1,0:T(8,128)(2,1)S(1)} %constant_dynamic-update-slice_fusion.2.own), channel_id=1, source_target_pairs={{0,2},{1,3},{2,0},{3,1},{4,6},{5,7},{6,4},{7,5},{8,10},{9,11},{10,... | collective-permute-start | bytes 3096584 | tf_op jit(solution)/shard_map/ppermute | solution.py:620
  (16 other events, 50.3 us)

commit v3 on v2

--- a/solution.py
+++ b/solution.py
@@ -20,6 +20,8 @@
 SPAN = 2 * WIN_LON - 1
 LEVELS = 2
 
+BATCH = (1, 3, 6, 8)
+
 norm_epsilon = 1e-05
 grad_epsilon = 1e-06
 masked_score = -1e30
@@ -47,6 +49,23 @@
 
 def mm_tn(a, b):
     return lax.dot_general(a, b, (((0,), (0,)), ((), ())), preferred_element_type=f32)
+
+
+LIMIT = pltpu.CompilerParams(vmem_limit_bytes=24 << 20)
+
+LIMIT_TWO = pltpu.CompilerParams(vmem_limit_bytes=24 << 20)
+
+
+def near_in(*values):
+    return [pltpu.with_memory_space_constraint(v, pltpu.VMEM) for v in values]
+
+
+def far_in(*values):
+    return [pltpu.with_memory_space_constraint(v, pltpu.HBM) for v in values]
+
+
+def near_out(shapes):
+    return [pltpu.VMEM(s.shape, s.dtype) for s in shapes]
 
 
 def parts_rows(rows, cols, ahead):
@@ -181,10 +200,10 @@
     rows_ref[...] = jnp.zeros(rows_ref.shape, f32)
     for b in range(bands):
         for h in range(HEADS1):
-            rows_ref[8 * b + h : 8 * b + h + 1, :] = table_one[h, pl.ds(kinds_one[b], 1), :]
+            rows_ref[8 * b + h : 8 * b + h + 1, :] = table_one[h, pl.ds(kinds_one[0, b], 1), :]
     for h in range(HEADS2):
         at = 8 * bands + h
-        rows_ref[at : at + 1, :] = table_two[h, pl.ds(kinds_two[0], 1), :]
+        rows_ref[at : at + 1, :] = table_two[h, pl.ds(kinds_two[0, 0], 1), :]
     runs_ref[...] = jnp.zeros(runs_ref.shape, f32)
     for z in range(LEVELS):
         for ap in range(WIN_LAT):
@@ -219,7 +238,7 @@
 
 
 def bias_call(kinds_one, kinds_two, table_one, table_two):
-    bands = kinds_one.shape[0]
+    bands = kinds_one.shape[1]
     target = np.full((8, WIN_LON * 128), -1, np.int32)
     for bp in range(WIN_LON):
         for aq in range(WIN_LAT):
@@ -234,14 +253,15 @@
         in_specs=[smem, smem, vmem, vmem, vmem],
         out_specs=[vmem] * 2,
         out_shape=(
-            jax.ShapeDtypeStruct((bands * LEVELS, HEADS1 * SPOTS, 128), f32),
-            jax.ShapeDtypeStruct((LEVELS, HEADS2 * SPOTS, 128), f32),
+            pltpu.VMEM((bands * LEVELS, HEADS1 * SPOTS, 128), f32),
+            pltpu.VMEM((LEVELS, HEADS2 * SPOTS, 128), f32),
         ),
+        compiler_params=LIMIT,
         scratch_shapes=[
             pltpu.VMEM((slots, table_one.shape[2]), f32),
             pltpu.VMEM((LEVELS * WIN_LAT * slots, 256), f32),
         ],
-    )(kinds_one, kinds_two, table_one, table_two, target)
+    )(kinds_one, kinds_two, *far_in(table_one, table_two, jnp.asarray(target)))
 
 
 def halo_call(tokens, cot, lane1):
@@ -253,12 +273,13 @@
         in_specs=[pl.BlockSpec(memory_space=pl.ANY)] * 2,
         out_specs=[pl.BlockSpec(memory_space=pltpu.VMEM)] * 3,
         out_shape=(
-            jax.ShapeDtypeStruct((HALF_LAT, levels, 2 * lanes - 3 * lane1), bf16),
-            jax.ShapeDtypeStruct((rows - HALF_LAT + 2 * low, levels, lane1), bf16),
-            jax.ShapeDtypeStruct((HALF_LAT, levels, 3 * lane1), bf16),
+            pltpu.VMEM((HALF_LAT, levels, 2 * lanes - 3 * lane1), bf16),
+            pltpu.VMEM((rows - HALF_LAT + 2 * low, levels, lane1), bf16),
+            pltpu.VMEM((HALF_LAT, levels, 3 * lane1), bf16),
         ),
+        compiler_params=LIMIT,
         scratch_shapes=[pltpu.SemaphoreType.DMA((7,))],
-    )(tokens, cot)
+    )(*far_in(tokens, cot))
 
 
 def halo_copies(tokens, cot, lat, lon, diag, sems):
@@ -346,21 +367,16 @@
     units = count // SPOTS
     bands_span = bias.shape[0] // LEVELS
     per_band = units // bands_span
-    for u in range(units):
-        band, level = u // per_band, u % LEVELS
-        r0 = u * SPOTS
-        for at, width in head_groups(channels):
-            masks = lane_head_masks(width)
-            h0 = at // HEAD
-            query = packed_ref[r0 : r0 + SPOTS, at : at + width]
-            key = packed_ref[r0 : r0 + SPOTS, channels + at : channels + at + width].astype(bf16)
-            value = packed_ref[r0 : r0 + SPOTS, 2 * channels + at : 2 * channels + at + width].astype(bf16)
-            rows = slice(h0 * SPOTS, (h0 + len(masks)) * SPOTS)
-            scores = mm_nt(spread_heads(query, masks).astype(bf16), key) * HEAD ** (-0.5)
-            scores = scores + bias[band * LEVELS + level, rows, 0:SPOTS]
-            probs = softmax_rows(scores).astype(bf16)
-            keep_probs[u, rows, 0:SPOTS] = probs
-            att_ref[r0 : r0 + SPOTS, at : at + width] = gather_heads(mm(probs, value), masks)
+
+    def bias_of(key_of):
+        u, rows = key_of
+        return bias[u // per_band * LEVELS + u % LEVELS, rows, 0:SPOTS]
+
+    def keep(key_of, weights):
+        u, rows = key_of
+        keep_probs[u, rows, 0:SPOTS] = weights.astype(bf16)
+
+    attention(packed_ref, att_ref, bias_of, keep, head_jobs(units, channels), channels, BATCH[0])
     attended = att_ref[...].astype(bf16)
     keep_att[...] = attended
     block = (values + mm(attended, w_proj[...])).astype(bf16)
@@ -403,20 +419,14 @@
     hat, scale_two = rms_stats(merged)
     normed = (hat * gain_two[...][None, :]).astype(bf16)
     packed_ref[...] = mm(normed, w_qkv[...]).astype(bf16).astype(f32)
-    masks = lane_head_masks(128)
-    per = len(masks)
-    for z in range(LEVELS):
-        r0 = z * SPOTS
-        for at, width in head_groups(channels):
-            h0 = at // HEAD
-            rows = slice(h0 * SPOTS, (h0 + per) * SPOTS)
-            query = packed_ref[r0 : r0 + SPOTS, at : at + width]
-            key = packed_ref[r0 : r0 + SPOTS, channels + at : channels + at + width].astype(bf16)
-            value = packed_ref[r0 : r0 + SPOTS, 2 * channels + at : 2 * channels + at + width].astype(bf16)
-            scores = mm_nt(spread_heads(query, masks).astype(bf16), key) * HEAD ** (-0.5)
-            probs = softmax_rows(scores + bias[z, rows, 0:SPOTS])
-            probs_ref[z, rows, 0:SPOTS] = probs
-            att_ref[r0 : r0 + SPOTS, at : at + width] = gather_heads(mm(probs.astype(bf16), value), masks)
+
+    def keep(key_of, weights):
+        probs_ref[key_of[0], key_of[1], 0:SPOTS] = weights
+
+    jobs = head_jobs(LEVELS, channels)
+    attention(
+        packed_ref, att_ref, lambda k: bias[k[0], k[1], 0:SPOTS], keep, jobs, channels, BATCH[1]
+    )
     attended = att_ref[...].astype(bf16)
     block = (merged + mm(attended, w_proj[...])).astype(bf16)
     lace_rows = lace_ref.shape[0]
@@ -434,14 +444,9 @@
     at_sum = groups * thin
     sums_ref[at_sum : at_sum + channels, :] = mm_tn(attended, d_block_low)
     att_ref[...] = mm_nt(d_block_low, w_proj[...]).astype(bf16).astype(f32)
-    for z in range(LEVELS):
-        r0 = z * SPOTS
-        for at, width in head_groups(channels):
-            h0 = at // HEAD
-            rows = slice(h0 * SPOTS, (h0 + per) * SPOTS)
-            attention_back(
-                packed_ref, att_ref, d_packed_ref, probs_ref[z, rows, 0:SPOTS], masks, r0, at, width, channels
-            )
+    attention_back(
+        packed_ref, att_ref, d_packed_ref, lambda k: probs_ref[k[0], k[1], 0:SPOTS], jobs, channels, BATCH[2]
+    )
     d_packed = d_packed_ref[...].astype(bf16)
     at_sum += channels
     for n in range(3):
@@ -474,22 +479,70 @@
     sums_send[...] = sums_ref[pl.ds(other_row, half), :].astype(bf16)
 
 
-def attention_back(packed_ref, d_att_ref, d_packed_ref, probs, masks, r0, at, width, channels):
-    query = packed_ref[r0 : r0 + SPOTS, at : at + width]
-    key = packed_ref[r0 : r0 + SPOTS, channels + at : channels + at + width].astype(bf16)
-    value = packed_ref[r0 : r0 + SPOTS, 2 * channels + at : 2 * channels + at + width].astype(bf16)
-    d_att = spread_heads(d_att_ref[r0 : r0 + SPOTS, at : at + width], masks).astype(bf16)
-    probs_low = probs.astype(bf16)
-    probs = probs.astype(f32)
-    d_probs = mm_nt(d_att, value).astype(bf16).astype(f32)
-    d_value = mm_tn(probs_low, d_att)
-    inner = jnp.sum(probs * d_probs, axis=-1, keepdims=True)
-    d_scores = (probs * (d_probs - inner) * HEAD ** (-0.5)).astype(bf16)
-    d_query = gather_heads(mm(d_scores, key), masks)
-    d_key = mm_tn(d_scores, spread_heads(query, masks).astype(bf16))
-    d_packed_ref[r0 : r0 + SPOTS, at : at + width] = d_query
-    d_packed_ref[r0 : r0 + SPOTS, channels + at : channels + at + width] = d_key
-    d_packed_ref[r0 : r0 + SPOTS, 2 * channels + at : 2 * channels + at + width] = d_value
+def qkv_of(packed_ref, r0, at, width, channels):
+    rows = slice(r0, r0 + SPOTS)
+    query = packed_ref[rows, at : at + width]
+    key = packed_ref[rows, channels + at : channels + at + width].astype(bf16)
+    value = packed_ref[rows, 2 * channels + at : 2 * channels + at + width].astype(bf16)
+    return query, key, value
+
+
+def batches(jobs, size):
+    return [jobs[n : n + size] for n in range(0, len(jobs), size)]
+
+
+def attention_back(packed_ref, d_att_ref, d_packed_ref, probs_of, jobs, channels, size):
+    for batch in batches(jobs, size):
+        state = []
+        for r0, at, width, key_of in batch:
+            masks = lane_head_masks(width)
+            value = qkv_of(packed_ref, r0, at, width, channels)[2]
+            d_att = spread_heads(d_att_ref[r0 : r0 + SPOTS, at : at + width], masks).astype(bf16)
+            state.append((d_att, mm_nt(d_att, value)))
+        scores = []
+        for (r0, at, width, key_of), (d_att, d_probs) in zip(batch, state):
+            probs = probs_of(key_of).astype(f32)
+            d_probs = d_probs.astype(bf16).astype(f32)
+            inner = jnp.sum(probs * d_probs, axis=-1, keepdims=True)
+            scores.append((probs * (d_probs - inner) * HEAD ** (-0.5)).astype(bf16))
+        for (r0, at, width, key_of), (d_att, _), d_scores in zip(batch, state, scores):
+            masks = lane_head_masks(width)
+            query, key, _ = qkv_of(packed_ref, r0, at, width, channels)
+            rows = slice(r0, r0 + SPOTS)
+            d_packed_ref[rows, at : at + width] = gather_heads(mm(d_scores, key), masks)
+            d_packed_ref[rows, channels + at : channels + at + width] = mm_tn(
+                d_scores, spread_heads(query, masks).astype(bf16)
+            )
+            d_packed_ref[rows, 2 * channels + at : 2 * channels + at + width] = mm_tn(
+                probs_of(key_of).astype(bf16), d_att
+            )
+
+
+def attention(packed_ref, att_ref, bias_of, keep, jobs, channels, size):
+    for batch in batches(jobs, size):
+        scores = []
+        for r0, at, width, key_of in batch:
+            masks = lane_head_masks(width)
+            query, key, _ = qkv_of(packed_ref, r0, at, width, channels)
+            scores.append(mm_nt(spread_heads(query, masks).astype(bf16), key))
+        probs = []
+        for (r0, at, width, key_of), score in zip(batch, scores):
+            weights = softmax_rows(score * HEAD ** (-0.5) + bias_of(key_of))
+            keep(key_of, weights)
+            probs.append(weights.astype(bf16))
+        for (r0, at, width, key_of), weights in zip(batch, probs):
+            value = qkv_of(packed_ref, r0, at, width, channels)[2]
+            att_ref[r0 : r0 + SPOTS, at : at + width] = gather_heads(
+                mm(weights, value), lane_head_masks(width)
+            )
+
+
+def head_jobs(units, channels):
+    return [
+        (u * SPOTS, at, width, (u, slice(at // HEAD * SPOTS, (at + width) // HEAD * SPOTS)))
+        for u in range(units)
+        for at, width in head_groups(channels)
+    ]
 
 
 def backward_one_kernel(
@@ -510,15 +563,10 @@
     normed = (hat * gain[...][None, :]).astype(bf16)
     packed_ref[...] = keep_packed[...].astype(f32)
     att_ref[...] = mm_nt(d_block_low, w_proj[...]).astype(bf16).astype(f32)
-    for u in range(count // SPOTS):
-        r0 = u * SPOTS
-        for at, width in head_groups(channels):
-            masks = lane_head_masks(width)
-            h0 = at // HEAD
-            rows = slice(h0 * SPOTS, (h0 + len(masks)) * SPOTS)
-            attention_back(
-                packed_ref, att_ref, d_packed_ref, keep_probs[u, rows, 0:SPOTS], masks, r0, at, width, channels
-            )
+    attention_back(
+        packed_ref, att_ref, d_packed_ref, lambda k: keep_probs[k[0], k[1], 0:SPOTS],
+        head_jobs(count // SPOTS, channels), channels, BATCH[3],
+    )
     d_packed = d_packed_ref[...].astype(bf16)
     sums_ref[:, 0 : 3 * channels] = mm_tn(normed, d_packed)
     sums_ref[:, 3 * channels : 4 * channels] = mm_tn(keep_att[...], d_block_low)
@@ -574,10 +622,23 @@
     return (send(lat, 0, step), send(lon, step, 0), send(diag, step, step))
 
 
-def joined(main, lat, lon, diag):
-    top = jnp.concatenate([diag, lat], axis=2)
-    rest = jnp.concatenate([lon, main], axis=2)
-    return jnp.concatenate([top, rest], axis=0).transpose(1, 0, 2)
+def join_kernel(res_main, d_main, lat, lon, diag, result, d_tokens):
+    rows, lanes = d_tokens.shape[0], d_tokens.shape[2]
+    cut = HALF_LAT
+    kept = d_main.shape[2]
+    lane1 = lanes - kept
+    d_tokens[cut:rows, :, lane1:lanes] = d_main[...]
+    d_tokens[0:cut, :, lane1:lanes] = lat[:, :, 0:kept]
+    d_tokens[cut:rows, :, 0:lane1] = lon[0 : rows - cut]
+    d_tokens[0:cut, :, 0:lane1] = diag[:, :, 0:lane1]
+    low = res_main.shape[0]
+    lane2 = 2 * lane1
+    result[cut : cut + low, :, lane2:lanes] = res_main[...]
+    result[0:cut, :, lane2:lanes] = lat[:, :, kept:]
+    result[0:cut, :, 0:lane2] = diag[:, :, lane1:]
+    for n in range(2):
+        at = rows - cut + n * low
+        result[cut : cut + low, :, n * lane1 : (n + 1) * lane1] = lon[at : at + low]
 
 
 def place_stages():
@@ -628,38 +689,90 @@
     return at ^ d if stage == 0 else (at + d) % size
 
 
-def scatter(value, stages):
-    for n, (size, step, at) in enumerate(stages):
-        chunks = value.reshape(size, value.shape[0] // size, value.shape[1])
-        total = lax.dynamic_index_in_dim(chunks, at, 0, False).astype(f32)
-        got = [hop(lax.dynamic_index_in_dim(chunks, target(n, at, d, size), 0, False), step, d) for d in range(1, size)]
-        for part in got:
-            total = total + part.astype(f32)
-        value = total.astype(bf16)
-    return value
-
-
-def paired(keep, sent):
-    return (keep.astype(f32) + pair(sent).astype(f32)).astype(bf16)
-
-
-def gather(two, one, stages):
-    for n, (size, step, at) in reversed(list(enumerate(stages))):
-        message = jnp.concatenate([two, one], axis=0)
-        got = [message] + [hop(message, step, d) for d in range(1, size)]
-        if n == 0:
-            return jnp.concatenate(got, axis=0)
-        rows = two.shape[0]
-        two = jnp.concatenate([m[:rows] for m in got], axis=0)
-        one = sum(m[rows:].astype(f32) for m in got).astype(bf16)
-
-
-def finish_kernel(own, far, g_qkv_one, g_proj_one, g_merge, g_qkv_two, g_proj_two,
-                  two_ref, one_ref, *, stage_sizes):
+def total_of(refs, rows):
+    total = refs[0][rows, :].astype(f32)
+    for r in refs[1:]:
+        total = total + r[rows, :].astype(f32)
+    return total
+
+
+def split_kernel(*refs, count, stage):
+    size, _, at = place_stages()[stage]
+    outs, scratch = refs[count:-1], refs[-1]
+    rows = scratch.shape[1]
+    for p in range(size):
+        scratch[p] = total_of(refs[:count], slice(p * rows, (p + 1) * rows))
+    for d in range(size):
+        outs[d][...] = scratch[target(stage, at, d, size)].astype(bf16)
+
+
+def sum_split(values, stage):
+    size = place_stages()[stage][0]
+    rows, width = values[0].shape
+    vmem = pl.BlockSpec(memory_space=pltpu.VMEM)
+    return pl.pallas_call(
+        functools.partial(split_kernel, count=len(values), stage=stage),
+        in_specs=[vmem] * len(values),
+        out_specs=[vmem] * size,
+        out_shape=[pltpu.VMEM((rows // size, width), bf16)] * size,
+        scratch_shapes=[pltpu.VMEM((size, rows // size, width), f32)],
+        compiler_params=LIMIT,
+    )(*near_in(*values))
+
+
+def message_kernel(*refs, count):
+    out = refs[-1]
+    rows = refs[0].shape[0]
+    out[0:rows, :] = total_of(refs[:count], slice(0, rows)).astype(bf16)
+    small = refs[count].shape[0]
+    out[rows : rows + small, :] = total_of(refs[count:-1], slice(0, small)).astype(bf16)
+
+
+def message_of(two, one):
+    vmem = pl.BlockSpec(memory_space=pltpu.VMEM)
+    values = [*two, *one]
+    return pl.pallas_call(
+        functools.partial(message_kernel, count=len(two)),
+        name="message",
+        in_specs=[vmem] * len(values),
+        out_specs=vmem,
+        out_shape=pltpu.VMEM((two[0].shape[0] + one[0].shape[0], two[0].shape[1]), bf16),
+        compiler_params=LIMIT,
+    )(*near_in(*values))
+
+
+def widen_kernel(*refs, rows):
+    out, ins = refs[-1], refs[:-1]
+    for n, r in enumerate(ins):
+        out[n * rows : (n + 1) * rows, :] = r[0:rows, :]
+    total = ins[0].shape[0]
+    out[len(ins) * rows :, :] = total_of(ins, slice(rows, total)).astype(bf16)
+
+
+def widen(messages, small):
+    vmem = pl.BlockSpec(memory_space=pltpu.VMEM)
+    rows = messages[0].shape[0] - small
+    return pl.pallas_call(
+        functools.partial(widen_kernel, rows=rows),
+        name="widen",
+        in_specs=[vmem] * len(messages),
+        out_specs=vmem,
+        out_shape=pltpu.VMEM((rows * len(messages) + small, messages[0].shape[1]), bf16),
+        compiler_params=LIMIT,
+    )(*near_in(*messages))
+
+
+def moves(values, stage):
+    size, step, _ = place_stages()[stage]
+    return [values[0]] + [hop(values[d], step, d) for d in range(1, size)]
+
+
+def finish_kernel(*refs, stage_sizes):
+    near = stage_sizes[0]
+    own, far = refs[:near], refs[near : 2 * near]
+    g_qkv_one, g_proj_one, g_merge, g_qkv_two, g_proj_two, two_ref, one_ref = refs[2 * near :]
     mine = core_of()
     spots = [at for _, _, at in place_stages()]
-    near = stage_sizes[0]
-    span = own.shape[0] // near
     inner = two_ref.shape[0] // (2 * near)
     size = two_ref.shape[1]
     places = [jnp.int32(0)]
@@ -671,13 +784,13 @@
     for d in range(near):
         place = spots[0] ^ d
         for p in range(inner):
-            rows = slice(d * span + p * size, d * span + (p + 1) * size)
+            rows = slice(p * size, (p + 1) * size)
             at = place * inner + places[p]
-            two_ref[mine * near * inner + at] = own[rows, :].astype(f32)
-            two_ref[(1 - mine) * near * inner + at] = far[rows, :].astype(f32)
-        rows = slice(d * span + inner * size, (d + 1) * span)
-        one_ref[mine * near + place] = own[rows, :].astype(f32)
-        one_ref[(1 - mine) * near + place] = far[rows, :].astype(f32)
+            two_ref[mine * near * inner + at] = own[d][rows, :].astype(f32)
+            two_ref[(1 - mine) * near * inner + at] = far[d][rows, :].astype(f32)
+        rows = slice(inner * size, own[d].shape[0])
+        one_ref[mine * near + place] = own[d][rows, :].astype(f32)
+        one_ref[(1 - mine) * near + place] = far[d][rows, :].astype(f32)
 
     def scale_of(parts, entries):
         total = parts[0]
@@ -770,7 +883,7 @@
     cot = cotangent.transpose(1, 0, 2)
     halos = exchange(*halo_call(lattice, cot, HALF_LON * c1), -1)
     bias_one, bias_two = bias_call(
-        kinds_one[0], kinds_two[0], table_one.swapaxes(0, 1), table_two.swapaxes(0, 1)
+        kinds_one, kinds_two, table_one.swapaxes(0, 1), table_two.swapaxes(0, 1)
     )
 
     def part_shapes(dtype=bf16):
@@ -790,19 +903,22 @@
         name="forward_one",
         in_specs=[vmem] * 9,
         out_specs=[vmem] * 8,
-        out_shape=part_shapes()
-        + [
-            jax.ShapeDtypeStruct((count1, c1), bf16),
-            jax.ShapeDtypeStruct((count1, 3 * c1), bf16),
-            jax.ShapeDtypeStruct((units1, HEADS1 * SPOTS, 128), bf16),
-            jax.ShapeDtypeStruct((count1, c1), bf16),
-        ],
+        out_shape=near_out(
+            part_shapes()
+            + [
+                jax.ShapeDtypeStruct((count1, c1), bf16),
+                jax.ShapeDtypeStruct((count1, 3 * c1), bf16),
+                jax.ShapeDtypeStruct((units1, HEADS1 * SPOTS, 128), bf16),
+                jax.ShapeDtypeStruct((count1, c1), bf16),
+            ]
+        ),
+        compiler_params=LIMIT,
         scratch_shapes=[
             pltpu.VMEM((LEVELS * rows1, cols1 * c1), f32),
             pltpu.VMEM((count1, 3 * c1), f32),
             pltpu.VMEM((count1, c1), f32),
         ],
-    )(lattice, *halos, bias_one, gain_one, qkv_one, proj_one, index)
+    )(*near_in(lattice, *halos, bias_one, gain_one, qkv_one, proj_one, index))
     parts, kept = fwd[:4], fwd[4:]
     got = exchange(*parts[1:], -1)
 
@@ -813,9 +929,12 @@
         name="merge_two",
         in_specs=[vmem] * 15,
         out_specs=[vmem] * 10,
-        out_shape=lace_shapes(rows2, cols2, c2)
-        + part_shapes()
-        + [jax.ShapeDtypeStruct((total_two // 2, c2), bf16)] * 2,
+        out_shape=near_out(
+            lace_shapes(rows2, cols2, c2)
+            + part_shapes()
+            + [jax.ShapeDtypeStruct((total_two // 2, c2), bf16)] * 2
+        ),
+        compiler_params=LIMIT_TWO,
         scratch_shapes=[
             pltpu.VMEM((lace2_pad, cols2 * c2), f32),
             pltpu.VMEM((LEVELS, HEADS2 * SPOTS, 128), f32),
@@ -824,12 +943,13 @@
             pltpu.VMEM((tokens2, 3 * c2), f32),
             pltpu.VMEM((total_two, c2), f32),
         ],
-    )(parts[0], *got, cot, *halos, bias_two, gain_merge, gain_two,
-      merge_weight, qkv_two, proj_two, index)
+    )(*near_in(parts[0], *got, cot, *halos, bias_two, gain_merge, gain_two,
+                merge_weight, qkv_two, proj_two, index))
     res, d_parts, sums_two = two[:4], two[4:8], two[8:]
-    half_two = paired(*sums_two)
     d_got = exchange(*d_parts[1:], 1)
-    mine_two = scatter(half_two, stages)
+    two_parts = [sums_two[0], pair(sums_two[1])]
+    for n in range(len(stages)):
+        two_parts = moves(sum_split(two_parts, n), n)
 
     lanes1, lane1 = tokens.shape[2], HALF_LON * c1
     one = pl.pallas_call(
@@ -837,11 +957,14 @@
         name="backward_one",
         in_specs=[vmem] * 15,
         out_specs=[vmem] * 6,
-        out_shape=[
-            jax.ShapeDtypeStruct((rows1 - HALF_LAT, LEVELS, lanes1 - lane1), bf16),
-            *(jax.ShapeDtypeStruct(h.shape, bf16) for h in halos),
-        ]
-        + [jax.ShapeDtypeStruct((c1, 2 * c1), bf16)] * 2,
+        out_shape=near_out(
+            [
+                jax.ShapeDtypeStruct((rows1 - HALF_LAT, LEVELS, lanes1 - lane1), bf16),
+                *(jax.ShapeDtypeStruct(h.shape, bf16) for h in halos),
+            ]
+            + [jax.ShapeDtypeStruct((c1, 2 * c1), bf16)] * 2
+        ),
+        compiler_params=LIMIT,
         scratch_shapes=[
             pltpu.VMEM((LEVELS * rows1, cols1 * c1), f32),
             pltpu.VMEM((count1, 3 * c1), f32),
@@ -849,16 +972,29 @@
             pltpu.VMEM((count1, 3 * c1), f32),
             pltpu.VMEM((c1, 4 * c1), f32),
         ],
-    )(d_parts[0], *d_got, *kept, *res[1:], gain_one, qkv_one, proj_one, index)
+    )(*near_in(d_parts[0], *d_got, *kept, *res[1:], gain_one, qkv_one, proj_one, index))
     d_tok, sums_one = one[:4], one[4:]
-    mine_one = scatter(paired(*sums_one), stages[:1])
-    own = gather(mine_two, mine_one, stages)
-    far = pair(own)
-    lat, lon, diag = exchange(*d_tok[1:], 1)
-    kept, low, cut2 = lanes1 - lane1, rows1 - HALF_LAT, rows2 - HALF_LAT
-    d_tokens = joined(d_tok[0], lat[:, :, :kept], lon[:low], diag[:, :, :lane1])
-    lon = jnp.concatenate([lon[low : low + cut2], lon[low + cut2 :]], axis=2)
-    result = joined(res[0], lat[:, :, kept:], lon, diag[:, :, lane1:])
+    one_parts = [sums_one[0], pair(sums_one[1])]
+    one_parts = moves(sum_split(one_parts, 0), 0)
+    message = message_of(two_parts, one_parts)
+    small = one_parts[0].shape[0]
+    for n in range(len(stages) - 1, 0, -1):
+        message = widen(moves([message] * stages[n][0], n), small)
+    own = moves([message] * stages[0][0], 0)
+    far = [pair(m) for m in own]
+    back = exchange(*d_tok[1:], 1)
+    joined = pl.pallas_call(
+        join_kernel,
+        name="join",
+        in_specs=[vmem] * 5,
+        out_specs=[vmem] * 2,
+        out_shape=[
+            jax.ShapeDtypeStruct((rows2, LEVELS, lanes1), bf16),
+            jax.ShapeDtypeStruct((rows1, LEVELS, lanes1), bf16),
+        ],
+        compiler_params=LIMIT,
+    )(*near_in(res[0], d_tok[0], *back))
+    result, d_tokens = (v.transpose(1, 0, 2) for v in joined)
 
     near = stages[0][0]
     inner = 1
@@ -867,16 +1003,17 @@
     grads = pl.pallas_call(
         functools.partial(finish_kernel, stage_sizes=tuple(size for size, _, _ in stages)),
         name="finish",
-        in_specs=[vmem] * 2,
+        in_specs=[vmem] * (2 * near),
         out_specs=[vmem] * 5,
         out_shape=[
             jax.ShapeDtypeStruct(w.shape, bf16) for w in (qkv_one, proj_one, merge_weight, qkv_two, proj_two)
         ],
         scratch_shapes=[
-            pltpu.VMEM((2 * near * inner,) + mine_two.shape, f32),
-            pltpu.VMEM((2 * near,) + mine_one.shape, f32),
+            pltpu.VMEM((2 * near * inner,) + two_parts[0].shape, f32),
+            pltpu.VMEM((2 * near,) + one_parts[0].shape, f32),
         ],
-    )(own, far)
+        compiler_params=LIMIT,
+    )(*near_in(*own, *far))
     return (result, d_tokens, *grads)
 
 

time: 116 us -> 108 us (0.931); the launches traced: 114 us -> 108 us
  Pallas kernels: 36.5 us -> 23.2 us
  waiting for transfers between devices: 38.9 us -> 45.7 us
  starting transfers between devices: 30.6 us -> 36.7 us
  local copies, waits for them, and re-layouts: 3.75 us -> 0.71 us
  other arithmetic: 2.25 us -> 0 us
    ppermute x12, waiting for transfers between devices: 15.4 us -> 24.8 us  [send(): return lax.ppermute(values, AXES, route)]
    pallas_call x1, Pallas kernels: 10.5 us -> 5.24 us  [shards(): pl.pallas_call(functools.partial(backward_one_kernel, cols=cols1, columns...]
    ppermute x18 -> x21, starting transfers between devices: 16.1 us -> 20.3 us  [hop(): return lax.ppermute(values, AXES, route)]
    pallas_call x1, Pallas kernels: 11 us -> 7.26 us  [shards(): pl.pallas_call(functools.partial(merge_two_kernel, cols=cols2, columns=(2...]
    unnamed x39 -> x24, local copies, waits for them, and re-layouts: 3.45 us -> 0.71 us
    ppermute x18 -> x21, waiting for transfers between devices: 23.5 us -> 20.9 us  [hop(): return lax.ppermute(values, AXES, route)]
    pallas_call x1, Pallas kernels: 5.84 us -> 3.47 us  [shards(): pl.pallas_call(functools.partial(forward_one_kernel, cols=cols1, columns=...]
    ppermute x12, starting transfers between devices: 14.4 us -> 16.4 us  [send(): return lax.ppermute(values, AXES, route)]
  transfers between devices with their start and end apart: 30 -> 33, of which waited for: 15 -> 16; matrix products, arithmetic and copies ran while one was open for 2% -> 0% of each run, Pallas kernels for 13% -> 9%
where the time goes in v3:
time: 108 us
  waiting for transfers between devices  45.7 us (42%)
  starting transfers between devices  36.7 us (34%)
  Pallas kernels  23.2 us (21%)
  between operations  1.6 us (1%)
    ppermute x12, waiting for transfers between devices, send(): return lax.ppermute(values, AXES, route)  24.8 us
    ppermute x21, waiting for transfers between devices, hop(): return lax.ppermute(values, AXES, route)  20.9 us
    ppermute x21, starting transfers between devices, hop(): return lax.ppermute(values, AXES, route)  20.3 us
    ppermute x12, starting transfers between devices, send(): return lax.ppermute(values, AXES, route)  16.4 us
    pallas_call x1, Pallas kernels, shards(): pl.pallas_call(functools.partial(merge_two_kernel, cols=cols2, columns=(2...  7.26 us
    pallas_call x1, Pallas kernels, shards(): pl.pallas_call(functools.partial(backward_one_kernel, cols=cols1, columns...  5.24 us
    pallas_call x1, Pallas kernels, shards(): pl.pallas_call(functools.partial(forward_one_kernel, cols=cols1, columns=...  3.47 us
    pallas_call x1, Pallas kernels, bias_call(): pl.pallas_call(expand_bias, name='bias', in_specs=[smem, smem, vmem, vmem...  2.8 us
  transfers between devices with their start and end apart: 33, of which 16 were waited for; matrix products, arithmetic and copies ran while one was open for 0% of the time, Pallas kernels for 9%

profile of v3, /device:TPU:0, one launch (start us, length us, event | category | flops | bytes accessed | tf_op | source)
XLA Modules:
  0.0 108.0 jit_solution(7334021280427171655)
XLA Ops:
  1.6 3.1 %collective-permute-start = (bf16[3,2,5760]{2,1,0:T(2,128)(2,1)S(1)}, bf16[3,2,5760]{2,1,0:T(2,128)(2,1)S(1)}, u32[]{:S(2)}, u32[]{:S(2)}) collective-permute-start(bf16[3,2,5760]{2,1,0:T(2,128)(2,1)S(1)} %get-tuple-element.55), channel_id=1, source_target_pairs={{0,1},{1,0},{2,3},{3,2},{4,5},{5,4},{6,7},{7,6},{8,9},{9,8},{10,11... | collective-permute-start | bytes 207368 | tf_op jit(solution)/shard_map/ppermute | solution.py:618
  4.7 3.7 %collective-permute-start.1 = (bf16[15,2,1152]{2,1,0:T(2,128)(2,1)S(1)}, bf16[15,2,1152]{2,1,0:T(2,128)(2,1)S(1)}, u32[]{:S(2)}, u32[]{:S(2)}) collective-permute-start(bf16[15,2,1152]{2,1,0:T(2,128)(2,1)S(1)} %get-tuple-element.56), channel_id=1, source_target_pairs={{0,30},{1,31},{2,0},{3,1},{4,2},{5,3},{6,4},{7,5},{8,6},{9,7},{10,... | collective-permute-start | bytes 207368 | tf_op jit(solution)/shard_map/ppermute | solution.py:618
  10.6 2.8 %bias.1 = (f32[4,432,128]{2,1,0:T(8,128)S(1)}, f32[2,864,128]{2,1,0:T(8,128)S(1)}) custom-call(s32[1,2]{1,0:T(1,128)S(1)} %copy-done.11, s32[1,1]{1,0:T(1,128)S(6)} %copy.23.kinds_two, f32[6,8,3312]{2,1,0:T(8,128)} %bitcast.11, f32[12,8,3312]{2,1,0:T(8,128)} %bitcast.10, s32[8,1536]{1,0:T(8,128)} %constant.5.clone.target), custom_call_target="tpu_custom_call" | custom-call | tf_op jit(solution)/shard_map/bias/pallas_call | solution.py:250
  13.6 3.5 %forward_one.1 = (bf16[336,192]{1,0:T(8,128)(2,1)S(1)}, bf16[112,192]{1,0:T(8,128)(2,1)S(1)}, bf16[112,192]{1,0:T(8,128)(2,1)S(1)}, bf16[48,192]{1,0:T(8,128)(2,...) custom-call(bf16[12,2,4608]{2,1,0:T(2,128)(2,1)S(1)} %bitcast.7, ...), custom_call_target="tpu_custom_call" | custom-call | tf_op jit(solution)/shard_map/forward_one/pallas_call | solution.py:901
  17.0 1.6 %collective-permute-start.3 = (bf16[112,192]{1,0:T(8,128)(2,1)S(1)}, bf16[112,192]{1,0:T(8,128)(2,1)S(1)}, u32[]{:S(2)}, u32[]{:S(2)}) collective-permute-start(bf16[112,192]{1,0:T(8,128)(2,1)S(1)} %get-tuple-element.60), channel_id=1, source_target_pairs={{0,1},{1,0},{2,3},{3,2},{4,5},{5,4},{6,7},{7,6},{8,9},{9,8},{10,11... | collective-permute-start | bytes 129032 | tf_op jit(solution)/shard_map/ppermute | solution.py:618
  18.6 1.6 %collective-permute-start.4 = (bf16[112,192]{1,0:T(8,128)(2,1)S(1)}, bf16[112,192]{1,0:T(8,128)(2,1)S(1)}, u32[]{:S(2)}, u32[]{:S(2)}) collective-permute-start(bf16[112,192]{1,0:T(8,128)(2,1)S(1)} %get-tuple-element.61), channel_id=1, source_target_pairs={{0,30},{1,31},{2,0},{3,1},{4,2},{5,3},{6,4},{7,5},{8,6},{9,7},{10,... | collective-permute-start | bytes 129032 | tf_op jit(solution)/shard_map/ppermute | solution.py:618
  21.2 2.6 %collective-permute-done.5.diag = bf16[48,192]{1,0:T(8,128)(2,1)S(1)} collective-permute-done((bf16[48,192]{1,0:T(8,128)(2,1)S(1)}, bf16[48,192]{1,0:T(8,128)(2,1)S(1)}, u32[]{:S(2)}, u32[]{:S(2)}) %collective-permute-start.5) | collective-permute-done | bytes 18464 | tf_op jit(solution)/shard_map/ppermute | solution.py:618
  23.8 7.3 %merge_two.1 = (bf16[3,2,2304]{2,1,0:T(2,128)(2,1)S(1)}, bf16[3,2,2304]{2,1,0:T(2,128)(2,1)S(1)}, bf16[3,2,2304]{2,1,0:T(2,128)(2,1)S(1)}, bf16[3,2,2304]{2,1,0:...) custom-call(bf16[336,192]{1,0:T(8,128)(2,1)S(1)} %get-tuple-element., ...), custom_call_target="tpu_custom_call" | custom-call | tf_op jit(solution)/shard_map/merge_two/pallas_call | solution.py:927
  31.1 1.3 %collective-permute-start.8 = (bf16[48,192]{1,0:T(8,128)(2,1)S(1)}, bf16[48,192]{1,0:T(8,128)(2,1)S(1)}, u32[]{:S(2)}, u32[]{:S(2)}) collective-permute-start(bf16[48,192]{1,0:T(8,128)(2,1)S(1)} %get-tuple-element.68), channel_id=1, source_target_pairs={{0,3},{1,2},{2,5},{3,4},{4,7},{5,6},{6,9},{7,8},{8,11},{9,10},{10,... | collective-permute-start | bytes 55304 | tf_op jit(solution)/shard_map/ppermute | solution.py:618
  32.5 1.1 collective-permute-done.12.refs_1_
  33.9 1.3 %collective-permute-start.13 = (bf16[288,384]{1,0:T(8,128)(2,1)S(1)}, bf16[288,384]{1,0:T(8,128)(2,1)S(1)}, u32[]{:S(2)}, u32[]{:S(2)}) collective-permute-start(bf16[288,384]{1,0:T(8,128)(2,1)S(1)} %get-tuple-element.85), channel_id=1, source_target_pairs={{0,1},{1,0},{2,3},{3,2},{4,5},{5,4},{6,7},{7,6},{8,9},{9,8},{10,11... | collective-permute-start | bytes 663560 | tf_op jit(solution)/shard_map/ppermute | solution.py:681
  35.2 2.2 %collective-permute-start.15 = (bf16[288,384]{1,0:T(8,128)(2,1)S(1)}, bf16[288,384]{1,0:T(8,128)(2,1)S(1)}, u32[]{:S(2)}, u32[]{:S(2)}) collective-permute-start(bf16[288,384]{1,0:T(8,128)(2,1)S(1)} %get-tuple-element.87), channel_id=1, source_target_pairs={{0,5},{1,4},{2,7},{3,6},{4,1},{5,0},{6,3},{7,2},{8,13},{9,12},{10,... | collective-permute-start | bytes 663560 | tf_op jit(solution)/shard_map/ppermute | solution.py:681
  37.4 1.2 %collective-permute-start.6 = (bf16[112,192]{1,0:T(8,128)(2,1)S(1)}, bf16[112,192]{1,0:T(8,128)(2,1)S(1)}, u32[]{:S(2)}, u32[]{:S(2)}) collective-permute-start(bf16[112,192]{1,0:T(8,128)(2,1)S(1)} %get-tuple-element.66), channel_id=1, source_target_pairs={{0,1},{1,0},{2,3},{3,2},{4,5},{5,4},{6,7},{7,6},{8,9},{9,8},{10,11... | collective-permute-start | bytes 129032 | tf_op jit(solution)/shard_map/ppermute | solution.py:618
  38.7 6.1 %collective-permute-done.6.lat = bf16[112,192]{1,0:T(8,128)(2,1)S(1)} collective-permute-done((bf16[112,192]{1,0:T(8,128)(2,1)S(1)}, bf16[112,192]{1,0:T(8,128)(2,1)S(1)}, u32[]{:S(2)}, u32[]{:S(2)}) %collective-permute-start.6) | collective-permute-done | bytes 43040 | tf_op jit(solution)/shard_map/ppermute | solution.py:618
  45.1 5.2 %backward_one.1 = (bf16[9,2,3456]{2,1,0:T(2,128)(2,1)S(1)}, bf16[3,2,5760]{2,1,0:T(2,128)(2,1)S(1)}, bf16[15,2,1152]{2,1,0:T(2,128)(2,1)S(1)}, bf16[3,2,3456]{2,...) custom-call(bf16[336,192]{1,0:T(8,128)(2,1)S(1)} %get-tuple-element.65.main, ...), custom_call_target="tpu_custom_call" | custom-call | tf_op jit(solution)/shard_map/backward_one/pallas_call | solution.py:955
  51.8 1.1 collective-permute-start.20
  53.1 4.8 %collective-permute-start.17 = (bf16[72,384]{1,0:T(8,128)(2,1)S(1)}, bf16[72,384]{1,0:T(8,128)(2,1)S(1)}, u32[]{:S(2)}, u32[]{:S(2)}) collective-permute-start(bf16[72,384]{1,0:T(8,128)(2,1)S(1)} %get-tuple-element.90), channel_id=1, source_target_pairs={{0,16},{1,17},{2,18},{3,19},{4,20},{5,21},{6,22},{7,23},{8,24},{9,... | collective-permute-start | bytes 165896 | tf_op jit(solution)/shard_map/ppermute | solution.py:681
  57.9 2.7 %collective-permute-start.21 = (bf16[48,384]{1,0:T(8,128)(2,1)S(1)}, bf16[48,384]{1,0:T(8,128)(2,1)S(1)}, u32[]{:S(2)}, u32[]{:S(2)}) collective-permute-start(bf16[48,384]{1,0:T(8,128)(2,1)S(1)} %get-tuple-element.96), channel_id=1, source_target_pairs={{0,4},{1,5},{2,6},{3,7},{4,0},{5,1},{6,2},{7,3},{8,12},{9,13},{10,... | collective-permute-start | bytes 110600 | tf_op jit(solution)/shard_map/ppermute | solution.py:681
  61.0 1.6 %collective-permute-done.21.refs_6_ = bf16[48,384]{1,0:T(8,128)(2,1)S(1)} collective-permute-done((bf16[48,384]{1,0:T(8,128)(2,1)S(1)}, bf16[48,384]{1,0:T(8,128)(2,1)S(1)}, u32[]{:S(2)}, u32[]{:S(2)}) %collective-permute-start.21) | collective-permute-done | bytes 36896 | tf_op jit(solution)/shard_map/ppermute | solution.py:681
  62.6 2.9 %collective-permute-done.22.refs_7_ = bf16[48,384]{1,0:T(8,128)(2,1)S(1)} collective-permute-done((bf16[48,384]{1,0:T(8,128)(2,1)S(1)}, bf16[48,384]{1,0:T(8,128)(2,1)S(1)}, u32[]{:S(2)}, u32[]{:S(2)}) %collective-permute-start.22) | collective-permute-done | bytes 36896 | tf_op jit(solution)/shard_map/ppermute | solution.py:681
  65.6 1.5 %collective-permute-start.25 = (bf16[120,384]{1,0:T(8,128)(2,1)S(1)}, bf16[120,384]{1,0:T(8,128)(2,1)S(1)}, u32[]{:S(2)}, u32[]{:S(2)}) collective-permute-start(bf16[120,384]{1,0:T(8,128)(2,1)S(1)} %message.1.refs_0_), channel_id=1, source_target_pairs={{0,24},{1,25},{2,26},{3,27},{4,28},{5,29},{6,30},{7,31},{8,0},{9,1... | collective-permute-start | bytes 276488 | tf_op jit(solution)/shard_map/ppermute | solution.py:681
  67.1 2.0 %collective-permute-start.24 = (bf16[120,384]{1,0:T(8,128)(2,1)S(1)}, bf16[120,384]{1,0:T(8,128)(2,1)S(1)}, u32[]{:S(2)}, u32[]{:S(2)}) collective-permute-start(bf16[120,384]{1,0:T(8,128)(2,1)S(1)} %message.1.refs_0_), channel_id=1, source_target_pairs={{0,16},{1,17},{2,18},{3,19},{4,20},{5,21},{6,22},{7,23},{8,24},{9,... | collective-permute-start | bytes 276488 | tf_op jit(solution)/shard_map/ppermute | solution.py:681
  69.2 2.4 %collective-permute-done.25.refs_3_ = bf16[120,384]{1,0:T(8,128)(2,1)S(1)} collective-permute-done((bf16[120,384]{1,0:T(8,128)(2,1)S(1)}, bf16[120,384]{1,0:T(8,128)(2,1)S(1)}, u32[]{:S(2)}, u32[]{:S(2)}) %collective-permute-start.25) | collective-permute-done | bytes 92192 | tf_op jit(solution)/shard_map/ppermute | solution.py:681
  71.6 2.9 %collective-permute-done.24.refs_2_ = bf16[120,384]{1,0:T(8,128)(2,1)S(1)} collective-permute-done((bf16[120,384]{1,0:T(8,128)(2,1)S(1)}, bf16[120,384]{1,0:T(8,128)(2,1)S(1)}, u32[]{:S(2)}, u32[]{:S(2)}) %collective-permute-start.24) | collective-permute-done | bytes 92192 | tf_op jit(solution)/shard_map/ppermute | solution.py:681
  76.6 1.5 %collective-permute-start.27 = (bf16[336,384]{1,0:T(8,128)(2,1)S(1)}, bf16[336,384]{1,0:T(8,128)(2,1)S(1)}, u32[]{:S(2)}, u32[]{:S(2)}) collective-permute-start(bf16[336,384]{1,0:T(8,128)(2,1)S(1)} %widen.1.refs_0_), channel_id=1, source_target_pairs={{0,4},{1,5},{2,6},{3,7},{4,0},{5,1},{6,2},{7,3},{8,12},{9,13},{10,... | collective-permute-start | bytes 774152 | tf_op jit(solution)/shard_map/ppermute | solution.py:681
  78.0 1.1 %collective-permute-start.26 = (bf16[336,384]{1,0:T(8,128)(2,1)S(1)}, bf16[336,384]{1,0:T(8,128)(2,1)S(1)}, u32[]{:S(2)}, u32[]{:S(2)}) collective-permute-start(bf16[336,384]{1,0:T(8,128)(2,1)S(1)} %widen.1.refs_0_), channel_id=1, source_target_pairs={{0,1},{1,0},{2,3},{3,2},{4,5},{5,4},{6,7},{7,6},{8,9},{9,8},{10,11... | collective-permute-start | bytes 774152 | tf_op jit(solution)/shard_map/ppermute | solution.py:681
  79.1 5.3 %collective-permute-done.28.refs_3_ = bf16[336,384]{1,0:T(8,128)(2,1)S(1)} collective-permute-done((bf16[336,384]{1,0:T(8,128)(2,1)S(1)}, bf16[336,384]{1,0:T(8,128)(2,1)S(1)}, u32[]{:S(2)}, u32[]{:S(2)}) %collective-permute-start.28) | collective-permute-done | bytes 258080 | tf_op jit(solution)/shard_map/ppermute | solution.py:681
  84.5 2.2 %collective-permute-done.27.refs_2_ = bf16[336,384]{1,0:T(8,128)(2,1)S(1)} collective-permute-done((bf16[336,384]{1,0:T(8,128)(2,1)S(1)}, bf16[336,384]{1,0:T(8,128)(2,1)S(1)}, u32[]{:S(2)}, u32[]{:S(2)}) %collective-permute-start.27) | collective-permute-done | bytes 258080 | tf_op jit(solution)/shard_map/ppermute | solution.py:681
  88.2 6.1 %collective-permute-done.11.diag = bf16[3,2,3456]{2,1,0:T(2,128)(2,1)S(1)} collective-permute-done((bf16[3,2,3456]{2,1,0:T(2,128)(2,1)S(1)}, bf16[3,2,3456]{2,1,0:T(2,128)(2,1)S(1)}, u32[]{:S(2)}, u32[]{:S(2)}) %collective-permute-start.11) | collective-permute-done | bytes 41504 | tf_op jit(solution)/shard_map/ppermute | solution.py:618
  95.4 3.3 %collective-permute-done.9.lat = bf16[3,2,5760]{2,1,0:T(2,128)(2,1)S(1)} collective-permute-done((bf16[3,2,5760]{2,1,0:T(2,128)(2,1)S(1)}, bf16[3,2,5760]{2,1,0:T(2,128)(2,1)S(1)}, u32[]{:S(2)}, u32[]{:S(2)}) %collective-permute-start.9) | collective-permute-done | bytes 69152 | tf_op jit(solution)/shard_map/ppermute | solution.py:618
  98.7 6.4 %collective-permute-done.10.lon = bf16[15,2,1152]{2,1,0:T(2,128)(2,1)S(1)} collective-permute-done((bf16[15,2,1152]{2,1,0:T(2,128)(2,1)S(1)}, bf16[15,2,1152]{2,1,0:T(2,128)(2,1)S(1)}, u32[]{:S(2)}, u32[]{:S(2)}) %collective-permute-start.10) | collective-permute-done | bytes 69152 | tf_op jit(solution)/shard_map/ppermute | solution.py:618
  105.8 2.1 %finish.1 = (bf16[192,576]{1,0:T(8,128)(2,1)}, bf16[192,192]{1,0:T(8,128)(2,1)}, bf16[768,384]{1,0:T(8,128)(2,1)}, bf16[384,1152]{1,0:T(8,128)(2,1)}, bf16[384,384]{1,0:T(8,128)(2,1)}) custom-call(bf16[336,384]{1,0:T(8,128)(2,1)S(1)} %widen.1.refs_0_, bf16[336,384]{1,0:T(8,128)(2,1)S(1)} %collective-permute-done.26.refs_1_, ...), custom_call_target="tpu_custom_call" | custom-call | tf_op jit(solution)/shard_map/finish/pallas_call | solution.py:1003
  (70 shorter events, 11.7 us)
Async XLA Ops:
  1.6 11.9 %collective-permute-start = (bf16[3,2,5760]{2,1,0:T(2,128)(2,1)S(1)}, bf16[3,2,5760]{2,1,0:T(2,128)(2,1)S(1)}, u32[]{:S(2)}, u32[]{:S(2)}) collective-permute-start(bf16[3,2,5760]{2,1,0:T(2,128)(2,1)S(1)} %get-tuple-element.55), channel_id=1, source_target_pairs={{0,1},{1,0},{2,3},{3,2},{4,5},{5,4},{6,7},{7,6},{8,9},{9,8},{10,11... | collective-permute-start | bytes 207368 | tf_op jit(solution)/shard_map/ppermute | solution.py:618
  4.7 8.8 %collective-permute-start.1 = (bf16[15,2,1152]{2,1,0:T(2,128)(2,1)S(1)}, bf16[15,2,1152]{2,1,0:T(2,128)(2,1)S(1)}, u32[]{:S(2)}, u32[]{:S(2)}) collective-permute-start(bf16[15,2,1152]{2,1,0:T(2,128)(2,1)S(1)} %get-tuple-element.56), channel_id=1, source_target_pairs={{0,30},{1,31},{2,0},{3,1},{4,2},{5,3},{6,4},{7,5},{8,6},{9,7},{10,... | collective-permute-start | bytes 207368 | tf_op jit(solution)/shard_map/ppermute | solution.py:618
  8.4 5.1 %collective-permute-start.2 = (bf16[3,2,3456]{2,1,0:T(2,128)(2,1)S(1)}, bf16[3,2,3456]{2,1,0:T(2,128)(2,1)S(1)}, u32[]{:S(2)}, u32[]{:S(2)}) collective-permute-start(bf16[3,2,3456]{2,1,0:T(2,128)(2,1)S(1)} %get-tuple-element.57), channel_id=1, source_target_pairs={{0,31},{1,30},{2,1},{3,0},{4,3},{5,2},{6,5},{7,4},{8,7},{9,6},{10,... | collective-permute-start | bytes 124424 | tf_op jit(solution)/shard_map/ppermute | solution.py:618
  17.0 6.7 %collective-permute-start.3 = (bf16[112,192]{1,0:T(8,128)(2,1)S(1)}, bf16[112,192]{1,0:T(8,128)(2,1)S(1)}, u32[]{:S(2)}, u32[]{:S(2)}) collective-permute-start(bf16[112,192]{1,0:T(8,128)(2,1)S(1)} %get-tuple-element.60), channel_id=1, source_target_pairs={{0,1},{1,0},{2,3},{3,2},{4,5},{5,4},{6,7},{7,6},{8,9},{9,8},{10,11... | collective-permute-start | bytes 129032 | tf_op jit(solution)/shard_map/ppermute | solution.py:618
  18.6 5.1 %collective-permute-start.4 = (bf16[112,192]{1,0:T(8,128)(2,1)S(1)}, bf16[112,192]{1,0:T(8,128)(2,1)S(1)}, u32[]{:S(2)}, u32[]{:S(2)}) collective-permute-start(bf16[112,192]{1,0:T(8,128)(2,1)S(1)} %get-tuple-element.61), channel_id=1, source_target_pairs={{0,30},{1,31},{2,0},{3,1},{4,2},{5,3},{6,4},{7,5},{8,6},{9,7},{10,... | collective-permute-start | bytes 129032 | tf_op jit(solution)/shard_map/ppermute | solution.py:618
  20.2 3.5 %collective-permute-start.5 = (bf16[48,192]{1,0:T(8,128)(2,1)S(1)}, bf16[48,192]{1,0:T(8,128)(2,1)S(1)}, u32[]{:S(2)}, u32[]{:S(2)}) collective-permute-start(bf16[48,192]{1,0:T(8,128)(2,1)S(1)} %get-tuple-element.62), channel_id=1, source_target_pairs={{0,31},{1,30},{2,1},{3,0},{4,3},{5,2},{6,5},{7,4},{8,7},{9,6},{10,... | collective-permute-start | bytes 55304 | tf_op jit(solution)/shard_map/ppermute | solution.py:618
  31.0 2.5 %collective-permute-start.12 = (bf16[1152,384]{1,0:T(8,128)(2,1)S(1)}, bf16[1152,384]{1,0:T(8,128)(2,1)S(1)}, u32[]{:S(2)}, u32[]{:S(2)}) collective-permute-start(bf16[1152,384]{1,0:T(8,128)(2,1)S(1)} %get-tuple-element.83), channel_id=1, source_target_pairs={{0,2},{1,3},{2,0},{3,1},{4,6},{5,7},{6,4},{7,5},{8,10},{9,11},{10,... | collective-permute-start | bytes 2654216 | tf_op jit(solution)/shard_map/ppermute | solution.py:681
  31.1 7.6 %collective-permute-start.8 = (bf16[48,192]{1,0:T(8,128)(2,1)S(1)}, bf16[48,192]{1,0:T(8,128)(2,1)S(1)}, u32[]{:S(2)}, u32[]{:S(2)}) collective-permute-start(bf16[48,192]{1,0:T(8,128)(2,1)S(1)} %get-tuple-element.68), channel_id=1, source_target_pairs={{0,3},{1,2},{2,5},{3,4},{4,7},{5,6},{6,9},{7,8},{8,11},{9,10},{10,... | collective-permute-start | bytes 55304 | tf_op jit(solution)/shard_map/ppermute | solution.py:618
  33.9 19.0 %collective-permute-start.13 = (bf16[288,384]{1,0:T(8,128)(2,1)S(1)}, bf16[288,384]{1,0:T(8,128)(2,1)S(1)}, u32[]{:S(2)}, u32[]{:S(2)}) collective-permute-start(bf16[288,384]{1,0:T(8,128)(2,1)S(1)} %get-tuple-element.85), channel_id=1, source_target_pairs={{0,1},{1,0},{2,3},{3,2},{4,5},{5,4},{6,7},{7,6},{8,9},{9,8},{10,11... | collective-permute-start | bytes 663560 | tf_op jit(solution)/shard_map/ppermute | solution.py:681
  35.2 17.7 %collective-permute-start.14 = (bf16[288,384]{1,0:T(8,128)(2,1)S(1)}, bf16[288,384]{1,0:T(8,128)(2,1)S(1)}, u32[]{:S(2)}, u32[]{:S(2)}) collective-permute-start(bf16[288,384]{1,0:T(8,128)(2,1)S(1)} %get-tuple-element.86), channel_id=1, source_target_pairs={{0,4},{1,5},{2,6},{3,7},{4,0},{5,1},{6,2},{7,3},{8,12},{9,13},{10,... | collective-permute-start | bytes 663560 | tf_op jit(solution)/shard_map/ppermute | solution.py:681
  35.2 17.7 %collective-permute-start.15 = (bf16[288,384]{1,0:T(8,128)(2,1)S(1)}, bf16[288,384]{1,0:T(8,128)(2,1)S(1)}, u32[]{:S(2)}, u32[]{:S(2)}) collective-permute-start(bf16[288,384]{1,0:T(8,128)(2,1)S(1)} %get-tuple-element.87), channel_id=1, source_target_pairs={{0,5},{1,4},{2,7},{3,6},{4,1},{5,0},{6,3},{7,2},{8,13},{9,12},{10,... | collective-permute-start | bytes 663560 | tf_op jit(solution)/shard_map/ppermute | solution.py:681
  37.4 7.4 %collective-permute-start.6 = (bf16[112,192]{1,0:T(8,128)(2,1)S(1)}, bf16[112,192]{1,0:T(8,128)(2,1)S(1)}, u32[]{:S(2)}, u32[]{:S(2)}) collective-permute-start(bf16[112,192]{1,0:T(8,128)(2,1)S(1)} %get-tuple-element.66), channel_id=1, source_target_pairs={{0,1},{1,0},{2,3},{3,2},{4,5},{5,4},{6,7},{7,6},{8,9},{9,8},{10,11... | collective-permute-start | bytes 129032 | tf_op jit(solution)/shard_map/ppermute | solution.py:618
  38.7 6.4 %collective-permute-start.7 = (bf16[112,192]{1,0:T(8,128)(2,1)S(1)}, bf16[112,192]{1,0:T(8,128)(2,1)S(1)}, u32[]{:S(2)}, u32[]{:S(2)}) collective-permute-start(bf16[112,192]{1,0:T(8,128)(2,1)S(1)} %get-tuple-element.67), channel_id=1, source_target_pairs={{0,2},{1,3},{2,4},{3,5},{4,6},{5,7},{6,8},{7,9},{8,10},{9,11},{10,... | collective-permute-start | bytes 129032 | tf_op jit(solution)/shard_map/ppermute | solution.py:618
  51.8 8.8 %collective-permute-start.20 = (bf16[48,384]{1,0:T(8,128)(2,1)S(1)}, bf16[48,384]{1,0:T(8,128)(2,1)S(1)}, u32[]{:S(2)}, u32[]{:S(2)}) collective-permute-start(bf16[48,384]{1,0:T(8,128)(2,1)S(1)} %get-tuple-element.95), channel_id=1, source_target_pairs={{0,1},{1,0},{2,3},{3,2},{4,5},{5,4},{6,7},{7,6},{8,9},{9,8},{10,11... | collective-permute-start | bytes 110600 | tf_op jit(solution)/shard_map/ppermute | solution.py:681
  53.1 12.5 %collective-permute-start.16 = (bf16[72,384]{1,0:T(8,128)(2,1)S(1)}, bf16[72,384]{1,0:T(8,128)(2,1)S(1)}, u32[]{:S(2)}, u32[]{:S(2)}) collective-permute-start(bf16[72,384]{1,0:T(8,128)(2,1)S(1)} %get-tuple-element.89), channel_id=1, source_target_pairs={{0,8},{1,9},{2,10},{3,11},{4,12},{5,13},{6,14},{7,15},{8,16},{9,17... | collective-permute-start | bytes 165896 | tf_op jit(solution)/shard_map/ppermute | solution.py:681
  53.1 12.4 %collective-permute-start.17 = (bf16[72,384]{1,0:T(8,128)(2,1)S(1)}, bf16[72,384]{1,0:T(8,128)(2,1)S(1)}, u32[]{:S(2)}, u32[]{:S(2)}) collective-permute-start(bf16[72,384]{1,0:T(8,128)(2,1)S(1)} %get-tuple-element.90), channel_id=1, source_target_pairs={{0,16},{1,17},{2,18},{3,19},{4,20},{5,21},{6,22},{7,23},{8,24},{9,... | collective-permute-start | bytes 165896 | tf_op jit(solution)/shard_map/ppermute | solution.py:681
  57.9 7.6 %collective-permute-start.18 = (bf16[72,384]{1,0:T(8,128)(2,1)S(1)}, bf16[72,384]{1,0:T(8,128)(2,1)S(1)}, u32[]{:S(2)}, u32[]{:S(2)}) collective-permute-start(bf16[72,384]{1,0:T(8,128)(2,1)S(1)} %get-tuple-element.91), channel_id=1, source_target_pairs={{0,24},{1,25},{2,26},{3,27},{4,28},{5,29},{6,30},{7,31},{8,0},{9,1... | collective-permute-start | bytes 165896 | tf_op jit(solution)/shard_map/ppermute | solution.py:681
  57.9 4.7 %collective-permute-start.21 = (bf16[48,384]{1,0:T(8,128)(2,1)S(1)}, bf16[48,384]{1,0:T(8,128)(2,1)S(1)}, u32[]{:S(2)}, u32[]{:S(2)}) collective-permute-start(bf16[48,384]{1,0:T(8,128)(2,1)S(1)} %get-tuple-element.96), channel_id=1, source_target_pairs={{0,4},{1,5},{2,6},{3,7},{4,0},{5,1},{6,2},{7,3},{8,12},{9,13},{10,... | collective-permute-start | bytes 110600 | tf_op jit(solution)/shard_map/ppermute | solution.py:681
  60.6 4.9 %collective-permute-start.22 = (bf16[48,384]{1,0:T(8,128)(2,1)S(1)}, bf16[48,384]{1,0:T(8,128)(2,1)S(1)}, u32[]{:S(2)}, u32[]{:S(2)}) collective-permute-start(bf16[48,384]{1,0:T(8,128)(2,1)S(1)} %get-tuple-element.97), channel_id=1, source_target_pairs={{0,5},{1,4},{2,7},{3,6},{4,1},{5,0},{6,3},{7,2},{8,13},{9,12},{10,... | collective-permute-start | bytes 110600 | tf_op jit(solution)/shard_map/ppermute | solution.py:681
  65.6 6.0 %collective-permute-start.25 = (bf16[120,384]{1,0:T(8,128)(2,1)S(1)}, bf16[120,384]{1,0:T(8,128)(2,1)S(1)}, u32[]{:S(2)}, u32[]{:S(2)}) collective-permute-start(bf16[120,384]{1,0:T(8,128)(2,1)S(1)} %message.1.refs_0_), channel_id=1, source_target_pairs={{0,24},{1,25},{2,26},{3,27},{4,28},{5,29},{6,30},{7,31},{8,0},{9,1... | collective-permute-start | bytes 276488 | tf_op jit(solution)/shard_map/ppermute | solution.py:681
  67.1 7.5 %collective-permute-start.24 = (bf16[120,384]{1,0:T(8,128)(2,1)S(1)}, bf16[120,384]{1,0:T(8,128)(2,1)S(1)}, u32[]{:S(2)}, u32[]{:S(2)}) collective-permute-start(bf16[120,384]{1,0:T(8,128)(2,1)S(1)} %message.1.refs_0_), channel_id=1, source_target_pairs={{0,16},{1,17},{2,18},{3,19},{4,20},{5,21},{6,22},{7,23},{8,24},{9,... | collective-permute-start | bytes 276488 | tf_op jit(solution)/shard_map/ppermute | solution.py:681
  69.1 6.4 %collective-permute-start.23 = (bf16[120,384]{1,0:T(8,128)(2,1)S(1)}, bf16[120,384]{1,0:T(8,128)(2,1)S(1)}, u32[]{:S(2)}, u32[]{:S(2)}) collective-permute-start(bf16[120,384]{1,0:T(8,128)(2,1)S(1)} %message.1.refs_0_), channel_id=1, source_target_pairs={{0,8},{1,9},{2,10},{3,11},{4,12},{5,13},{6,14},{7,15},{8,16},{9,17... | collective-permute-start | bytes 276488 | tf_op jit(solution)/shard_map/ppermute | solution.py:681
  75.6 8.9 %collective-permute-start.28 = (bf16[336,384]{1,0:T(8,128)(2,1)S(1)}, bf16[336,384]{1,0:T(8,128)(2,1)S(1)}, u32[]{:S(2)}, u32[]{:S(2)}) collective-permute-start(bf16[336,384]{1,0:T(8,128)(2,1)S(1)} %widen.1.refs_0_), channel_id=1, source_target_pairs={{0,5},{1,4},{2,7},{3,6},{4,1},{5,0},{6,3},{7,2},{8,13},{9,12},{10,... | collective-permute-start | bytes 774152 | tf_op jit(solution)/shard_map/ppermute | solution.py:681
  76.6 10.1 %collective-permute-start.27 = (bf16[336,384]{1,0:T(8,128)(2,1)S(1)}, bf16[336,384]{1,0:T(8,128)(2,1)S(1)}, u32[]{:S(2)}, u32[]{:S(2)}) collective-permute-start(bf16[336,384]{1,0:T(8,128)(2,1)S(1)} %widen.1.refs_0_), channel_id=1, source_target_pairs={{0,4},{1,5},{2,6},{3,7},{4,0},{5,1},{6,2},{7,3},{8,12},{9,13},{10,... | collective-permute-start | bytes 774152 | tf_op jit(solution)/shard_map/ppermute | solution.py:681
  78.0 9.1 %collective-permute-start.26 = (bf16[336,384]{1,0:T(8,128)(2,1)S(1)}, bf16[336,384]{1,0:T(8,128)(2,1)S(1)}, u32[]{:S(2)}, u32[]{:S(2)}) collective-permute-start(bf16[336,384]{1,0:T(8,128)(2,1)S(1)} %widen.1.refs_0_), channel_id=1, source_target_pairs={{0,1},{1,0},{2,3},{3,2},{4,5},{5,4},{6,7},{7,6},{8,9},{9,8},{10,11... | collective-permute-start | bytes 774152 | tf_op jit(solution)/shard_map/ppermute | solution.py:681
  79.1 26.7 %collective-permute-start.29 = (bf16[336,384]{1,0:T(8,128)(2,1)S(1)}, bf16[336,384]{1,0:T(8,128)(2,1)S(1)}, u32[]{:S(2)}, u32[]{:S(2)}) collective-permute-start(bf16[336,384]{1,0:T(8,128)(2,1)S(1)} %widen.1.refs_0_), channel_id=1, source_target_pairs={{0,2},{1,3},{2,0},{3,1},{4,6},{5,7},{6,4},{7,5},{8,10},{9,11},{10,... | collective-permute-start | bytes 774152 | tf_op jit(solution)/shard_map/ppermute | solution.py:681
  84.5 21.4 %collective-permute-start.32 = (bf16[336,384]{1,0:T(8,128)(2,1)S(1)}, bf16[336,384]{1,0:T(8,128)(2,1)S(1)}, u32[]{:S(2)}, u32[]{:S(2)}) collective-permute-start(bf16[336,384]{1,0:T(8,128)(2,1)S(1)} %collective-permute-done.28.refs_3_), channel_id=1, source_target_pairs={{0,2},{1,3},{2,0},{3,1},{4,6},{5,7},{6,4},{7,5},{8,10},{9,11},{10,... | collective-permute-start | bytes 774152 | tf_op jit(solution)/shard_map/ppermute | solution.py:681
  86.7 19.1 %collective-permute-start.31 = (bf16[336,384]{1,0:T(8,128)(2,1)S(1)}, bf16[336,384]{1,0:T(8,128)(2,1)S(1)}, u32[]{:S(2)}, u32[]{:S(2)}) collective-permute-start(bf16[336,384]{1,0:T(8,128)(2,1)S(1)} %collective-permute-done.27.refs_2_), channel_id=1, source_target_pairs={{0,2},{1,3},{2,0},{3,1},{4,6},{5,7},{6,4},{7,5},{8,10},{9,11},{10,... | collective-permute-start | bytes 774152 | tf_op jit(solution)/shard_map/ppermute | solution.py:681
  87.1 18.7 %collective-permute-start.30 = (bf16[336,384]{1,0:T(8,128)(2,1)S(1)}, bf16[336,384]{1,0:T(8,128)(2,1)S(1)}, u32[]{:S(2)}, u32[]{:S(2)}) collective-permute-start(bf16[336,384]{1,0:T(8,128)(2,1)S(1)} %collective-permute-done.26.refs_1_), channel_id=1, source_target_pairs={{0,2},{1,3},{2,0},{3,1},{4,6},{5,7},{6,4},{7,5},{8,10},{9,11},{10,... | collective-permute-start | bytes 774152 | tf_op jit(solution)/shard_map/ppermute | solution.py:681
  87.2 7.1 %collective-permute-start.11 = (bf16[3,2,3456]{2,1,0:T(2,128)(2,1)S(1)}, bf16[3,2,3456]{2,1,0:T(2,128)(2,1)S(1)}, u32[]{:S(2)}, u32[]{:S(2)}) collective-permute-start(bf16[3,2,3456]{2,1,0:T(2,128)(2,1)S(1)} %get-tuple-element.79), channel_id=1, source_target_pairs={{0,3},{1,2},{2,5},{3,4},{4,7},{5,6},{6,9},{7,8},{8,11},{9,10},{10,... | collective-permute-start | bytes 124424 | tf_op jit(solution)/shard_map/ppermute | solution.py:618
  94.3 4.3 %collective-permute-start.9 = (bf16[3,2,5760]{2,1,0:T(2,128)(2,1)S(1)}, bf16[3,2,5760]{2,1,0:T(2,128)(2,1)S(1)}, u32[]{:S(2)}, u32[]{:S(2)}) collective-permute-start(bf16[3,2,5760]{2,1,0:T(2,128)(2,1)S(1)} %get-tuple-element.77), channel_id=1, source_target_pairs={{0,1},{1,0},{2,3},{3,2},{4,5},{5,4},{6,7},{7,6},{8,9},{9,8},{10,11... | collective-permute-start | bytes 207368 | tf_op jit(solution)/shard_map/ppermute | solution.py:618
  98.6 6.4 %collective-permute-start.10 = (bf16[15,2,1152]{2,1,0:T(2,128)(2,1)S(1)}, bf16[15,2,1152]{2,1,0:T(2,128)(2,1)S(1)}, u32[]{:S(2)}, u32[]{:S(2)}) collective-permute-start(bf16[15,2,1152]{2,1,0:T(2,128)(2,1)S(1)} %get-tuple-element.78), channel_id=1, source_target_pairs={{0,2},{1,3},{2,4},{3,5},{4,6},{5,7},{6,8},{7,9},{8,10},{9,11},{10,... | collective-permute-start | bytes 207368 | tf_op jit(solution)/shard_map/ppermute | solution.py:618
  (13 other events, 128.3 us)

commit v4 on v3

--- a/solution.py
+++ b/solution.py
@@ -388,12 +388,26 @@
         start += out.shape[0]
 
 
+def cotangent_kernel(main, lat, lon, diag, w_proj, index, d_block, d_att, lace_ref, *, thin, cols, column):
+    channels = w_proj.shape[0]
+    tokens = d_block.shape[0]
+    lace_rows = lace_ref.shape[0]
+    lace_ref[...] = jnp.zeros(lace_ref.shape, f32)
+    unlace_two(main, lat, lon, diag, lace_ref, HALF_LON * thin)
+    stack = jnp.concatenate(
+        [lace_ref[:, channels * k : channels * (k + 1)] for k in range(cols)], axis=0
+    ).astype(bf16)
+    rolled = mm(one_hot(index, column, tokens, lace_rows * cols), stack).astype(bf16)
+    d_block[...] = rolled
+    d_att[...] = mm_nt(rolled, w_proj[...]).astype(bf16).astype(f32)
+
+
 def merge_two_kernel(
-    main, lat, lon, diag, cot_main, cot_lat, cot_lon, cot_diag, bias,
+    main, lat, lon, diag, d_block_in, d_att_in, bias,
     gain_merge, gain_two, w_merge, w_qkv, w_proj, index,
-    res_main, res_lat, res_lon, res_diag, d_main, d_lat, d_lon, d_diag, sums_keep, sums_send,
-    lace_ref, probs_ref, packed_ref, att_ref, d_packed_ref, sums_ref,
-    *, cols, columns,
+    out_block, d_main, d_lat, d_lon, d_diag, sums_keep, sums_send,
+    probs_ref, packed_ref, att_ref, d_packed_ref, sums_ref,
+    *, columns,
 ):
     channels = gain_two.shape[0]
     thin = main.shape[1]
@@ -429,23 +443,13 @@
     )
     attended = att_ref[...].astype(bf16)
     block = (merged + mm(attended, w_proj[...])).astype(bf16)
-    lace_rows = lace_ref.shape[0]
-    lattice = mm(one_hot(index, columns[1], lace_rows * cols, tokens), block)
-    for k in range(cols):
-        lace_ref[:, channels * k : channels * (k + 1)] = lattice[lace_rows * k : lace_rows * (k + 1)]
-    lace_out(lace_ref, res_main, res_lat, res_lon, res_diag, HALF_LAT, HALF_LON * channels)
-    lace_ref[...] = jnp.zeros(lace_ref.shape, f32)
-    unlace_two(cot_main, cot_lat, cot_lon, cot_diag, lace_ref, HALF_LON * thin)
-    cot_stack = jnp.concatenate(
-        [lace_ref[:, channels * k : channels * (k + 1)] for k in range(cols)], axis=0
-    ).astype(bf16)
-    d_block = mm(one_hot(index, columns[2], tokens, lace_rows * cols), cot_stack)
-    d_block_low = d_block.astype(bf16)
+    out_block[...] = block
+    d_block_low = d_block_in[...]
+    d_block = d_block_low.astype(f32)
     at_sum = groups * thin
     sums_ref[at_sum : at_sum + channels, :] = mm_tn(attended, d_block_low)
-    att_ref[...] = mm_nt(d_block_low, w_proj[...]).astype(bf16).astype(f32)
     attention_back(
-        packed_ref, att_ref, d_packed_ref, lambda k: probs_ref[k[0], k[1], 0:SPOTS], jobs, channels, BATCH[2]
+        packed_ref, d_att_in, d_packed_ref, lambda k: probs_ref[k[0], k[1], 0:SPOTS], jobs, channels, BATCH[2]
     )
     d_packed = d_packed_ref[...].astype(bf16)
     at_sum += channels
@@ -466,7 +470,7 @@
     d_group = jnp.concatenate(
         [scale_merge * (d_hats[g] - first - hats[g] * cross) for g in range(groups)], axis=0
     ).astype(bf16)
-    parts = mm(one_hot(index, columns[3], total, groups * tokens), d_group).astype(bf16)
+    parts = mm(one_hot(index, columns[1], total, groups * tokens), d_group).astype(bf16)
     start = 0
     for out in (d_main, d_lat, d_lon, d_diag):
         out[...] = parts[start : start + out.shape[0]]
@@ -546,10 +550,10 @@
 
 
 def backward_one_kernel(
-    main, lat, lon, diag, keep_x, keep_packed, keep_probs, keep_att, res_lat, res_lon, res_diag,
+    main, lat, lon, diag, keep_x, keep_packed, keep_probs, keep_att, block_two,
     gain, w_qkv, w_proj, index,
-    out_main, out_lat, out_lon, out_diag, sums_keep, sums_send,
-    lace_ref, packed_ref, att_ref, d_packed_ref, sums_ref,
+    res_main, out_main, out_lat, out_lon, out_diag, sums_keep, sums_send,
+    lace_ref, packed_ref, att_ref, d_packed_ref, sums_ref, lace_two_ref,
     *, cols, columns,
 ):
     channels = gain.shape[0]
@@ -582,12 +586,28 @@
         lace_ref, out_main, out_lat.at[:, :, 0:kept], out_lon.at[0:low], out_diag.at[:, :, 0:lane1],
         HALF_LAT, lane1,
     )
-    out_lat[:, :, kept:] = res_lat[...]
-    out_diag[:, :, lane1:] = res_diag[...]
-    count = res_lon.shape[0]
-    for n in range(2):
-        at = low + n * count
-        out_lon[at : at + count] = res_lon[:, :, n * lane1 : (n + 1) * lane1]
+    wide = block_two.shape[1]
+    wide_rows = lace_two_ref.shape[0]
+    wide_cols = lace_two_ref.shape[1] // wide
+    lattice = mm(
+        one_hot(index, columns[2], wide_rows * wide_cols, block_two.shape[0]), block_two[...]
+    )
+    for k in range(wide_cols):
+        lace_two_ref[:, wide * k : wide * (k + 1)] = lattice[wide_rows * k : wide_rows * (k + 1)]
+    kept_two = res_main.shape[2]
+    lanes = lace_two_ref.shape[1]
+    count = res_main.shape[0]
+    for j in range(count):
+        row = lace_two_ref[2 * j : 2 * j + 2, :].astype(bf16)
+        res_main[j] = row[:, 0:kept_two]
+        for n in range(2):
+            at = kept_two + n * lane1
+            out_lon[low + n * count + j] = row[:, at : at + lane1]
+    for n in range(HALF_LAT):
+        at = 2 * (count + n)
+        row = lace_two_ref[at : at + 2, :].astype(bf16)
+        out_lat[n, :, kept : kept + kept_two] = row[:, 0:kept_two]
+        out_diag[n, :, lane1 : lane1 + lanes - kept_two] = row[:, kept_two:lanes]
     mine = core_of()
     half = 2 * channels
     low = sums_ref[:, 0:half].astype(bf16)
@@ -656,10 +676,10 @@
 
     def wide(i, j, d):
         z = i // 2 // near_lon
-        return ((z + d) % far_lon) * 2 * near_lon + i % (2 * near_lon), j
+        return target(z, d, far_lon) * 2 * near_lon + i % (2 * near_lon), j
 
     def high(i, j, d):
-        return i, ((j // near_lat + d) % far_lat) * near_lat + j % near_lat
+        return i, target(j // near_lat, d, far_lat) * near_lat + j % near_lat
 
     lon_at, lat_at = lax.axis_index("lon"), lax.axis_index("lat")
     near_at = (lon_at // 2 % near_lon) * near_lat + lat_at % near_lat
@@ -685,8 +705,16 @@
     return hop(values, lambda i, j, d: (i ^ 1, j), 1)
 
 
-def target(stage, at, d, size):
-    return at ^ d if stage == 0 else (at + d) % size
+def near_target(at, d, size):
+    return at ^ d
+
+
+def target(at, d, size):
+    return (at + d) % size
+
+
+def source(at, d, size):
+    return lax.rem(at - d + size, size)
 
 
 def total_of(refs, rows):
@@ -703,7 +731,7 @@
     for p in range(size):
         scratch[p] = total_of(refs[:count], slice(p * rows, (p + 1) * rows))
     for d in range(size):
-        outs[d][...] = scratch[target(stage, at, d, size)].astype(bf16)
+        outs[d][...] = scratch[(near_target if stage == 0 else target)(at, d, size)].astype(bf16)
 
 
 def sum_split(values, stage):
@@ -779,7 +807,7 @@
     width = 1
     for n in range(len(stage_sizes) - 1, 0, -1):
         count = stage_sizes[n]
-        places = [lax.rem(spots[n] - d + count, count) * width + p for d in range(count) for p in places]
+        places = [source(spots[n], d, count) * width + p for d in range(count) for p in places]
         width *= count
     for d in range(near):
         place = spots[0] ^ d
@@ -889,13 +917,6 @@
     def part_shapes(dtype=bf16):
         return [jax.ShapeDtypeStruct((n, c1), dtype) for n in sizes_parts]
 
-    def lace_shapes(rows, cols, channels):
-        kr, kl, cl = rows - HALF_LAT, (cols - HALF_LON) * channels, HALF_LON * channels
-        return [
-            jax.ShapeDtypeStruct((r, LEVELS, n), bf16)
-            for r, n in ((kr, kl), (HALF_LAT, kl), (kr, cl), (HALF_LAT, cl))
-        ]
-
     count1 = LEVELS * rows1 * cols1
     units1 = count1 // SPOTS
     fwd = pl.pallas_call(
@@ -924,28 +945,36 @@
 
     tokens2 = LEVELS * SPOTS
     total_two = 4 * c1 + 4 * c2
+    d_block_two = pl.pallas_call(
+        functools.partial(cotangent_kernel, thin=c1, cols=cols2, column=4),
+        name="cot",
+        in_specs=[vmem] * 6,
+        out_specs=[vmem] * 2,
+        out_shape=[pltpu.VMEM((tokens2, c2), bf16), pltpu.VMEM((tokens2, c2), f32)],
+        scratch_shapes=[pltpu.VMEM((lace2_pad, cols2 * c2), f32)],
+        compiler_params=LIMIT,
+    )(*near_in(cot, *halos, proj_two, index))
     two = pl.pallas_call(
-        functools.partial(merge_two_kernel, cols=cols2, columns=(2, 3, 4, 5)),
+        functools.partial(merge_two_kernel, columns=(2, 5)),
         name="merge_two",
-        in_specs=[vmem] * 15,
-        out_specs=[vmem] * 10,
+        in_specs=[vmem] * 13,
+        out_specs=[vmem] * 7,
         out_shape=near_out(
-            lace_shapes(rows2, cols2, c2)
+            [jax.ShapeDtypeStruct((tokens2, c2), bf16)]
             + part_shapes()
             + [jax.ShapeDtypeStruct((total_two // 2, c2), bf16)] * 2
         ),
         compiler_params=LIMIT_TWO,
         scratch_shapes=[
-            pltpu.VMEM((lace2_pad, cols2 * c2), f32),
             pltpu.VMEM((LEVELS, HEADS2 * SPOTS, 128), f32),
             pltpu.VMEM((tokens2, 3 * c2), f32),
             pltpu.VMEM((tokens2, c2), f32),
             pltpu.VMEM((tokens2, 3 * c2), f32),
             pltpu.VMEM((total_two, c2), f32),
         ],
-    )(*near_in(parts[0], *got, cot, *halos, bias_two, gain_merge, gain_two,
+    )(*near_in(parts[0], *got, *d_block_two, bias_two, gain_merge, gain_two,
                 merge_weight, qkv_two, proj_two, index))
-    res, d_parts, sums_two = two[:4], two[4:8], two[8:]
+    block_two, d_parts, sums_two = two[0], two[1:5], two[5:]
     d_got = exchange(*d_parts[1:], 1)
     two_parts = [sums_two[0], pair(sums_two[1])]
     for n in range(len(stages)):
@@ -953,12 +982,13 @@
 
     lanes1, lane1 = tokens.shape[2], HALF_LON * c1
     one = pl.pallas_call(
-        functools.partial(backward_one_kernel, cols=cols1, columns=(6, 7)),
+        functools.partial(backward_one_kernel, cols=cols1, columns=(6, 7, 3)),
         name="backward_one",
-        in_specs=[vmem] * 15,
-        out_specs=[vmem] * 6,
+        in_specs=[vmem] * 13,
+        out_specs=[vmem] * 7,
         out_shape=near_out(
             [
+                jax.ShapeDtypeStruct((rows2 - HALF_LAT, LEVELS, lanes1 - 2 * lane1), bf16),
                 jax.ShapeDtypeStruct((rows1 - HALF_LAT, LEVELS, lanes1 - lane1), bf16),
                 *(jax.ShapeDtypeStruct(h.shape, bf16) for h in halos),
             ]
@@ -971,9 +1001,10 @@
             pltpu.VMEM((count1, c1), f32),
             pltpu.VMEM((count1, 3 * c1), f32),
             pltpu.VMEM((c1, 4 * c1), f32),
+            pltpu.VMEM((lace2_pad, cols2 * c2), f32),
         ],
-    )(*near_in(d_parts[0], *d_got, *kept, *res[1:], gain_one, qkv_one, proj_one, index))
-    d_tok, sums_one = one[:4], one[4:]
+    )(*near_in(d_parts[0], *d_got, *kept, block_two, gain_one, qkv_one, proj_one, index))
+    res_main, d_tok, sums_one = one[0], one[1:5], one[5:]
     one_parts = [sums_one[0], pair(sums_one[1])]
     one_parts = moves(sum_split(one_parts, 0), 0)
     message = message_of(two_parts, one_parts)
@@ -993,7 +1024,7 @@
             jax.ShapeDtypeStruct((rows1, LEVELS, lanes1), bf16),
         ],
         compiler_params=LIMIT,
-    )(*near_in(res[0], d_tok[0], *back))
+    )(*near_in(res_main, d_tok[0], *back))
     result, d_tokens = (v.transpose(1, 0, 2) for v in joined)
 
     near = stages[0][0]

time: 108 us -> 107 us (level)
    pallas_call x1 -> x2, Pallas kernels: 7.26 us -> 6.88 us  [the longest x1 6.43 us: shards(): pl.pallas_call(functools.partial(merge_two_kernel, columns=(2, 5)), name=...]
where the time goes in v4:
time: 107 us
  waiting for transfers between devices  45.1 us (42%)
  starting transfers between devices  36.9 us (34%)
  Pallas kernels  22.9 us (21%)
  between operations  1.6 us (1%)
    ppermute x12, waiting for transfers between devices, send(): return lax.ppermute(values, AXES, route)  24.3 us
    ppermute x21, waiting for transfers between devices, hop(): return lax.ppermute(values, AXES, route)  20.9 us
    ppermute x21, starting transfers between devices, hop(): return lax.ppermute(values, AXES, route)  20.3 us
    ppermute x12, starting transfers between devices, send(): return lax.ppermute(values, AXES, route)  16.6 us
    pallas_call x1, Pallas kernels, shards(): pl.pallas_call(functools.partial(merge_two_kernel, columns=(2, 5)), name=...  6.43 us
    pallas_call x1, Pallas kernels, shards(): pl.pallas_call(functools.partial(backward_one_kernel, cols=cols1, columns...  5.32 us
    pallas_call x1, Pallas kernels, shards(): pl.pallas_call(functools.partial(forward_one_kernel, cols=cols1, columns=...  3.47 us
    pallas_call x1, Pallas kernels, bias_call(): pl.pallas_call(expand_bias, name='bias', in_specs=[smem, smem, vmem, vmem...  2.8 us
  transfers between devices with their start and end apart: 33, of which 16 were waited for; matrix products, arithmetic and copies ran while one was open for 0% of the time, Pallas kernels for 9%

profile of v4, /device:TPU:0, one launch (start us, length us, event | category | flops | bytes accessed | tf_op | source)
XLA Modules:
  0.0 107.2 jit_solution(321713109982702123)
XLA Ops:
  1.6 3.1 %collective-permute-start = (bf16[3,2,5760]{2,1,0:T(2,128)(2,1)S(1)}, bf16[3,2,5760]{2,1,0:T(2,128)(2,1)S(1)}, u32[]{:S(2)}, u32[]{:S(2)}) collective-permute-start(bf16[3,2,5760]{2,1,0:T(2,128)(2,1)S(1)} %get-tuple-element.55), channel_id=1, source_target_pairs={{0,1},{1,0},{2,3},{3,2},{4,5},{5,4},{6,7},{7,6},{8,9},{9,8},{10,11... | collective-permute-start | bytes 207368 | tf_op jit(solution)/shard_map/ppermute | solution.py:638
  4.7 3.7 %collective-permute-start.1 = (bf16[15,2,1152]{2,1,0:T(2,128)(2,1)S(1)}, bf16[15,2,1152]{2,1,0:T(2,128)(2,1)S(1)}, u32[]{:S(2)}, u32[]{:S(2)}) collective-permute-start(bf16[15,2,1152]{2,1,0:T(2,128)(2,1)S(1)} %get-tuple-element.56), channel_id=1, source_target_pairs={{0,30},{1,31},{2,0},{3,1},{4,2},{5,3},{6,4},{7,5},{8,6},{9,7},{10,... | collective-permute-start | bytes 207368 | tf_op jit(solution)/shard_map/ppermute | solution.py:638
  10.6 2.8 %bias.1 = (f32[4,432,128]{2,1,0:T(8,128)S(1)}, f32[2,864,128]{2,1,0:T(8,128)S(1)}) custom-call(s32[1,2]{1,0:T(1,128)S(1)} %copy-done.11, s32[1,1]{1,0:T(1,128)S(6)} %copy.23.kinds_two, f32[6,8,3312]{2,1,0:T(8,128)} %bitcast.11, f32[12,8,3312]{2,1,0:T(8,128)} %bitcast.10, s32[8,1536]{1,0:T(8,128)} %constant.5.clone.target), custom_call_target="tpu_custom_call" | custom-call | tf_op jit(solution)/shard_map/bias/pallas_call | solution.py:250
  13.6 3.5 %forward_one.1 = (bf16[336,192]{1,0:T(8,128)(2,1)S(1)}, bf16[112,192]{1,0:T(8,128)(2,1)S(1)}, bf16[112,192]{1,0:T(8,128)(2,1)S(1)}, bf16[48,192]{1,0:T(8,128)(2,...) custom-call(bf16[12,2,4608]{2,1,0:T(2,128)(2,1)S(1)} %bitcast.7, ...), custom_call_target="tpu_custom_call" | custom-call | tf_op jit(solution)/shard_map/forward_one/pallas_call | solution.py:922
  17.0 1.6 %collective-permute-start.3 = (bf16[112,192]{1,0:T(8,128)(2,1)S(1)}, bf16[112,192]{1,0:T(8,128)(2,1)S(1)}, u32[]{:S(2)}, u32[]{:S(2)}) collective-permute-start(bf16[112,192]{1,0:T(8,128)(2,1)S(1)} %get-tuple-element.60), channel_id=1, source_target_pairs={{0,1},{1,0},{2,3},{3,2},{4,5},{5,4},{6,7},{7,6},{8,9},{9,8},{10,11... | collective-permute-start | bytes 129032 | tf_op jit(solution)/shard_map/ppermute | solution.py:638
  18.6 1.6 %collective-permute-start.4 = (bf16[112,192]{1,0:T(8,128)(2,1)S(1)}, bf16[112,192]{1,0:T(8,128)(2,1)S(1)}, u32[]{:S(2)}, u32[]{:S(2)}) collective-permute-start(bf16[112,192]{1,0:T(8,128)(2,1)S(1)} %get-tuple-element.61), channel_id=1, source_target_pairs={{0,30},{1,31},{2,0},{3,1},{4,2},{5,3},{6,4},{7,5},{8,6},{9,7},{10,... | collective-permute-start | bytes 129032 | tf_op jit(solution)/shard_map/ppermute | solution.py:638
  21.7 2.1 %collective-permute-done.5.diag = bf16[48,192]{1,0:T(8,128)(2,1)S(1)} collective-permute-done((bf16[48,192]{1,0:T(8,128)(2,1)S(1)}, bf16[48,192]{1,0:T(8,128)(2,1)S(1)}, u32[]{:S(2)}, u32[]{:S(2)}) %collective-permute-start.5) | collective-permute-done | bytes 18464 | tf_op jit(solution)/shard_map/ppermute | solution.py:638
  23.8 6.4 %merge_two.1 = (bf16[144,384]{1,0:T(8,128)(2,1)S(1)}, bf16[336,192]{1,0:T(8,128)(2,1)S(1)}, bf16[112,192]{1,0:T(8,128)(2,1)S(1)}, bf16[112,192]{1,0:T(8,128)(2,1...) custom-call(bf16[336,192]{1,0:T(8,128)(2,1)S(1)} %get-tuple-element.59.main, ...), custom_call_target="tpu_custom_call" | custom-call | tf_op jit(solution)/shard_map/merge_two/pallas_call | solution.py:957
  30.3 1.4 %collective-permute-start.8 = (bf16[48,192]{1,0:T(8,128)(2,1)S(1)}, bf16[48,192]{1,0:T(8,128)(2,1)S(1)}, u32[]{:S(2)}, u32[]{:S(2)}) collective-permute-start(bf16[48,192]{1,0:T(8,128)(2,1)S(1)} %get-tuple-element.69), channel_id=1, source_target_pairs={{0,3},{1,2},{2,5},{3,4},{4,7},{5,6},{6,9},{7,8},{8,11},{9,10},{10,... | collective-permute-start | bytes 55304 | tf_op jit(solution)/shard_map/ppermute | solution.py:638
  33.0 1.4 %collective-permute-start.13 = (bf16[288,384]{1,0:T(8,128)(2,1)S(1)}, bf16[288,384]{1,0:T(8,128)(2,1)S(1)}, u32[]{:S(2)}, u32[]{:S(2)}) collective-permute-start(bf16[288,384]{1,0:T(8,128)(2,1)S(1)} %get-tuple-element.85), channel_id=1, source_target_pairs={{0,1},{1,0},{2,3},{3,2},{4,5},{5,4},{6,7},{7,6},{8,9},{9,8},{10,11... | collective-permute-start | bytes 663560 | tf_op jit(solution)/shard_map/ppermute | solution.py:701
  34.4 2.2 %collective-permute-start.15 = (bf16[288,384]{1,0:T(8,128)(2,1)S(1)}, bf16[288,384]{1,0:T(8,128)(2,1)S(1)}, u32[]{:S(2)}, u32[]{:S(2)}) collective-permute-start(bf16[288,384]{1,0:T(8,128)(2,1)S(1)} %get-tuple-element.87), channel_id=1, source_target_pairs={{0,5},{1,4},{2,7},{3,6},{4,1},{5,0},{6,3},{7,2},{8,13},{9,12},{10,... | collective-permute-start | bytes 663560 | tf_op jit(solution)/shard_map/ppermute | solution.py:701
  36.6 1.3 %collective-permute-start.6 = (bf16[112,192]{1,0:T(8,128)(2,1)S(1)}, bf16[112,192]{1,0:T(8,128)(2,1)S(1)}, u32[]{:S(2)}, u32[]{:S(2)}) collective-permute-start(bf16[112,192]{1,0:T(8,128)(2,1)S(1)} %get-tuple-element.67), channel_id=1, source_target_pairs={{0,1},{1,0},{2,3},{3,2},{4,5},{5,4},{6,7},{7,6},{8,9},{9,8},{10,11... | collective-permute-start | bytes 129032 | tf_op jit(solution)/shard_map/ppermute | solution.py:638
  37.9 6.1 %collective-permute-done.6.lat = bf16[112,192]{1,0:T(8,128)(2,1)S(1)} collective-permute-done((bf16[112,192]{1,0:T(8,128)(2,1)S(1)}, bf16[112,192]{1,0:T(8,128)(2,1)S(1)}, u32[]{:S(2)}, u32[]{:S(2)}) %collective-permute-start.6) | collective-permute-done | bytes 43040 | tf_op jit(solution)/shard_map/ppermute | solution.py:638
  44.3 5.3 %backward_one.1 = (bf16[3,2,2304]{2,1,0:T(2,128)(2,1)S(1)}, bf16[9,2,3456]{2,1,0:T(2,128)(2,1)S(1)}, bf16[3,2,5760]{2,1,0:T(2,128)(2,1)S(1)}, bf16[15,2,1152]{2,...) custom-call(bf16[336,192]{1,0:T(8,128)(2,1)S(1)} %get-tuple-element., ...), custom_call_target="tpu_custom_call" | custom-call | tf_op jit(solution)/shard_map/backward_one/pallas_call | solution.py:984
  51.1 1.1 collective-permute-start.20
  52.4 4.8 %collective-permute-start.17 = (bf16[72,384]{1,0:T(8,128)(2,1)S(1)}, bf16[72,384]{1,0:T(8,128)(2,1)S(1)}, u32[]{:S(2)}, u32[]{:S(2)}) collective-permute-start(bf16[72,384]{1,0:T(8,128)(2,1)S(1)} %get-tuple-element.90), channel_id=1, source_target_pairs={{0,16},{1,17},{2,18},{3,19},{4,20},{5,21},{6,22},{7,23},{8,24},{9,... | collective-permute-start | bytes 165896 | tf_op jit(solution)/shard_map/ppermute | solution.py:701
  57.2 2.7 %collective-permute-start.21 = (bf16[48,384]{1,0:T(8,128)(2,1)S(1)}, bf16[48,384]{1,0:T(8,128)(2,1)S(1)}, u32[]{:S(2)}, u32[]{:S(2)}) collective-permute-start(bf16[48,384]{1,0:T(8,128)(2,1)S(1)} %get-tuple-element.96), channel_id=1, source_target_pairs={{0,4},{1,5},{2,6},{3,7},{4,0},{5,1},{6,2},{7,3},{8,12},{9,13},{10,... | collective-permute-start | bytes 110600 | tf_op jit(solution)/shard_map/ppermute | solution.py:701
  60.3 1.6 %collective-permute-done.21.refs_6_ = bf16[48,384]{1,0:T(8,128)(2,1)S(1)} collective-permute-done((bf16[48,384]{1,0:T(8,128)(2,1)S(1)}, bf16[48,384]{1,0:T(8,128)(2,1)S(1)}, u32[]{:S(2)}, u32[]{:S(2)}) %collective-permute-start.21) | collective-permute-done | bytes 36896 | tf_op jit(solution)/shard_map/ppermute | solution.py:701
  61.9 2.9 %collective-permute-done.22.refs_7_ = bf16[48,384]{1,0:T(8,128)(2,1)S(1)} collective-permute-done((bf16[48,384]{1,0:T(8,128)(2,1)S(1)}, bf16[48,384]{1,0:T(8,128)(2,1)S(1)}, u32[]{:S(2)}, u32[]{:S(2)}) %collective-permute-start.22) | collective-permute-done | bytes 36896 | tf_op jit(solution)/shard_map/ppermute | solution.py:701
  64.9 1.5 %collective-permute-start.25 = (bf16[120,384]{1,0:T(8,128)(2,1)S(1)}, bf16[120,384]{1,0:T(8,128)(2,1)S(1)}, u32[]{:S(2)}, u32[]{:S(2)}) collective-permute-start(bf16[120,384]{1,0:T(8,128)(2,1)S(1)} %message.1.refs_0_), channel_id=1, source_target_pairs={{0,24},{1,25},{2,26},{3,27},{4,28},{5,29},{6,30},{7,31},{8,0},{9,1... | collective-permute-start | bytes 276488 | tf_op jit(solution)/shard_map/ppermute | solution.py:701
  66.4 2.0 %collective-permute-start.24 = (bf16[120,384]{1,0:T(8,128)(2,1)S(1)}, bf16[120,384]{1,0:T(8,128)(2,1)S(1)}, u32[]{:S(2)}, u32[]{:S(2)}) collective-permute-start(bf16[120,384]{1,0:T(8,128)(2,1)S(1)} %message.1.refs_0_), channel_id=1, source_target_pairs={{0,16},{1,17},{2,18},{3,19},{4,20},{5,21},{6,22},{7,23},{8,24},{9,... | collective-permute-start | bytes 276488 | tf_op jit(solution)/shard_map/ppermute | solution.py:701
  68.5 2.4 %collective-permute-done.25.refs_3_ = bf16[120,384]{1,0:T(8,128)(2,1)S(1)} collective-permute-done((bf16[120,384]{1,0:T(8,128)(2,1)S(1)}, bf16[120,384]{1,0:T(8,128)(2,1)S(1)}, u32[]{:S(2)}, u32[]{:S(2)}) %collective-permute-start.25) | collective-permute-done | bytes 92192 | tf_op jit(solution)/shard_map/ppermute | solution.py:701
  70.9 2.9 %collective-permute-done.24.refs_2_ = bf16[120,384]{1,0:T(8,128)(2,1)S(1)} collective-permute-done((bf16[120,384]{1,0:T(8,128)(2,1)S(1)}, bf16[120,384]{1,0:T(8,128)(2,1)S(1)}, u32[]{:S(2)}, u32[]{:S(2)}) %collective-permute-start.24) | collective-permute-done | bytes 92192 | tf_op jit(solution)/shard_map/ppermute | solution.py:701
  75.8 1.5 %collective-permute-start.27 = (bf16[336,384]{1,0:T(8,128)(2,1)S(1)}, bf16[336,384]{1,0:T(8,128)(2,1)S(1)}, u32[]{:S(2)}, u32[]{:S(2)}) collective-permute-start(bf16[336,384]{1,0:T(8,128)(2,1)S(1)} %widen.1.refs_0_), channel_id=1, source_target_pairs={{0,4},{1,5},{2,6},{3,7},{4,0},{5,1},{6,2},{7,3},{8,12},{9,13},{10,... | collective-permute-start | bytes 774152 | tf_op jit(solution)/shard_map/ppermute | solution.py:701
  77.3 1.1 %collective-permute-start.26 = (bf16[336,384]{1,0:T(8,128)(2,1)S(1)}, bf16[336,384]{1,0:T(8,128)(2,1)S(1)}, u32[]{:S(2)}, u32[]{:S(2)}) collective-permute-start(bf16[336,384]{1,0:T(8,128)(2,1)S(1)} %widen.1.refs_0_), channel_id=1, source_target_pairs={{0,1},{1,0},{2,3},{3,2},{4,5},{5,4},{6,7},{7,6},{8,9},{9,8},{10,11... | collective-permute-start | bytes 774152 | tf_op jit(solution)/shard_map/ppermute | solution.py:701
  78.4 5.3 %collective-permute-done.28.refs_3_ = bf16[336,384]{1,0:T(8,128)(2,1)S(1)} collective-permute-done((bf16[336,384]{1,0:T(8,128)(2,1)S(1)}, bf16[336,384]{1,0:T(8,128)(2,1)S(1)}, u32[]{:S(2)}, u32[]{:S(2)}) %collective-permute-start.28) | collective-permute-done | bytes 258080 | tf_op jit(solution)/shard_map/ppermute | solution.py:701
  83.8 2.2 %collective-permute-done.27.refs_2_ = bf16[336,384]{1,0:T(8,128)(2,1)S(1)} collective-permute-done((bf16[336,384]{1,0:T(8,128)(2,1)S(1)}, bf16[336,384]{1,0:T(8,128)(2,1)S(1)}, u32[]{:S(2)}, u32[]{:S(2)}) %collective-permute-start.27) | collective-permute-done | bytes 258080 | tf_op jit(solution)/shard_map/ppermute | solution.py:701
  87.5 6.1 %collective-permute-done.11.diag = bf16[3,2,3456]{2,1,0:T(2,128)(2,1)S(1)} collective-permute-done((bf16[3,2,3456]{2,1,0:T(2,128)(2,1)S(1)}, bf16[3,2,3456]{2,1,0:T(2,128)(2,1)S(1)}, u32[]{:S(2)}, u32[]{:S(2)}) %collective-permute-start.11) | collective-permute-done | bytes 41504 | tf_op jit(solution)/shard_map/ppermute | solution.py:638
  93.6 1.0 collective-permute-start.9
  94.7 3.3 %collective-permute-done.9.lat = bf16[3,2,5760]{2,1,0:T(2,128)(2,1)S(1)} collective-permute-done((bf16[3,2,5760]{2,1,0:T(2,128)(2,1)S(1)}, bf16[3,2,5760]{2,1,0:T(2,128)(2,1)S(1)}, u32[]{:S(2)}, u32[]{:S(2)}) %collective-permute-start.9) | collective-permute-done | bytes 69152 | tf_op jit(solution)/shard_map/ppermute | solution.py:638
  97.9 6.4 %collective-permute-done.10.lon = bf16[15,2,1152]{2,1,0:T(2,128)(2,1)S(1)} collective-permute-done((bf16[15,2,1152]{2,1,0:T(2,128)(2,1)S(1)}, bf16[15,2,1152]{2,1,0:T(2,128)(2,1)S(1)}, u32[]{:S(2)}, u32[]{:S(2)}) %collective-permute-start.10) | collective-permute-done | bytes 69152 | tf_op jit(solution)/shard_map/ppermute | solution.py:638
  105.1 2.1 %finish.1 = (bf16[192,576]{1,0:T(8,128)(2,1)}, bf16[192,192]{1,0:T(8,128)(2,1)}, bf16[768,384]{1,0:T(8,128)(2,1)}, bf16[384,1152]{1,0:T(8,128)(2,1)}, bf16[384,384]{1,0:T(8,128)(2,1)}) custom-call(bf16[336,384]{1,0:T(8,128)(2,1)S(1)} %widen.1.refs_0_, bf16[336,384]{1,0:T(8,128)(2,1)S(1)} %collective-permute-done.26.refs_1_, ...), custom_call_target="tpu_custom_call" | custom-call | tf_op jit(solution)/shard_map/finish/pallas_call | solution.py:1034
  (71 shorter events, 12.2 us)
Async XLA Ops:
  1.6 11.8 %collective-permute-start = (bf16[3,2,5760]{2,1,0:T(2,128)(2,1)S(1)}, bf16[3,2,5760]{2,1,0:T(2,128)(2,1)S(1)}, u32[]{:S(2)}, u32[]{:S(2)}) collective-permute-start(bf16[3,2,5760]{2,1,0:T(2,128)(2,1)S(1)} %get-tuple-element.55), channel_id=1, source_target_pairs={{0,1},{1,0},{2,3},{3,2},{4,5},{5,4},{6,7},{7,6},{8,9},{9,8},{10,11... | collective-permute-start | bytes 207368 | tf_op jit(solution)/shard_map/ppermute | solution.py:638
  4.7 8.8 %collective-permute-start.1 = (bf16[15,2,1152]{2,1,0:T(2,128)(2,1)S(1)}, bf16[15,2,1152]{2,1,0:T(2,128)(2,1)S(1)}, u32[]{:S(2)}, u32[]{:S(2)}) collective-permute-start(bf16[15,2,1152]{2,1,0:T(2,128)(2,1)S(1)} %get-tuple-element.56), channel_id=1, source_target_pairs={{0,30},{1,31},{2,0},{3,1},{4,2},{5,3},{6,4},{7,5},{8,6},{9,7},{10,... | collective-permute-start | bytes 207368 | tf_op jit(solution)/shard_map/ppermute | solution.py:638
  8.4 5.0 %collective-permute-start.2 = (bf16[3,2,3456]{2,1,0:T(2,128)(2,1)S(1)}, bf16[3,2,3456]{2,1,0:T(2,128)(2,1)S(1)}, u32[]{:S(2)}, u32[]{:S(2)}) collective-permute-start(bf16[3,2,3456]{2,1,0:T(2,128)(2,1)S(1)} %get-tuple-element.57), channel_id=1, source_target_pairs={{0,31},{1,30},{2,1},{3,0},{4,3},{5,2},{6,5},{7,4},{8,7},{9,6},{10,... | collective-permute-start | bytes 124424 | tf_op jit(solution)/shard_map/ppermute | solution.py:638
  17.0 6.7 %collective-permute-start.3 = (bf16[112,192]{1,0:T(8,128)(2,1)S(1)}, bf16[112,192]{1,0:T(8,128)(2,1)S(1)}, u32[]{:S(2)}, u32[]{:S(2)}) collective-permute-start(bf16[112,192]{1,0:T(8,128)(2,1)S(1)} %get-tuple-element.60), channel_id=1, source_target_pairs={{0,1},{1,0},{2,3},{3,2},{4,5},{5,4},{6,7},{7,6},{8,9},{9,8},{10,11... | collective-permute-start | bytes 129032 | tf_op jit(solution)/shard_map/ppermute | solution.py:638
  18.6 5.1 %collective-permute-start.4 = (bf16[112,192]{1,0:T(8,128)(2,1)S(1)}, bf16[112,192]{1,0:T(8,128)(2,1)S(1)}, u32[]{:S(2)}, u32[]{:S(2)}) collective-permute-start(bf16[112,192]{1,0:T(8,128)(2,1)S(1)} %get-tuple-element.61), channel_id=1, source_target_pairs={{0,30},{1,31},{2,0},{3,1},{4,2},{5,3},{6,4},{7,5},{8,6},{9,7},{10,... | collective-permute-start | bytes 129032 | tf_op jit(solution)/shard_map/ppermute | solution.py:638
  20.2 3.5 %collective-permute-start.5 = (bf16[48,192]{1,0:T(8,128)(2,1)S(1)}, bf16[48,192]{1,0:T(8,128)(2,1)S(1)}, u32[]{:S(2)}, u32[]{:S(2)}) collective-permute-start(bf16[48,192]{1,0:T(8,128)(2,1)S(1)} %get-tuple-element.62), channel_id=1, source_target_pairs={{0,31},{1,30},{2,1},{3,0},{4,3},{5,2},{6,5},{7,4},{8,7},{9,6},{10,... | collective-permute-start | bytes 55304 | tf_op jit(solution)/shard_map/ppermute | solution.py:638
  30.2 2.5 %collective-permute-start.12 = (bf16[1152,384]{1,0:T(8,128)(2,1)S(1)}, bf16[1152,384]{1,0:T(8,128)(2,1)S(1)}, u32[]{:S(2)}, u32[]{:S(2)}) collective-permute-start(bf16[1152,384]{1,0:T(8,128)(2,1)S(1)} %get-tuple-element.83), channel_id=1, source_target_pairs={{0,2},{1,3},{2,0},{3,1},{4,6},{5,7},{6,4},{7,5},{8,10},{9,11},{10,... | collective-permute-start | bytes 2654216 | tf_op jit(solution)/shard_map/ppermute | solution.py:701
  30.3 7.6 %collective-permute-start.8 = (bf16[48,192]{1,0:T(8,128)(2,1)S(1)}, bf16[48,192]{1,0:T(8,128)(2,1)S(1)}, u32[]{:S(2)}, u32[]{:S(2)}) collective-permute-start(bf16[48,192]{1,0:T(8,128)(2,1)S(1)} %get-tuple-element.69), channel_id=1, source_target_pairs={{0,3},{1,2},{2,5},{3,4},{4,7},{5,6},{6,9},{7,8},{8,11},{9,10},{10,... | collective-permute-start | bytes 55304 | tf_op jit(solution)/shard_map/ppermute | solution.py:638
  33.0 19.1 %collective-permute-start.13 = (bf16[288,384]{1,0:T(8,128)(2,1)S(1)}, bf16[288,384]{1,0:T(8,128)(2,1)S(1)}, u32[]{:S(2)}, u32[]{:S(2)}) collective-permute-start(bf16[288,384]{1,0:T(8,128)(2,1)S(1)} %get-tuple-element.85), channel_id=1, source_target_pairs={{0,1},{1,0},{2,3},{3,2},{4,5},{5,4},{6,7},{7,6},{8,9},{9,8},{10,11... | collective-permute-start | bytes 663560 | tf_op jit(solution)/shard_map/ppermute | solution.py:701
  34.4 17.8 %collective-permute-start.14 = (bf16[288,384]{1,0:T(8,128)(2,1)S(1)}, bf16[288,384]{1,0:T(8,128)(2,1)S(1)}, u32[]{:S(2)}, u32[]{:S(2)}) collective-permute-start(bf16[288,384]{1,0:T(8,128)(2,1)S(1)} %get-tuple-element.86), channel_id=1, source_target_pairs={{0,4},{1,5},{2,6},{3,7},{4,0},{5,1},{6,2},{7,3},{8,12},{9,13},{10,... | collective-permute-start | bytes 663560 | tf_op jit(solution)/shard_map/ppermute | solution.py:701
  34.4 17.8 %collective-permute-start.15 = (bf16[288,384]{1,0:T(8,128)(2,1)S(1)}, bf16[288,384]{1,0:T(8,128)(2,1)S(1)}, u32[]{:S(2)}, u32[]{:S(2)}) collective-permute-start(bf16[288,384]{1,0:T(8,128)(2,1)S(1)} %get-tuple-element.87), channel_id=1, source_target_pairs={{0,5},{1,4},{2,7},{3,6},{4,1},{5,0},{6,3},{7,2},{8,13},{9,12},{10,... | collective-permute-start | bytes 663560 | tf_op jit(solution)/shard_map/ppermute | solution.py:701
  36.6 7.4 %collective-permute-start.6 = (bf16[112,192]{1,0:T(8,128)(2,1)S(1)}, bf16[112,192]{1,0:T(8,128)(2,1)S(1)}, u32[]{:S(2)}, u32[]{:S(2)}) collective-permute-start(bf16[112,192]{1,0:T(8,128)(2,1)S(1)} %get-tuple-element.67), channel_id=1, source_target_pairs={{0,1},{1,0},{2,3},{3,2},{4,5},{5,4},{6,7},{7,6},{8,9},{9,8},{10,11... | collective-permute-start | bytes 129032 | tf_op jit(solution)/shard_map/ppermute | solution.py:638
  37.9 6.4 %collective-permute-start.7 = (bf16[112,192]{1,0:T(8,128)(2,1)S(1)}, bf16[112,192]{1,0:T(8,128)(2,1)S(1)}, u32[]{:S(2)}, u32[]{:S(2)}) collective-permute-start(bf16[112,192]{1,0:T(8,128)(2,1)S(1)} %get-tuple-element.68), channel_id=1, source_target_pairs={{0,2},{1,3},{2,4},{3,5},{4,6},{5,7},{6,8},{7,9},{8,10},{9,11},{10,... | collective-permute-start | bytes 129032 | tf_op jit(solution)/shard_map/ppermute | solution.py:638
  51.1 8.8 %collective-permute-start.20 = (bf16[48,384]{1,0:T(8,128)(2,1)S(1)}, bf16[48,384]{1,0:T(8,128)(2,1)S(1)}, u32[]{:S(2)}, u32[]{:S(2)}) collective-permute-start(bf16[48,384]{1,0:T(8,128)(2,1)S(1)} %get-tuple-element.95), channel_id=1, source_target_pairs={{0,1},{1,0},{2,3},{3,2},{4,5},{5,4},{6,7},{7,6},{8,9},{9,8},{10,11... | collective-permute-start | bytes 110600 | tf_op jit(solution)/shard_map/ppermute | solution.py:701
  52.3 12.5 %collective-permute-start.16 = (bf16[72,384]{1,0:T(8,128)(2,1)S(1)}, bf16[72,384]{1,0:T(8,128)(2,1)S(1)}, u32[]{:S(2)}, u32[]{:S(2)}) collective-permute-start(bf16[72,384]{1,0:T(8,128)(2,1)S(1)} %get-tuple-element.89), channel_id=1, source_target_pairs={{0,8},{1,9},{2,10},{3,11},{4,12},{5,13},{6,14},{7,15},{8,16},{9,17... | collective-permute-start | bytes 165896 | tf_op jit(solution)/shard_map/ppermute | solution.py:701
  52.4 12.4 %collective-permute-start.17 = (bf16[72,384]{1,0:T(8,128)(2,1)S(1)}, bf16[72,384]{1,0:T(8,128)(2,1)S(1)}, u32[]{:S(2)}, u32[]{:S(2)}) collective-permute-start(bf16[72,384]{1,0:T(8,128)(2,1)S(1)} %get-tuple-element.90), channel_id=1, source_target_pairs={{0,16},{1,17},{2,18},{3,19},{4,20},{5,21},{6,22},{7,23},{8,24},{9,... | collective-permute-start | bytes 165896 | tf_op jit(solution)/shard_map/ppermute | solution.py:701
  57.2 7.6 %collective-permute-start.18 = (bf16[72,384]{1,0:T(8,128)(2,1)S(1)}, bf16[72,384]{1,0:T(8,128)(2,1)S(1)}, u32[]{:S(2)}, u32[]{:S(2)}) collective-permute-start(bf16[72,384]{1,0:T(8,128)(2,1)S(1)} %get-tuple-element.91), channel_id=1, source_target_pairs={{0,24},{1,25},{2,26},{3,27},{4,28},{5,29},{6,30},{7,31},{8,0},{9,1... | collective-permute-start | bytes 165896 | tf_op jit(solution)/shard_map/ppermute | solution.py:701
  57.2 4.7 %collective-permute-start.21 = (bf16[48,384]{1,0:T(8,128)(2,1)S(1)}, bf16[48,384]{1,0:T(8,128)(2,1)S(1)}, u32[]{:S(2)}, u32[]{:S(2)}) collective-permute-start(bf16[48,384]{1,0:T(8,128)(2,1)S(1)} %get-tuple-element.96), channel_id=1, source_target_pairs={{0,4},{1,5},{2,6},{3,7},{4,0},{5,1},{6,2},{7,3},{8,12},{9,13},{10,... | collective-permute-start | bytes 110600 | tf_op jit(solution)/shard_map/ppermute | solution.py:701
  59.9 4.9 %collective-permute-start.22 = (bf16[48,384]{1,0:T(8,128)(2,1)S(1)}, bf16[48,384]{1,0:T(8,128)(2,1)S(1)}, u32[]{:S(2)}, u32[]{:S(2)}) collective-permute-start(bf16[48,384]{1,0:T(8,128)(2,1)S(1)} %get-tuple-element.97), channel_id=1, source_target_pairs={{0,5},{1,4},{2,7},{3,6},{4,1},{5,0},{6,3},{7,2},{8,13},{9,12},{10,... | collective-permute-start | bytes 110600 | tf_op jit(solution)/shard_map/ppermute | solution.py:701
  64.9 6.0 %collective-permute-start.25 = (bf16[120,384]{1,0:T(8,128)(2,1)S(1)}, bf16[120,384]{1,0:T(8,128)(2,1)S(1)}, u32[]{:S(2)}, u32[]{:S(2)}) collective-permute-start(bf16[120,384]{1,0:T(8,128)(2,1)S(1)} %message.1.refs_0_), channel_id=1, source_target_pairs={{0,24},{1,25},{2,26},{3,27},{4,28},{5,29},{6,30},{7,31},{8,0},{9,1... | collective-permute-start | bytes 276488 | tf_op jit(solution)/shard_map/ppermute | solution.py:701
  66.4 7.5 %collective-permute-start.24 = (bf16[120,384]{1,0:T(8,128)(2,1)S(1)}, bf16[120,384]{1,0:T(8,128)(2,1)S(1)}, u32[]{:S(2)}, u32[]{:S(2)}) collective-permute-start(bf16[120,384]{1,0:T(8,128)(2,1)S(1)} %message.1.refs_0_), channel_id=1, source_target_pairs={{0,16},{1,17},{2,18},{3,19},{4,20},{5,21},{6,22},{7,23},{8,24},{9,... | collective-permute-start | bytes 276488 | tf_op jit(solution)/shard_map/ppermute | solution.py:701
  68.4 6.4 %collective-permute-start.23 = (bf16[120,384]{1,0:T(8,128)(2,1)S(1)}, bf16[120,384]{1,0:T(8,128)(2,1)S(1)}, u32[]{:S(2)}, u32[]{:S(2)}) collective-permute-start(bf16[120,384]{1,0:T(8,128)(2,1)S(1)} %message.1.refs_0_), channel_id=1, source_target_pairs={{0,8},{1,9},{2,10},{3,11},{4,12},{5,13},{6,14},{7,15},{8,16},{9,17... | collective-permute-start | bytes 276488 | tf_op jit(solution)/shard_map/ppermute | solution.py:701
  74.9 8.9 %collective-permute-start.28 = (bf16[336,384]{1,0:T(8,128)(2,1)S(1)}, bf16[336,384]{1,0:T(8,128)(2,1)S(1)}, u32[]{:S(2)}, u32[]{:S(2)}) collective-permute-start(bf16[336,384]{1,0:T(8,128)(2,1)S(1)} %widen.1.refs_0_), channel_id=1, source_target_pairs={{0,5},{1,4},{2,7},{3,6},{4,1},{5,0},{6,3},{7,2},{8,13},{9,12},{10,... | collective-permute-start | bytes 774152 | tf_op jit(solution)/shard_map/ppermute | solution.py:701
  75.8 10.1 %collective-permute-start.27 = (bf16[336,384]{1,0:T(8,128)(2,1)S(1)}, bf16[336,384]{1,0:T(8,128)(2,1)S(1)}, u32[]{:S(2)}, u32[]{:S(2)}) collective-permute-start(bf16[336,384]{1,0:T(8,128)(2,1)S(1)} %widen.1.refs_0_), channel_id=1, source_target_pairs={{0,4},{1,5},{2,6},{3,7},{4,0},{5,1},{6,2},{7,3},{8,12},{9,13},{10,... | collective-permute-start | bytes 774152 | tf_op jit(solution)/shard_map/ppermute | solution.py:701
  77.3 9.1 %collective-permute-start.26 = (bf16[336,384]{1,0:T(8,128)(2,1)S(1)}, bf16[336,384]{1,0:T(8,128)(2,1)S(1)}, u32[]{:S(2)}, u32[]{:S(2)}) collective-permute-start(bf16[336,384]{1,0:T(8,128)(2,1)S(1)} %widen.1.refs_0_), channel_id=1, source_target_pairs={{0,1},{1,0},{2,3},{3,2},{4,5},{5,4},{6,7},{7,6},{8,9},{9,8},{10,11... | collective-permute-start | bytes 774152 | tf_op jit(solution)/shard_map/ppermute | solution.py:701
  78.4 26.7 %collective-permute-start.29 = (bf16[336,384]{1,0:T(8,128)(2,1)S(1)}, bf16[336,384]{1,0:T(8,128)(2,1)S(1)}, u32[]{:S(2)}, u32[]{:S(2)}) collective-permute-start(bf16[336,384]{1,0:T(8,128)(2,1)S(1)} %widen.1.refs_0_), channel_id=1, source_target_pairs={{0,2},{1,3},{2,0},{3,1},{4,6},{5,7},{6,4},{7,5},{8,10},{9,11},{10,... | collective-permute-start | bytes 774152 | tf_op jit(solution)/shard_map/ppermute | solution.py:701
  83.8 21.4 %collective-permute-start.32 = (bf16[336,384]{1,0:T(8,128)(2,1)S(1)}, bf16[336,384]{1,0:T(8,128)(2,1)S(1)}, u32[]{:S(2)}, u32[]{:S(2)}) collective-permute-start(bf16[336,384]{1,0:T(8,128)(2,1)S(1)} %collective-permute-done.28.refs_3_), channel_id=1, source_target_pairs={{0,2},{1,3},{2,0},{3,1},{4,6},{5,7},{6,4},{7,5},{8,10},{9,11},{10,... | collective-permute-start | bytes 774152 | tf_op jit(solution)/shard_map/ppermute | solution.py:701
  86.0 19.1 %collective-permute-start.31 = (bf16[336,384]{1,0:T(8,128)(2,1)S(1)}, bf16[336,384]{1,0:T(8,128)(2,1)S(1)}, u32[]{:S(2)}, u32[]{:S(2)}) collective-permute-start(bf16[336,384]{1,0:T(8,128)(2,1)S(1)} %collective-permute-done.27.refs_2_), channel_id=1, source_target_pairs={{0,2},{1,3},{2,0},{3,1},{4,6},{5,7},{6,4},{7,5},{8,10},{9,11},{10,... | collective-permute-start | bytes 774152 | tf_op jit(solution)/shard_map/ppermute | solution.py:701
  86.4 18.7 %collective-permute-start.30 = (bf16[336,384]{1,0:T(8,128)(2,1)S(1)}, bf16[336,384]{1,0:T(8,128)(2,1)S(1)}, u32[]{:S(2)}, u32[]{:S(2)}) collective-permute-start(bf16[336,384]{1,0:T(8,128)(2,1)S(1)} %collective-permute-done.26.refs_1_), channel_id=1, source_target_pairs={{0,2},{1,3},{2,0},{3,1},{4,6},{5,7},{6,4},{7,5},{8,10},{9,11},{10,... | collective-permute-start | bytes 774152 | tf_op jit(solution)/shard_map/ppermute | solution.py:701
  86.5 7.1 %collective-permute-start.11 = (bf16[3,2,3456]{2,1,0:T(2,128)(2,1)S(1)}, bf16[3,2,3456]{2,1,0:T(2,128)(2,1)S(1)}, u32[]{:S(2)}, u32[]{:S(2)}) collective-permute-start(bf16[3,2,3456]{2,1,0:T(2,128)(2,1)S(1)} %get-tuple-element.79), channel_id=1, source_target_pairs={{0,3},{1,2},{2,5},{3,4},{4,7},{5,6},{6,9},{7,8},{8,11},{9,10},{10,... | collective-permute-start | bytes 124424 | tf_op jit(solution)/shard_map/ppermute | solution.py:638
  93.6 4.3 %collective-permute-start.9 = (bf16[3,2,5760]{2,1,0:T(2,128)(2,1)S(1)}, bf16[3,2,5760]{2,1,0:T(2,128)(2,1)S(1)}, u32[]{:S(2)}, u32[]{:S(2)}) collective-permute-start(bf16[3,2,5760]{2,1,0:T(2,128)(2,1)S(1)} %get-tuple-element.77), channel_id=1, source_target_pairs={{0,1},{1,0},{2,3},{3,2},{4,5},{5,4},{6,7},{7,6},{8,9},{9,8},{10,11... | collective-permute-start | bytes 207368 | tf_op jit(solution)/shard_map/ppermute | solution.py:638
  97.9 6.4 %collective-permute-start.10 = (bf16[15,2,1152]{2,1,0:T(2,128)(2,1)S(1)}, bf16[15,2,1152]{2,1,0:T(2,128)(2,1)S(1)}, u32[]{:S(2)}, u32[]{:S(2)}) collective-permute-start(bf16[15,2,1152]{2,1,0:T(2,128)(2,1)S(1)} %get-tuple-element.78), channel_id=1, source_target_pairs={{0,2},{1,3},{2,4},{3,5},{4,6},{5,7},{6,8},{7,9},{8,10},{9,11},{10,... | collective-permute-start | bytes 207368 | tf_op jit(solution)/shard_map/ppermute | solution.py:638
  (13 other events, 122.7 us)
